TPU v7x, 16 devices: a whole 2x2x2 slice. The times are simulated.
16 devices in a mesh: dp: 2 (over z), tp: 8 (over y, x, core).
Axes of the slice: x: 2, y: 2, z: 2, core: 2. Of those that a mesh axis runs over, the one named last changes fastest.
Arguments:
- x_in: bfloat16 [2, 2048, 2304], P('dp', 'tp'), parts along dimension 0
- x_mid: bfloat16 [2, 2048, 2304], P('dp', 'tp'), parts along dimension 0
- d_out: bfloat16 [2, 2048, 2304], P('dp', 'tp'), parts along dimension 0
- q_saved: bfloat16 [2, 2048, 24, 96], P('dp', None, 'tp'), parts along dimension 0
- k_saved: bfloat16 [2, 2048, 24, 96], P('dp', None, 'tp'), parts along dimension 0
- v_saved: bfloat16 [2, 2048, 24, 96], P('dp', None, 'tp'), parts along dimension 0
- z_saved: bfloat16 [2, 2048, 9216], P('dp', None, 'tp'), parts along dimension 0
- ln1_gain: float32 [2304], replicated
- ln1_bias: float32 [2304], replicated
- ln2_gain: float32 [2304], replicated
- ln2_bias: float32 [2304], replicated
- w_qkv: bfloat16 [3, 2304, 24, 96], P(None, None, 'tp')
- w_proj: bfloat16 [24, 96, 2304], P('tp')
- w_fc1: bfloat16 [2304, 9216], P(None, 'tp')
- w_fc2: bfloat16 [9216, 2304], P('tp')
Outputs:
- output 1: bfloat16 [2, 2048, 2304], P('dp', 'tp'), parts along dimension 0
- output 2: float32 [6, 2304, 24, 96], P('dp', None, 'tp'), parts along dimension 0
- output 3: float32 [6, 24, 96], P('dp', 'tp'), parts along dimension 0
- output 4: float32 [48, 96, 2304], P(('dp', 'tp')), parts along dimension 0
- output 5: float32 [4608, 9216], P('dp', 'tp'), parts along dimension 0
- output 6: float32 [18432], P(('dp', 'tp')), parts along dimension 0
- output 7: float32 [18432, 2304], P(('dp', 'tp')), parts along dimension 0
- output 8: float32 [12, 2304], P('dp'), parts along dimension 0
There are 2 independent parts. A program takes and returns all parts, laid end to end along the dimension named above; an argument that names none is the same for every part.
All inputs are finite; a program needn't handle non-finite values.
Results may differ from a plain program's by a relative error of at most 0.0111809.
Values are sent between devices in bfloat16 or wider.
A program may use at most 1 GiB of HBM per device.

v0:
```python
import jax, jax.numpy as jnp
from jax import lax
from jax.experimental import pallas as pl
from jax.experimental.pallas import tpu as pltpu
from jax.sharding import PartitionSpec as P
T=2048; E=96; NH=3; BQ=512; NQ=T//BQ; BLK=256
C=E**-0.5; C2=C*1.4426950408889634
f32=jnp.float32; bf16=jnp.bfloat16

def turn(h, core):
    return jnp.where(core==0, h, (h%2)*2+h//2)

def rel_pos(block, me):
    j=lax.bitwise_xor(block, me)
    return 2*turn(j//2, me%2)+j%2

def tn(a,b,ca,cb): return lax.dot_general(a,b,(((ca,),(cb,)),((),())),preferred_element_type=f32)

def fold8(a): return jnp.sum(a.reshape(a.shape[0]//8,8,a.shape[1]),axis=0)
def foldmax8(a): return jnp.max(a.reshape(a.shape[0]//8,8,a.shape[1]),axis=0)

def causal(s, fill):
    r=lax.broadcasted_iota(jnp.int32,s.shape,0); c=lax.broadcasted_iota(jnp.int32,s.shape,1)
    return jnp.where(r<=c,s,fill)

def fwd_kernel(me_ref,q_ref,k_ref,v_ref,_,ctx_ref,lse_ref,kt,sc,acc):
    i=pl.program_id(1)
    @pl.when(i==0)
    def _(): kt[...]=k_ref[0].T
    q=q_ref[0]
    def rows(j): return pl.ds(pl.multiple_of(j*BQ,BQ),BQ)
    def p1(j,m):
        s=jnp.dot(kt[rows(j),:],q,preferred_element_type=f32)
        sc[rows(j),:]=s
        return jnp.maximum(m,foldmax8(s))
    m=lax.fori_loop(0,i,p1,jnp.full((8,BQ),-1e30,f32))
    s=causal(jnp.dot(kt[rows(i),:],q,preferred_element_type=f32),-1e30)
    sc[rows(i),:]=s
    m=jnp.max(jnp.maximum(m,foldmax8(s)),axis=0,keepdims=True)*C2
    def p2(j,l):
        e=jnp.exp2(sc[rows(j),:]*C2-m)
        sc[rows(j),:]=e
        return l+fold8(e)
    l=jnp.sum(lax.fori_loop(0,i+1,p2,jnp.zeros((8,BQ),f32)),axis=0,keepdims=True)
    inv=1.0/l
    lse_ref[0]=m+jnp.log2(l)
    acc[...]=jnp.zeros_like(acc)
    def p3(j,_):
        p=(sc[rows(j),:]*inv).astype(bf16)
        acc[...]+=jnp.dot(v_ref[0,:,rows(j)],p,preferred_element_type=f32)
        return 0
    lax.fori_loop(0,i+1,p3,0)
    for a in range(BQ//BLK):
        pos=rel_pos(i*(BQ//BLK)+a,me_ref[0])
        ctx_ref[0,:,pl.ds(pl.multiple_of(pos*BLK,BLK),BLK)]=acc[:,a*BLK:(a+1)*BLK].astype(bf16)

def bwd_kernel(me_ref,q_ref,k_ref,v_ref,g_ref,lse_ref,_,out_ref,kt,vt,psc,dsc,g_sc,dq,dk,dv):
    i=pl.program_id(1)
    @pl.when(i==0)
    def _():
        kt[...]=k_ref[0].T
        vt[...]=v_ref[0].T
        dk[...]=jnp.zeros_like(dk); dv[...]=jnp.zeros_like(dv)
    def rows(j): return pl.ds(pl.multiple_of(j*BQ,BQ),BQ)
    for a in range(BQ//BLK):
        pos=rel_pos(i*(BQ//BLK)+a,me_ref[0])
        g_sc[:,a*BLK:(a+1)*BLK]=g_ref[0,:,pl.ds(pl.multiple_of(pos*BLK,BLK),BLK)]
    q=q_ref[0]; g=g_sc[...]; lse=lse_ref[0]
    def tile(j,d,diag):
        s=jnp.dot(kt[rows(j),:],q,preferred_element_type=f32)
        p=jnp.exp2(s*C2-lse)
        if diag: p=causal(p,0.0)
        dp=jnp.dot(vt[rows(j),:],g,preferred_element_type=f32)
        psc[rows(j),:]=p; dsc[rows(j),:]=dp
        return d+fold8(p*dp)
    d=lax.fori_loop(0,i,lambda j,d: tile(j,d,False),jnp.zeros((8,BQ),f32))
    delta=jnp.sum(tile(i,d,True),axis=0,keepdims=True)
    dq[...]=jnp.zeros_like(dq)
    def p2(j,_):
        p=psc[rows(j),:]
        ds=(p*(dsc[rows(j),:]-delta)*C).astype(bf16)
        dq[...]+=jnp.dot(k_ref[0,:,rows(j)],ds,preferred_element_type=f32)
        dk[:,rows(j)]+=tn(q,ds,1,1)
        dv[:,rows(j)]+=tn(g,p.astype(bf16),1,1)
        return 0
    lax.fori_loop(0,i+1,p2,0)
    for a in range(BQ//BLK):
        pos=rel_pos(i*(BQ//BLK)+a,me_ref[0])
        out_ref[0,0,:,pl.ds(pl.multiple_of(pos*BLK,BLK),BLK)]=dq[:,a*BLK:(a+1)*BLK].astype(bf16)
    @pl.when(i==NQ-1)
    def _():
        for b in range(T//BLK):
            at=pl.ds(pl.multiple_of(rel_pos(b,me_ref[0])*BLK,BLK),BLK)
            out_ref[1,0,:,at]=dk[:,b*BLK:(b+1)*BLK].astype(bf16)
            out_ref[2,0,:,at]=dv[:,b*BLK:(b+1)*BLK].astype(bf16)

NEL=(NQ*(NQ+1)//2)*BQ*BQ
def attn_call(kernel, n, ins, in_specs, out_specs, out_shape, scratch, flops, prev):
    al={}
    if prev is None: prev=ins[0]
    else: al={len(ins):0}
    return pl.pallas_call(kernel,
        grid_spec=pltpu.PrefetchScalarGridSpec(num_scalar_prefetch=1,grid=(n,NQ),
            in_specs=in_specs+[pl.BlockSpec(memory_space=pl.ANY if al else pltpu.SMEM)],out_specs=out_specs,scratch_shapes=scratch),
        out_shape=out_shape,input_output_aliases=al,
        compiler_params=pltpu.CompilerParams(dimension_semantics=("arbitrary","arbitrary"),vmem_limit_bytes=40<<20),
        cost_estimate=pl.CostEstimate(flops=n*flops,bytes_accessed=n*(3<<20),transcendentals=n*NEL))(*ins,prev)
def head_specs(h0):
    full=pl.BlockSpec((1,E,T),lambda h,i,me:(h+h0,0,0))
    return full,pl.BlockSpec((1,E,BQ),lambda h,i,me:(h+h0,0,i)),pl.BlockSpec((1,1,BQ),lambda h,i,me:(h,0,i))
def attn_fwd(h0,n,me,q,k,v,prev):
    full,qblk,lblk=head_specs(h0)
    return attn_call(fwd_kernel,n,(me,q,k,v),[qblk,full,full],[full,lblk],
        [jax.ShapeDtypeStruct((NH,E,T),bf16),jax.ShapeDtypeStruct((n,1,T),f32)],
        [pltpu.VMEM((T,E),bf16),pltpu.VMEM((T,BQ),f32),pltpu.VMEM((E,BQ),f32)],NEL*1024,prev)
def attn_bwd(h0,n,me,q,k,v,g,lse,prev):
    full,qblk,lblk=head_specs(h0)
    return attn_call(bwd_kernel,n,(me,q,k,v,g,lse),[qblk,full,full,full,lblk],
        pl.BlockSpec((3,1,E,T),lambda h,i,me:(0,h+h0,0,0)),jax.ShapeDtypeStruct((3,NH,E,T),bf16),
        [pltpu.VMEM((T,E),bf16),pltpu.VMEM((T,E),bf16),pltpu.VMEM((T,BQ),f32),pltpu.VMEM((T,BQ),f32),
         pltpu.VMEM((E,BQ),bf16),pltpu.VMEM((E,BQ),f32),pltpu.VMEM((E,T),f32),pltpu.VMEM((E,T),f32)],NEL*2048,prev)

LN_EPS=1e-5
GELU_COEF=0.044715
GELU_SCALE=0.7978845608028654
D=2304
F=1152
ANY=pl.ANY

def send(a, pairs):
    return lax.ppermute(a, 'tp', pairs)
def partner(a): return send(a, [(i, i ^ 1) for i in range(8)])
def hop_a(a):
    return send(a, [(i, i ^ (2 if i % 2 == 0 else 4)) for i in range(8)])
def hop_b(a): return send(a, [(i, i ^ (4 if i % 2 == 0 else 2)) for i in range(8)])
def after(x, *deps): return lax.optimization_barrier((x,)+deps)[0]

def add2(a, b): return (a.astype(f32)+b.astype(f32)).astype(bf16)

def layer_norm_fwd(token_rows, norm_gain, norm_bias):
    rows_f32 = token_rows.astype(f32)
    centered = rows_f32 - jnp.mean(rows_f32, axis=-1, keepdims=True)
    inv_std = lax.rsqrt(jnp.mean(centered * centered, axis=-1, keepdims=True) + LN_EPS)
    return (centered * inv_std * norm_gain + norm_bias).astype(bf16)

def ln_bwd_kernel(own, ro, a_in, b_in, rows, skip, gain, out, vec):
    i=pl.program_id(0)
    dh=(own[...].astype(f32)+ro[...].astype(f32))+(a_in[...].astype(f32)+b_in[...].astype(f32))
    r=rows[...].astype(f32)
    cen=r-jnp.mean(r,axis=-1,keepdims=True)
    rstd=lax.rsqrt(jnp.mean(cen*cen,axis=-1,keepdims=True)+LN_EPS)
    hat=cen*rstd
    gh=dh*gain[...]
    cg=gh-jnp.mean(gh,axis=-1,keepdims=True)
    sk=skip[...].astype(f32)
    o=(sk+rstd*(cg-hat*jnp.mean(gh*hat,axis=-1,keepdims=True))).astype(bf16)
    out[...]=o
    @pl.when(i==0)
    def _(): vec[...]=jnp.zeros_like(vec)
    vec[0]+=fold8(dh*hat); vec[1]+=fold8(dh); vec[2]+=fold8(o.astype(f32)); vec[3]+=fold8(sk)

def ln_bwd(parts, rows, skip, gain):
    R=64
    blk=pl.BlockSpec((R,D),lambda i:(i,0))
    out,vec=pl.pallas_call(ln_bwd_kernel,grid=(256//R,),
        in_specs=[blk]*6+[pl.BlockSpec((1,D),lambda i:(0,0))],
        out_specs=[blk,pl.BlockSpec((4,8,D),lambda i:(0,0,0))],
        out_shape=[jax.ShapeDtypeStruct((256,D),bf16),jax.ShapeDtypeStruct((4,8,D),f32)],
        compiler_params=pltpu.CompilerParams(dimension_semantics=("arbitrary",)),
        cost_estimate=pl.CostEstimate(flops=256*D*1000,bytes_accessed=6<<20,transcendentals=0))(*parts,rows,skip,gain.reshape(1,D))
    return out,jnp.sum(vec,axis=1)

def call(kernel, grid, in_specs, out_specs, out_shape, scratch, flops, args):
    return pl.pallas_call(kernel,grid=grid,in_specs=in_specs,out_specs=out_specs,out_shape=out_shape,
        scratch_shapes=scratch,compiler_params=pltpu.CompilerParams(dimension_semantics=("arbitrary",)*len(grid),vmem_limit_bytes=40<<20),
        cost_estimate=pl.CostEstimate(flops=flops,bytes_accessed=30<<20,transcendentals=0))(*args)

def gelu_kernel(blk_ref, z, u, slope):
    zf=z[...].astype(f32)
    th=jnp.tanh(GELU_SCALE*(zf+GELU_COEF*zf*zf*zf))
    u[...]=(0.5*zf*(1.0+th)).astype(bf16)
    slope[...]=0.5*(1.0+th)+0.5*zf*(1.0-th*th)*GELU_SCALE*(1.0+3.0*GELU_COEF*zf*zf)

def gelu(blk, z):
    out=pl.BlockSpec((BLK,F),lambda p,blk:(p,0))
    return pl.pallas_call(gelu_kernel,name="gelu",
        grid_spec=pltpu.PrefetchScalarGridSpec(num_scalar_prefetch=1,grid=(8,),
            in_specs=[pl.BlockSpec((BLK,F),lambda p,blk:(blk[p],0))],out_specs=[out,out]),
        out_shape=[jax.ShapeDtypeStruct((T,F),bf16),jax.ShapeDtypeStruct((T,F),f32)],
        compiler_params=pltpu.CompilerParams(dimension_semantics=("arbitrary",)),
        cost_estimate=pl.CostEstimate(flops=T*F*1000,bytes_accessed=20<<20,transcendentals=T*F))(blk,z)

def mlp(first, pieces, slope, w2, w1, prev):
    n=len(pieces)//2
    def kernel(*refs):
        dy=refs[:2*n]; sl,w2h,w1h=refs[2*n:2*n+3]
        refs=refs[2*n+(3 if prev is None else 4):]
        dz_ref,db_ref=refs[:2]; dh=refs[2:2+2*n]
        x,w2s,w1s,st,xsem,wsem,osem=refs[2+2*n:]
        s=pl.program_id(0)
        class wcopy:
            def __init__(self, k):
                h,v=((w2h,w2s),(w1h,w1s))[k]
                r=v.shape[0]//4
                self.cs=[pltpu.make_async_copy(h.at[j*r:(j+1)*r],v.at[j*r:(j+1)*r],wsem.at[k,j]) for j in range(4)]
            def start(self):
                for c in self.cs: c.start()
            def wait(self):
                for c in self.cs: c.wait()
        def xcopy(p): return pltpu.make_async_copy(dy[p],x.at[p*BLK:(p+1)*BLK],xsem.at[p])
        def ocopy(p): return pltpu.make_async_copy(st.at[p*BLK:(p+1)*BLK],dh[p],osem.at[p])
        @pl.when(s==0)
        def _():
            xcopy(0).start()
            wcopy(0).start()
            for p in range(1,2*n): xcopy(p).start()
            wcopy(1).start()
            db_ref[...]=jnp.zeros_like(db_ref)
            wcopy(0).wait()
        for k in range(2*n):
            @pl.when(s==k)
            def _(): xcopy(k).wait()
        rows=pl.ds(pl.multiple_of(s*BLK,BLK),BLK)
        dz=(tn(x[rows,:],w2s[...],1,1)*sl[...]).astype(bf16)
        dz_ref[...]=dz
        db_ref[...]+=fold8(dz.astype(f32))
        @pl.when(s==0)
        def _(): wcopy(1).wait()
        def part(c,_):
            at=pl.ds(pl.multiple_of(c*768,768),768)
            st[rows,at]=tn(dz_ref[...],w1s[at,:],1,1).astype(bf16)
            return 0
        lax.fori_loop(0,3,part,0)
        for k in range(2*n):
            @pl.when(s==k)
            def _(): ocopy(k).start()
        @pl.when(s==2*n-1)
        def _():
            for p in range(2*n): ocopy(p).wait()
    any_=pl.BlockSpec(memory_space=ANY)
    step=pl.BlockSpec((BLK,F),lambda s:(s+2*first,0))
    outs=pl.pallas_call(kernel,grid=(2*n,),
        in_specs=[any_]*(2*n)+[step]+[any_]*(2 if prev is None else 3),
        out_specs=[step,pl.BlockSpec((8,F),lambda s:(0,0))]+[any_]*(2*n),
        out_shape=[jax.ShapeDtypeStruct((T,F),bf16),jax.ShapeDtypeStruct((8,F),f32)]+[jax.ShapeDtypeStruct((BLK,D),bf16)]*(2*n),
        scratch_shapes=[pltpu.VMEM((2*n*BLK,D),bf16),pltpu.VMEM((F,D),bf16),pltpu.VMEM((D,F),bf16),pltpu.VMEM((2*n*BLK,D),bf16),
         pltpu.SemaphoreType.DMA((2*n,)),pltpu.SemaphoreType.DMA((2,4)),pltpu.SemaphoreType.DMA((2*n,))],
        input_output_aliases={} if prev is None else {2*n+3:0},
        compiler_params=pltpu.CompilerParams(dimension_semantics=("arbitrary",),vmem_limit_bytes=48<<20),
        cost_estimate=pl.CostEstimate(flops=n*T*D*F,bytes_accessed=20<<20,transcendentals=0))(*pieces,slope,w2,w1,*(() if prev is None else (prev,)))
    return outs[0],outs[1],list(outs[2:])

def attn_in_grad(chips, dqkv, wqkv):
    c0,c1=chips
    def kernel(g,w,*refs):
        dh=refs[:4]; st,sem=refs[4:]
        s=pl.program_id(0)
        def ocopy(p): return pltpu.make_async_copy(st.at[p*BLK:(p+1)*BLK],dh[p],sem.at[p])
        rows=pl.ds(pl.multiple_of(s*BLK,BLK),BLK)
        def part(c,_):
            at=pl.ds(pl.multiple_of(c*768,768),768)
            st[rows,at]=tn(g[...],w[:,at],0,0).astype(bf16)
            return 0
        lax.fori_loop(0,3,part,0)
        for k in range(4):
            @pl.when(s==k)
            def _(): ocopy(k).start()
        @pl.when(s==3)
        def _():
            for p in range(4): ocopy(p).wait()
    K=3*NH*E
    return call(kernel,(4,),[pl.BlockSpec((K,BLK),lambda s:(0,2*(c0+(c1-c0)*(s//2))+s%2)),pl.BlockSpec((K,D),lambda s:(0,0))],
        [pl.BlockSpec(memory_space=ANY)]*4,[jax.ShapeDtypeStruct((BLK,D),bf16)]*4,
        [pltpu.VMEM((4*BLK,D),bf16),pltpu.SemaphoreType.DMA((4,))],T*D*K,(dqkv,wqkv))

def gathered_mm(body, pieces, other, n, out_spec, out_shape, flops, cols=(0,D), into=None):
    W=(cols[1]-cols[0])//n
    def kernel(*refs):
        ps=refs[:8]; o_ref=refs[8]; out,full,sem=refs[-3:]
        s=pl.program_id(0)
        def copy(t,p): return pltpu.make_async_copy(ps[p].at[:,cols[0]+t*W:cols[0]+(t+1)*W],full.at[t,p*BLK:(p+1)*BLK],sem.at[t,p])
        @pl.when(s==0)
        def _():
            for t in range(n):
                for p in range(8): copy(t,p).start()
        for t in range(n):
            @pl.when(s==t)
            def _():
                for p in range(8): copy(t,p).wait()
        out[...]=body(full[s],o_ref)
    any_=pl.BlockSpec(memory_space=ANY)
    extra=() if into is None else (into,)
    return pl.pallas_call(kernel,grid=(n,),in_specs=[any_]*8+[pl.BlockSpec(other.shape,lambda s:(0,0))]+[any_]*len(extra),out_specs=out_spec,out_shape=out_shape,
        scratch_shapes=[pltpu.VMEM((n,T,W),bf16),pltpu.SemaphoreType.DMA((n,8))],input_output_aliases={9:0} if extra else {},
        compiler_params=pltpu.CompilerParams(dimension_semantics=("arbitrary",),vmem_limit_bytes=60<<20),
        cost_estimate=pl.CostEstimate(flops=flops,bytes_accessed=30<<20,transcendentals=0))(*pieces,other,*extra)

def ctx_grad(first, pieces, wo, into):
    n=len(pieces)//2
    def kernel(*refs):
        ps=refs[:2*n]; w=refs[2*n]; out,full,sem=refs[-3:]
        s=pl.program_id(0)
        def copy(p): return pltpu.make_async_copy(ps[p],full.at[p//2,(p%2)*BLK:(p%2+1)*BLK],sem.at[p])
        @pl.when(s==0)
        def _():
            for p in range(2*n): copy(p).start()
        for k in range(n):
            @pl.when(s==k)
            def _():
                copy(2*k).wait(); copy(2*k+1).wait()
        out[...]=tn(w[...],full[s],1,1).astype(bf16)
    any_=pl.BlockSpec(memory_space=ANY)
    extra=() if into is None else (into,)
    return pl.pallas_call(kernel,grid=(n,),in_specs=[any_]*(2*n)+[pl.BlockSpec((NH*E,D),lambda s:(0,0))]+[any_]*len(extra),
        out_specs=pl.BlockSpec((NH*E,2*BLK),lambda s:(0,s+first)),out_shape=jax.ShapeDtypeStruct((NH*E,T),bf16),
        scratch_shapes=[pltpu.VMEM((n,2*BLK,D),bf16),pltpu.SemaphoreType.DMA((2*n,))],input_output_aliases={2*n+1:0} if extra else {},
        compiler_params=pltpu.CompilerParams(dimension_semantics=("arbitrary",),vmem_limit_bytes=24<<20),
        cost_estimate=pl.CostEstimate(flops=n*512*D*NH*E*2,bytes_accessed=10<<20,transcendentals=0))(*pieces,wo,*extra)

def solution(mesh):
    def layer(x_in, x_mid, d_out, q_saved, k_saved, v_saved, z_saved, g1, b1, g2, b2, w_qkv, w_proj, w_fc1, w_fc2):
        me=lax.axis_index('tp').astype(jnp.int32)
        me1=jnp.reshape(me,(1,))
        p8=jnp.arange(8,dtype=jnp.int32)
        blk=lax.bitwise_xor(me,2*turn(p8//2,me%2)+p8%2)
        x_in, x_mid, d_out, z = x_in[0], x_mid[0], d_out[0], z_saved[0]
        heads=lambda a: a[0].transpose(1,2,0)
        q,k,v=heads(q_saved),heads(k_saved),heads(v_saved)
        wqkv=w_qkv.transpose(0,2,3,1).reshape(3*NH*E,D)
        wo=w_proj.reshape(NH*E,D)
        dya,dyb,dyp=hop_a(d_out),hop_b(d_out),partner(d_out)
        u,slope=gelu(blk,z)
        dz,db_0,(o0,o1)=mlp(0,[d_out,dyp],slope,w_fc2,w_fc1,None)
        dya=after(dya,db_0)
        dyd=hop_b(dya)
        h2_local=layer_norm_fwd(after(x_mid,dya),g2,b2)
        h2a,h2b,h2p=hop_a(h2_local),hop_b(h2_local),partner(h2_local)
        dypa,dypb=partner(dya),partner(dyb)
        dz,db_1,(pa0,pa1,pb0,pb1)=mlp(1,[dya,dypb,dyb,dypa],slope,w_fc2,w_fc1,dz)
        ra,rb,ro=partner(pb1),partner(pa1),partner(o1)
        a_in=hop_a(add2(pa0,ra))
        dypd=partner(dyd)
        dz,db_2,(pd0,pd1)=mlp(3,[dyd,dypd],slope,w_fc2,w_fc1,dz)
        d_sum=add2(pd0,partner(pd1))
        d_in=hop_a(d_sum)
        ctx,lse01=attn_fwd(0,2,me1,after(q,d_sum),k,v,None)
        b_sum=(pb0.astype(f32)+after(rb,lse01).astype(f32)+d_in.astype(f32)).astype(bf16)
        b_in=hop_b(b_sum)
        h2a=after(h2a,b_sum)
        h2d=hop_b(h2a); h2pa,h2pb=partner(h2a),partner(h2b)
        ctx,lse2=attn_fwd(2,1,me1,after(q,b_sum),k,v,ctx)
        mid,vec2=ln_bwd((after(o0,lse2),ro,a_in,b_in),x_mid,d_out,g2)
        grad_bfc1=jnp.sum(db_0+db_1+db_2,axis=0)
        dxa,dxb,dxp=hop_a(mid),hop_b(mid),partner(mid)
        dys=[d_out,dyp,dya,dypb,dyb,dypa,dyd,dypd]
        grad_wfc2=gathered_mm(lambda x,o: tn(o[...],x,0,0),dys,after(u,mid),9,
            pl.BlockSpec((F,256),lambda s:(0,s)),jax.ShapeDtypeStruct((F,D),f32),2*T*D*F)
        h1_local=layer_norm_fwd(after(x_in,mid),g1,b1)
        dxa=after(dxa,grad_wfc2,h1_local)
        dxd=hop_b(dxa)
        dxpa,dxpb=partner(dxa),partner(dxb)
        h2pd=partner(after(h2d,grad_wfc2))
        h2=[h2_local,h2p,h2a,h2pb,h2b,h2pa,h2d,h2pd]
        grad_wfc1=gathered_mm(lambda x,o: tn(x,o[...],0,0),h2,after(dz,dxa),3,
            pl.BlockSpec((768,F),lambda s:(s,0)),jax.ShapeDtypeStruct((D,F),f32),2*T*D*F)
        dctx=ctx_grad(0,[mid,dxp,dxa,dxpb,dxb,dxpa],after(wo,grad_wfc1),None)
        dxd=after(dxd,dctx)
        dxpd=partner(dxd)
        h1_local=after(h1_local,dxd)
        h1a,h1b,h1p=hop_a(h1_local),hop_b(h1_local),partner(h1_local)
        dx1=[mid,dxp,dxa,dxpb,dxb,dxpa,dxd,dxpd]
        dctx=ctx_grad(3,[dxd,dxpd],wo,dctx).reshape(NH,E,T)
        dqkv=attn_bwd(0,2,me1,q,k,v,dctx,lse01,None)
        h1a=after(h1a,dqkv)
        h1d=hop_b(h1a); h1pa,h1pb=partner(h1a),partner(h1b)
        dqkv=attn_bwd(2,1,me1,q,k,v,dctx,lse2,dqkv)
        dqkv=dqkv.reshape(3*NH*E,T)
        pd0,pd1,pa0,pa1=attn_in_grad((3,1),dqkv,wqkv)
        d_sum=add2(pd0,partner(pd1))
        d_in=hop_a(d_sum)
        rb=partner(pa1)
        pb0,pb1,o0,o1=attn_in_grad((2,0),after(dqkv,d_sum),wqkv)
        ra,ro=partner(pb1),partner(o1)
        a_sum=add2(pa0,ra)
        a_in=hop_a(a_sum)
        b_sum=(pb0.astype(f32)+after(rb,a_sum).astype(f32)+d_in.astype(f32)).astype(bf16)
        b_in=hop_b(b_sum)
        h1pd=partner(after(h1d,dqkv))
        h1=[h1_local,h1p,h1a,h1pb,h1b,h1pa,h1d,h1pd]
        grad_wqkv=gathered_mm(lambda x,o: jnp.dot(o[...],x,preferred_element_type=f32),h1,after(dqkv,b_sum),3,
            pl.BlockSpec((3*NH*E,768),lambda s:(0,s)),jax.ShapeDtypeStruct((3*NH*E,D),f32),6*T*D*NH*E)
        dx,vec1=ln_bwd((after(o0,grad_wqkv),ro,a_in,b_in),x_in,mid,g1)
        grad_vecs=jnp.concatenate([vec1[:2],vec2],axis=0)
        def all_sum(vecs,k): return vecs+send(vecs,[(i,i^k) for i in range(8)])
        vecs=all_sum(grad_vecs,1)
        grad_wproj=gathered_mm(lambda x,o: jnp.dot(o[...],x,preferred_element_type=f32),dx1,after(ctx,dx).reshape(NH*E,T),3,
            pl.BlockSpec((NH*E,768),lambda s:(0,s)),jax.ShapeDtypeStruct((NH*E,D),f32),2*T*D*NH*E)
        vecs=all_sum(after(vecs,grad_wproj),2)
        grad_bqkv=jnp.sum(after(dqkv,grad_wproj),axis=1,dtype=f32).reshape(3,NH,E)
        grad_vecs=all_sum(vecs,4)
        grad_wproj=grad_wproj.reshape(NH,E,D)
        grad_wqkv=grad_wqkv.reshape(3,NH,E,D).transpose(0,3,1,2)
        return dx[None], grad_wqkv, grad_bqkv, grad_wproj, grad_wfc1, grad_bfc1, grad_wfc2, grad_vecs

    tok_spec = P('dp', 'tp', None)
    head_spec = P('dp', None, 'tp', None)
    in_specs = (tok_spec, tok_spec, tok_spec, head_spec, head_spec, head_spec, P('dp', None, 'tp'),
                P(None), P(None), P(None), P(None),
                P(None, None, 'tp', None), P('tp', None, None), P(None, 'tp'), P('tp', None))
    out_specs = (tok_spec, P('dp', None, 'tp', None), P('dp', 'tp', None), P(('dp', 'tp'), None, None),
                 P('dp', 'tp'), P(('dp', 'tp')), P(('dp', 'tp'), None), P('dp', None))
    return jax.shard_map(layer, mesh=mesh, in_specs=in_specs, out_specs=out_specs, check_vma=False)
```

profile of v0, /device:TPU:0, one launch (start us, length us, event | category | flops | bytes accessed | tf_op | source)
XLA Modules:
  0.0 367.4 jit_solution(13139772977651194358)
XLA Ops:
  0.6 0.8 collective-permute-start
  1.4 2.5 collective-permute-start.1
  3.9 1.5 collective-permute-start.2
  6.0 11.9 %gelu.1 = (bf16[2048,1152]{1,0:T(8,128)(2,1)}, f32[2048,1152]{1,0:T(8,128)}) custom-call(s32[8]{0:T(128)} %fusion.13.blk_ref, bf16[2048,1152]{1,0:T(8,128)(2,1)} %bitcast.64), custom_call_target="tpu_custom_call" | custom-call | flops 2359296000 | bytes 20971520 | tf_op jit(solution)/shard_map/gelu/pallas_call | solution.py:186
  17.9 13.8 %shard_map.206 = (bf16[2048,1152]{1,0:T(8,128)(2,1)}, f32[8,1152]{1,0:T(8,128)S(1)}, bf16[256,2304]{1,0:T(8,128)(2,1)S(1)}, bf16[256,2304]{1,0:T(8,128)(2,1)S(1)}) custom-call(bf16[256,2304]{1,0:T(8,128)(2,1)S(1)} %bitcast.33, bf16[256,2304]{1,0:T(8,128)(2,1)S(1)} %collective-permute-done.refs_1_, f32[2048,1152]{1,0:T(8,128)} %get-tuple-element.64.refs_2_.refs_4_, ...), custom_call_target="tpu_custom_call" | custom-call | flops 5435817984 | bytes 20971520 | tf_op jit(solution)/shard_map/pallas_call | solution.py:242
  31.6 0.6 copy-done.12
  33.3 15.2 %collective-permute-done.6.refs_0_.refs_6_ = bf16[256,2304]{1,0:T(8,128)(2,1)S(1)} collective-permute-done((bf16[256,2304]{1,0:T(8,128)(2,1)S(1)}, bf16[256,2304]{1,0:T(8,128)(2,1)S(1)}, u32[]{:S(2)}, u32[]{:S(2)}) %collective-permute-start.6) | collective-permute-done | bytes 1179680 | tf_op jit(solution)/shard_map/ppermute | solution.py:131
  48.8 1.1 copy-done.42
  50.3 22.5 %shard_map.207 = (bf16[2048,1152]{1,0:T(8,128)(2,1)}, f32[8,1152]{1,0:T(8,128)S(1)}, bf16[256,2304]{1,0:T(8,128)(2,1)S(1)}, bf16[256,2304]{1,0:T(8,128)(2,1)S(1)...) custom-call(bf16[256,2304]{1,0:T(8,128)(2,1)S(1)} %collective-permute-done.1.refs_, ...), custom_call_target="tpu_custom_call", output_to_operand_aliasing={{0}: (7, {})} | custom-call | flops 10871635968 | bytes 20971520 | tf_op jit(solution)/shard_map/pallas_call | solution.py:242
  72.8 0.6 copy-done.14
  73.4 13.8 %shard_map.208 = (bf16[2048,1152]{1,0:T(8,128)(2,1)}, f32[8,1152]{1,0:T(8,128)S(1)}, bf16[256,2304]{1,0:T(8,128)(2,1)S(1)}, bf16[256,2304]{1,0:T(8,128)(2,1)S(1)}) custom-call(bf16[256,2304]{1,0:T(8,128)(2,1)S(1)} %collective-permute-done.6.refs_0_.refs_6_, ...), custom_call_target="tpu_custom_call", output_to_operand_aliasing={{0}: (5, {})} | custom-call | flops 5435817984 | bytes 20971520 | tf_op jit(solution)/shard_map/pallas_call | solution.py:242
  89.4 1.4 collective-permute-start.21
  92.6 1.0 copy-done.19
  94.3 14.3 %shard_map.209 = (bf16[3,96,2048]{2,1,0:T(8,128)(2,1)S(1)}, f32[2,1,2048]{2,1,0:T(1,128)S(1)}) custom-call(s32[1]{0:T(128)} %bitcast.me_ref._, bf16[3,96,2048]{2,1,0:T(8,128)(2,1)S(1)} %bitcast.43, bf16[3,96,2048]{2,1,0:T(8,128)(2,1)S(1)} %bitcast.47, bf16[3,96,2048]{2,1,0:T(8,128)(2,1)S(1)} %bitcast.51, s32[1]{0:T(128)} %bitcast.me_ref._), custom_call_target="tpu_custom_call" | custom-call | flops 5368709120 | bytes 6291456 | tf_op jit(solution)/shard_map/pallas_call | solution.py:102
  108.6 1.5 collective-permute-start.12
  110.2 19.5 %collective-permute-done.9 = bf16[256,2304]{1,0:T(8,128)(2,1)S(1)} collective-permute-done((bf16[256,2304]{1,0:T(8,128)(2,1)S(1)}, bf16[256,2304]{1,0:T(8,128)(2,1)S(1)}, u32[]{:S(2)}, u32[]{:S(2)}) %collective-permute-start.9) | collective-permute-done | bytes 1179680 | tf_op jit(solution)/shard_map/ppermute | solution.py:131
  130.7 0.6 reshape.76.gain
  131.8 7.1 %shard_map.210 = (bf16[3,96,2048]{2,1,0:T(8,128)(2,1)S(1)}, f32[1,1,2048]{2,1,0:T(1,128)S(1)}) custom-call(s32[1]{0:T(128)} %bitcast.me_ref._, bf16[3,96,2048]{2,1,0:T(8,128)(2,1)S(1)} %bitcast.44, bf16[3,96,2048]{2,1,0:T(8,128)(2,1)S(1)} %bitcast.48, bf16[3,96,2048]{2,1,0:T(8,128)(2,1)S(1)} %bitcast.52, ...), custom_call_target="tpu_custom_call", output_to_operand_aliasing={{0}: (4, {})} | custom-call | flops 2684354560 | bytes 3145728 | tf_op jit(solution)/shard_map/pallas_call | solution.py:102
  139.0 1.0 copy-done.9
  140.0 1.5 collective-permute-start.25
  141.5 10.0 %collective-permute-done.12.a_in = bf16[256,2304]{1,0:T(8,128)(2,1)S(1)} collective-permute-done((bf16[256,2304]{1,0:T(8,128)(2,1)S(1)}, bf16[256,2304]{1,0:T(8,128)(2,1)S(1)}, u32[]{:S(2)}, u32[]{:S(2)}) %collective-permute-start.12) | collective-permute-done | bytes 1179680 | tf_op jit(solution)/shard_map/ppermute | solution.py:131
  151.6 1.0 copy-done.33
  152.6 2.8 collective-permute-done.13.b_in
  155.3 6.3 %shard_map.211 = (bf16[256,2304]{1,0:T(8,128)(2,1)}, f32[4,8,2304]{2,1,0:T(8,128)}) custom-call(bf16[256,2304]{1,0:T(8,128)(2,1)} %copy-done.10, bf16[256,2304]{1,0:T(8,128)(2,1)} %copy-done.32, bf16[256,2304]{1,0:T(8,128)(2,1)} %copy-done.33, bf16[256,2304]{1,0:T(8,128)(2,1)} %collective-permute-done.13.b_in, bf16[256,2304]{1,0:T(8,128)(2,1)} %bitcast.55, ...), custom_call_target="tpu_custom_call" | custom-call | flops 589824000 | bytes 6291456 | tf_op jit(solution)/shard_map/pallas_call | solution.py:165
  161.6 0.9 collective-permute-start.17
  162.5 1.1 collective-permute-start.14
  163.9 19.0 %shard_map.212 = f32[1152,2304]{1,0:T(8,128)} custom-call(bf16[256,2304]{1,0:T(8,128)(2,1)} %bitcast.32, bf16[256,2304]{1,0:T(8,128)(2,1)} %copy-done.6, bf16[256,2304]{1,0:T(8,128)(2,1)} %copy-done.25, bf16[256,2304]{1,0:T(8,128)(2,1)} %copy-done.42, bf16[256,2304]{1,0:T(8,128)(2,1)} %collective-permute-done.2.refs_2_.refs_4_, ...), custom_call_target="tpu_custom_call" | custom-call | flops 10871635968 | bytes 31457280 | tf_op jit(solution)/shard_map/pallas_call | solution.py:293
  183.0 8.7 %collective-permute-done.14.refs_2_ = bf16[256,2304]{1,0:T(8,128)(2,1)} collective-permute-done((bf16[256,2304]{1,0:T(8,128)(2,1)}, bf16[256,2304]{1,0:T(8,128)(2,1)}, u32[]{:S(2)}, u32[]{:S(2)}) %collective-permute-start.14) | collective-permute-done | bytes 1179680 | tf_op jit(solution)/shard_map/ppermute | solution.py:131
  192.2 1.5 fusion.11.refs_0_
  194.8 1.1 collective-permute-start.15
  195.9 19.1 %shard_map.213 = f32[2304,1152]{1,0:T(8,128)} custom-call(bf16[256,2304]{1,0:T(8,128)(2,1)} %copy-done.31, bf16[256,2304]{1,0:T(8,128)(2,1)} %collective-permute-done.20.refs_1_, bf16[256,2304]{1,0:T(8,128)(2,1)} %collective-permute-done.21.refs_2_, bf16[256,2304]{1,0:T(8,128)(2,1)} %collective-permute-done.23.refs_3_, ...), custom_call_target="tpu_custom_call" | custom-call | flops 10871635968 | bytes 31457280 | tf_op jit(solution)/shard_map/pallas_call | solution.py:293
  215.0 4.3 %shard_map.214.refs_3_ = bf16[288,2048]{1,0:T(8,128)(2,1)S(1)} custom-call(bf16[256,2304]{1,0:T(8,128)(2,1)S(1)} %copy-done, bf16[256,2304]{1,0:T(8,128)(2,1)} %collective-permute-done.16.refs_1_, bf16[256,2304]{1,0:T(8,128)(2,1)} %collective-permute-done.14.refs_2_, bf16[256,2304]{1,0:T(8,128)(2,1)} %collective-permute-done.18.refs_3_, ...), custom_call_target="tpu_custom_call" | custom-call | flops 2038431744 | bytes 10485760 | tf_op jit(solution)/shard_map/pallas_call | solution.py:314
  219.5 0.9 collective-permute-start.30
  220.4 2.1 collective-permute-done.27.refs_1_.refs_7_
  222.5 2.6 shard_map.215
  225.2 22.6 %shard_map.216._ = bf16[3,3,96,2048]{3,2,1,0:T(8,128)(2,1)S(1)} custom-call(s32[1]{0:T(128)} %bitcast.me_ref._, bf16[3,96,2048]{2,1,0:T(8,128)(2,1)S(1)} %bitcast.45, bf16[3,96,2048]{2,1,0:T(8,128)(2,1)S(1)} %bitcast.49, bf16[3,96,2048]{2,1,0:T(8,128)(2,1)S(1)} %bitcast.53, bf16[3,96,2048]{2,1,0:T(8,128)(2,1)S(1)} %bitcast.34, f32[2,1,2048]{2,1,0:T(1,128)S(1)} %copy-done.27, ...), custom_call_target="tpu_custom_call" | custom-call | flops 10737418240 | bytes 6291456 | tf_op jit(solution)/shard_map/pallas_call | solution.py:102
  247.8 11.3 %shard_map.217 = bf16[3,3,96,2048]{3,2,1,0:T(8,128)(2,1)S(1)} custom-call(s32[1]{0:T(128)} %bitcast.me_ref._, bf16[3,96,2048]{2,1,0:T(8,128)(2,1)S(1)} %bitcast.46, bf16[3,96,2048]{2,1,0:T(8,128)(2,1)S(1)} %bitcast.50, bf16[3,96,2048]{2,1,0:T(8,128)(2,1)S(1)} %bitcast.54, bf16[3,96,2048]{2,1,0:T(8,128)(2,1)S(1)} %bitcast.35, ...), custom_call_target="tpu_custom_call", output_to_operand_aliasing={{}: (6, {})} | custom-call | flops 5368709120 | bytes 3145728 | tf_op jit(solution)/shard_map/pallas_call | solution.py:102
  259.1 9.1 %shard_map.218 = (bf16[256,2304]{1,0:T(8,128)(2,1)S(1)}, bf16[256,2304]{1,0:T(8,128)(2,1)S(1)}, bf16[256,2304]{1,0:T(8,128)(2,1)S(1)}, bf16[256,2304]{1,0:T(8,128)(2,1)S(1)}) custom-call(bf16[864,2048]{1,0:T(8,128)(2,1)S(1)} %bitcast.36, bf16[864,2304]{1,0:T(8,128)(2,1)S(1)} %bitcast.41), custom_call_target="tpu_custom_call" | custom-call | flops 4076863488 | bytes 31457280 | tf_op jit(solution)/shard_map/pallas_call | solution.py:174
  268.4 0.9 collective-permute-start.31
  269.3 1.1 collective-permute-start.34
  270.4 0.7 collective-permute-done.28
  271.4 9.7 %shard_map.219 = (bf16[256,2304]{1,0:T(8,128)(2,1)S(1)}, bf16[256,2304]{1,0:T(8,128)(2,1)S(1)}, bf16[256,2304]{1,0:T(8,128)(2,1)S(1)}, bf16[256,2304]{1,0:T(8,128)(2,1)}) custom-call(bf16[864,2048]{1,0:T(8,128)(2,1)S(1)} %bitcast.37, bf16[864,2304]{1,0:T(8,128)(2,1)S(1)} %bitcast.42), custom_call_target="tpu_custom_call" | custom-call | flops 4076863488 | bytes 31457280 | tf_op jit(solution)/shard_map/pallas_call | solution.py:174
  281.7 0.9 collective-permute-start.38
  282.6 27.4 %collective-permute-done.34.refs_6_ = bf16[256,2304]{1,0:T(8,128)(2,1)} collective-permute-done((bf16[256,2304]{1,0:T(8,128)(2,1)}, bf16[256,2304]{1,0:T(8,128)(2,1)}, u32[]{:S(2)}, u32[]{:S(2)}) %collective-permute-start.34) | collective-permute-done | bytes 1179680 | tf_op jit(solution)/shard_map/ppermute | solution.py:131
  311.6 1.5 add_convert_fusion
  313.1 0.9 collective-permute-start.41
  314.0 2.3 collective-permute-done.32.refs_3_
  316.2 0.9 collective-permute-start.40
  317.2 0.6 broadcast_in_dim.4.gain
  317.8 1.7 reduce_sum.79
  319.4 14.4 %shard_map.220 = f32[864,2304]{1,0:T(8,128)} custom-call(bf16[256,2304]{1,0:T(8,128)(2,1)} %fusion.11.refs_0_, bf16[256,2304]{1,0:T(8,128)(2,1)} %copy-done.45, bf16[256,2304]{1,0:T(8,128)(2,1)} %collective-permute-done.30.refs_2_, bf16[256,2304]{1,0:T(8,128)(2,1)} %copy-done.46, bf16[256,2304]{1,0:T(8,128)(2,1)} %copy-done.44, ...), custom_call_target="tpu_custom_call" | custom-call | flops 8153726976 | bytes 31457280 | tf_op jit(solution)/shard_map/pallas_call | solution.py:293
  333.9 6.1 %collective-permute-done.41.b_in = bf16[256,2304]{1,0:T(8,128)(2,1)S(1)} collective-permute-done((bf16[256,2304]{1,0:T(8,128)(2,1)}, bf16[256,2304]{1,0:T(8,128)(2,1)S(1)}, u32[]{:S(2)}, u32[]{:S(2)}) %collective-permute-start.41) | collective-permute-done | bytes 1179680 | tf_op jit(solution)/shard_map/ppermute | solution.py:131
  340.0 1.7 collective-permute-done.40.a_in
  341.7 6.1 %shard_map.221 = (bf16[256,2304]{1,0:T(8,128)(2,1)}, f32[4,8,2304]{2,1,0:T(8,128)}) custom-call(bf16[256,2304]{1,0:T(8,128)(2,1)} %copy-done.11, bf16[256,2304]{1,0:T(8,128)(2,1)} %copy-done.34, bf16[256,2304]{1,0:T(8,128)(2,1)} %collective-permute-done.40.a_in, bf16[256,2304]{1,0:T(8,128)(2,1)} %copy-done.35, bf16[256,2304]{1,0:T(8,128)(2,1)} %bitcast.59, ...), custom_call_target="tpu_custom_call" | custom-call | flops 589824000 | bytes 6291456 | tf_op jit(solution)/shard_map/pallas_call | solution.py:165
  347.8 1.0 reduce_sum.78
  348.9 0.8 pad_maximum_fusion
  350.0 7.8 %shard_map.222 = f32[288,2304]{1,0:T(8,128)} custom-call(bf16[256,2304]{1,0:T(8,128)(2,1)} %get-tuple-element.84.refs_0_.skip, bf16[256,2304]{1,0:T(8,128)(2,1)} %collective-permute-done.16.refs_1_, bf16[256,2304]{1,0:T(8,128)(2,1)} %collective-permute-done.14.refs_2_, bf16[256,2304]{1,0:T(8,128)(2,1)} %collective-permute-done.18.refs_3_, ...), custom_call_target="tpu_custom_call" | custom-call | flops 2717908992 | bytes 31457280 | tf_op jit(solution)/shard_map/pallas_call | solution.py:293
  357.9 1.0 collective-permute-start.43
  358.9 0.6 add_reduce_fusion
  359.5 2.8 collective-permute-done.43
  362.3 0.9 collective-permute-start.44
  363.8 0.7 reshape.83
  364.5 2.2 collective-permute-done.44
  366.7 0.6 add.116
  (167 shorter events, 13.8 us)
Async XLA Ops:
  0.6 17.2 %collective-permute-start = (bf16[256,2304]{1,0:T(8,128)(2,1)}, bf16[256,2304]{1,0:T(8,128)(2,1)S(1)}, u32[]{:S(2)}, u32[]{:S(2)}) collective-permute-start(bf16[256,2304]{1,0:T(8,128)(2,1)} %bitcast.28), channel_id=1, source_target_pairs={{0,1},{1,0},{2,3},{3,2},{4,5},{5,4},{6,7},{7,6},{8,9},{9,8},{10,11... | collective-permute-start | bytes 3538952 | tf_op jit(solution)/shard_map/ppermute | solution.py:131
  1.4 30.9 %collective-permute-start.1 = (bf16[256,2304]{1,0:T(8,128)(2,1)}, bf16[256,2304]{1,0:T(8,128)(2,1)S(1)}, u32[]{:S(2)}, u32[]{:S(2)}) collective-permute-start(bf16[256,2304]{1,0:T(8,128)(2,1)} %bitcast.29), channel_id=1, source_target_pairs={{0,2},{1,5},{2,0},{3,7},{4,6},{5,1},{6,4},{7,3},{8,10},{9,13},{10,... | collective-permute-start | bytes 3538952 | tf_op jit(solution)/shard_map/ppermute | solution.py:131
  3.9 28.9 %collective-permute-start.2 = (bf16[256,2304]{1,0:T(8,128)(2,1)}, bf16[256,2304]{1,0:T(8,128)(2,1)}, u32[]{:S(2)}, u32[]{:S(2)}) collective-permute-start(bf16[256,2304]{1,0:T(8,128)(2,1)} %bitcast.30), channel_id=1, source_target_pairs={{0,4},{1,3},{2,6},{3,1},{4,0},{5,7},{6,2},{7,5},{8,12},{9,11},{10,... | collective-permute-start | bytes 3538952 | tf_op jit(solution)/shard_map/ppermute | solution.py:131
  6.0 11.9 %copy-start.2 = (bf16[1,256,2304]{2,1,0:T(8,128)(2,1)S(1)}, bf16[1,256,2304]{2,1,0:T(8,128)(2,1)}, u32[]{:S(2)}) copy-start(bf16[1,256,2304]{2,1,0:T(8,128)(2,1)} %param.17) | copy-start | bytes 3538948
  17.8 13.8 %copy-start.6 = (bf16[256,2304]{1,0:T(8,128)(2,1)}, bf16[256,2304]{1,0:T(8,128)(2,1)S(1)}, u32[]{:S(2)}) copy-start(bf16[256,2304]{1,0:T(8,128)(2,1)S(1)} %collective-permute-done.refs_1_) | copy-start | bytes 3538948
  17.8 30.6 %copy-start.28 = (bf16[1,256,2304]{2,1,0:T(8,128)(2,1)S(1)}, bf16[1,256,2304]{2,1,0:T(8,128)(2,1)}, u32[]{:S(2)}) copy-start(bf16[1,256,2304]{2,1,0:T(8,128)(2,1)} %param.16) | copy-start | bytes 3538948
  32.2 16.5 %copy-start.10 = (bf16[256,2304]{1,0:T(8,128)(2,1)}, bf16[256,2304]{1,0:T(8,128)(2,1)S(1)}, u32[]{:S(2)}) copy-start(bf16[256,2304]{1,0:T(8,128)(2,1)S(1)} %get-tuple-element.80.own) | copy-start | bytes 3538948
  32.3 40.5 %copy-start.25 = (bf16[256,2304]{1,0:T(8,128)(2,1)}, bf16[256,2304]{1,0:T(8,128)(2,1)S(1)}, u32[]{:S(2)}) copy-start(bf16[256,2304]{1,0:T(8,128)(2,1)S(1)} %collective-permute-done.1.refs_0_.refs_2_) | copy-start | bytes 3538948
  32.3 16.2 %collective-permute-start.6 = (bf16[256,2304]{1,0:T(8,128)(2,1)S(1)}, bf16[256,2304]{1,0:T(8,128)(2,1)S(1)}, u32[]{:S(2)}, u32[]{:S(2)}) collective-permute-start(bf16[256,2304]{1,0:T(8,128)(2,1)S(1)} %collective-permute-done.1.refs_0_.refs_2_), channel_id=1, source_target_pairs={{0,4},{1,3},{2,6},{3,1},{4,0},{5,7},{6,2},{7,5},{8,12},{9,11},{10,... | collective-permute-start | bytes 3538952 | tf_op jit(solution)/shard_map/ppermute | solution.py:131
  32.8 15.9 %collective-permute-start.3 = (bf16[256,2304]{1,0:T(8,128)(2,1)}, bf16[256,2304]{1,0:T(8,128)(2,1)S(1)}, u32[]{:S(2)}, u32[]{:S(2)}) collective-permute-start(bf16[256,2304]{1,0:T(8,128)(2,1)} %collective-permute-done.2.refs_2_.refs_4_), channel_id=1, source_target_pairs={{0,1},{1,0},{2,3},{3,2},{4,5},{5,4},{6,7},{7,6},{8,9},{9,8},{10,11... | collective-permute-start | bytes 3538952 | tf_op jit(solution)/shard_map/ppermute | solution.py:131
  32.8 16.0 %collective-permute-start.4 = (bf16[256,2304]{1,0:T(8,128)(2,1)S(1)}, bf16[256,2304]{1,0:T(8,128)(2,1)S(1)}, u32[]{:S(2)}, u32[]{:S(2)}) collective-permute-start(bf16[256,2304]{1,0:T(8,128)(2,1)S(1)} %collective-permute-done.1.refs_0_.refs_2_), channel_id=1, source_target_pairs={{0,1},{1,0},{2,3},{3,2},{4,5},{5,4},{6,7},{7,6},{8,9},{9,8},{10,11... | collective-permute-start | bytes 3538952 | tf_op jit(solution)/shard_map/ppermute | solution.py:131
  48.5 24.9 %copy-start.7 = (bf16[256,2304]{1,0:T(8,128)(2,1)}, bf16[256,2304]{1,0:T(8,128)(2,1)S(1)}, u32[]{:S(2)}) copy-start(bf16[256,2304]{1,0:T(8,128)(2,1)S(1)} %collective-permute-done.6.refs_0_.refs_6_) | copy-start | bytes 3538948
  48.5 24.9 %collective-permute-start.7 = (bf16[256,2304]{1,0:T(8,128)(2,1)S(1)}, bf16[256,2304]{1,0:T(8,128)(2,1)S(1)}, u32[]{:S(2)}, u32[]{:S(2)}) collective-permute-start(bf16[256,2304]{1,0:T(8,128)(2,1)S(1)} %collective-permute-done.6.refs_0_.refs_6_), channel_id=1, source_target_pairs={{0,1},{1,0},{2,3},{3,2},{4,5},{5,4},{6,7},{7,6},{8,9},{9,8},{10,11... | collective-permute-start | bytes 3538952 | tf_op jit(solution)/shard_map/ppermute | solution.py:131
  73.4 13.8 %copy-start.8 = (bf16[256,2304]{1,0:T(8,128)(2,1)}, bf16[256,2304]{1,0:T(8,128)(2,1)S(1)}, u32[]{:S(2)}) copy-start(bf16[256,2304]{1,0:T(8,128)(2,1)S(1)} %collective-permute-done.7.refs_1_.refs_7_) | copy-start | bytes 3538948
  87.2 3.6 collective-permute-start.8
  88.1 3.7 %collective-permute-start.11 = (bf16[256,2304]{1,0:T(8,128)(2,1)S(1)}, bf16[256,2304]{1,0:T(8,128)(2,1)S(1)}, u32[]{:S(2)}, u32[]{:S(2)}) collective-permute-start(bf16[256,2304]{1,0:T(8,128)(2,1)S(1)} %get-tuple-element.83), channel_id=1, source_target_pairs={{0,1},{1,0},{2,3},{3,2},{4,5},{5,4},{6,7},{7,6},{8,9},{9,8},{10,11... | collective-permute-start | bytes 3538952 | tf_op jit(solution)/shard_map/ppermute | solution.py:131
  88.8 42.5 %copy-start.31 = (bf16[256,2304]{1,0:T(8,128)(2,1)}, bf16[256,2304]{1,0:T(8,128)(2,1)S(1)}, u32[]{:S(2)}) copy-start(bf16[256,2304]{1,0:T(8,128)(2,1)S(1)} %fusion.7.refs_0_) | copy-start | bytes 3538948
  88.8 42.5 %collective-permute-start.22 = (bf16[256,2304]{1,0:T(8,128)(2,1)S(1)}, bf16[256,2304]{1,0:T(8,128)(2,1)}, u32[]{:S(2)}, u32[]{:S(2)}) collective-permute-start(bf16[256,2304]{1,0:T(8,128)(2,1)S(1)} %fusion.7.refs_0_), channel_id=1, source_target_pairs={{0,4},{1,3},{2,6},{3,1},{4,0},{5,7},{6,2},{7,5},{8,12},{9,11},{10,... | collective-permute-start | bytes 3538952 | tf_op jit(solution)/shard_map/ppermute | solution.py:131
  89.4 42.4 %collective-permute-start.21 = (bf16[256,2304]{1,0:T(8,128)(2,1)S(1)}, bf16[256,2304]{1,0:T(8,128)(2,1)}, u32[]{:S(2)}, u32[]{:S(2)}) collective-permute-start(bf16[256,2304]{1,0:T(8,128)(2,1)S(1)} %fusion.7.refs_0_), channel_id=1, source_target_pairs={{0,2},{1,5},{2,0},{3,7},{4,6},{5,1},{6,4},{7,3},{8,10},{9,13},{10,... | collective-permute-start | bytes 3538952 | tf_op jit(solution)/shard_map/ppermute | solution.py:131
  90.8 49.2 %collective-permute-start.10 = (bf16[256,2304]{1,0:T(8,128)(2,1)S(1)}, bf16[256,2304]{1,0:T(8,128)(2,1)S(1)}, u32[]{:S(2)}, u32[]{:S(2)}) collective-permute-start(bf16[256,2304]{1,0:T(8,128)(2,1)S(1)} %get-tuple-element.81), channel_id=1, source_target_pairs={{0,1},{1,0},{2,3},{3,2},{4,5},{5,4},{6,7},{7,6},{8,9},{9,8},{10,11... | collective-permute-start | bytes 3538952 | tf_op jit(solution)/shard_map/ppermute | solution.py:131
  90.8 17.8 %collective-permute-start.5 = (bf16[256,2304]{1,0:T(8,128)(2,1)S(1)}, bf16[256,2304]{1,0:T(8,128)(2,1)S(1)}, u32[]{:S(2)}, u32[]{:S(2)}) collective-permute-start(bf16[256,2304]{1,0:T(8,128)(2,1)S(1)} %get-tuple-element.70), channel_id=1, source_target_pairs={{0,1},{1,0},{2,3},{3,2},{4,5},{5,4},{6,7},{7,6},{8,9},{9,8},{10,11... | collective-permute-start | bytes 3538952 | tf_op jit(solution)/shard_map/ppermute | solution.py:131
  91.8 37.9 %collective-permute-start.9 = (bf16[256,2304]{1,0:T(8,128)(2,1)S(1)}, bf16[256,2304]{1,0:T(8,128)(2,1)S(1)}, u32[]{:S(2)}, u32[]{:S(2)}) collective-permute-start(bf16[256,2304]{1,0:T(8,128)(2,1)S(1)} %add_convert_fusion.5), channel_id=1, source_target_pairs={{0,2},{1,5},{2,0},{3,7},{4,6},{5,1},{6,4},{7,3},{8,10},{9,13},{10,... | collective-permute-start | bytes 3538952 | tf_op jit(solution)/shard_map/ppermute | solution.py:131
  108.6 21.5 %copy-start.26 = (f32[2,1,2048]{2,1,0:T(1,128)}, f32[2,1,2048]{2,1,0:T(1,128)S(1)}, u32[]{:S(2)}) copy-start(f32[2,1,2048]{2,1,0:T(1,128)S(1)} %get-tuple-element.75.lse_ref) | copy-start | bytes 49156
  108.6 42.9 %collective-permute-start.12 = (bf16[256,2304]{1,0:T(8,128)(2,1)S(1)}, bf16[256,2304]{1,0:T(8,128)(2,1)S(1)}, u32[]{:S(2)}, u32[]{:S(2)}) collective-permute-start(bf16[256,2304]{1,0:T(8,128)(2,1)S(1)} %add_convert_fusion.3), channel_id=1, source_target_pairs={{0,2},{1,5},{2,0},{3,7},{4,6},{5,1},{6,4},{7,3},{8,10},{9,13},{10,... | collective-permute-start | bytes 3538952 | tf_op jit(solution)/shard_map/ppermute | solution.py:131
  130.1 25.2 %collective-permute-start.13 = (bf16[256,2304]{1,0:T(8,128)(2,1)S(1)}, bf16[256,2304]{1,0:T(8,128)(2,1)}, u32[]{:S(2)}, u32[]{:S(2)}) collective-permute-start(bf16[256,2304]{1,0:T(8,128)(2,1)S(1)} %add_convert_fusion.4), channel_id=1, source_target_pairs={{0,4},{1,3},{2,6},{3,1},{4,0},{5,7},{6,2},{7,5},{8,12},{9,11},{10,... | collective-permute-start | bytes 3538952 | tf_op jit(solution)/shard_map/ppermute | solution.py:131
  131.3 62.4 %collective-permute-start.20 = (bf16[256,2304]{1,0:T(8,128)(2,1)S(1)}, bf16[256,2304]{1,0:T(8,128)(2,1)}, u32[]{:S(2)}, u32[]{:S(2)}) collective-permute-start(bf16[256,2304]{1,0:T(8,128)(2,1)S(1)} %fusion.7.refs_0_), channel_id=1, source_target_pairs={{0,1},{1,0},{2,3},{3,2},{4,5},{5,4},{6,7},{7,6},{8,9},{9,8},{10,11... | collective-permute-start | bytes 3538952 | tf_op jit(solution)/shard_map/ppermute | solution.py:131
  131.8 62.5 %collective-permute-start.23 = (bf16[256,2304]{1,0:T(8,128)(2,1)}, bf16[256,2304]{1,0:T(8,128)(2,1)}, u32[]{:S(2)}, u32[]{:S(2)}) collective-permute-start(bf16[256,2304]{1,0:T(8,128)(2,1)} %collective-permute-done.22.refs_4_), channel_id=1, source_target_pairs={{0,1},{1,0},{2,3},{3,2},{4,5},{5,4},{6,7},{7,6},{8,9},{9,8},{10,11... | collective-permute-start | bytes 3538952 | tf_op jit(solution)/shard_map/ppermute | solution.py:131
  140.0 23.7 %copy-start.29 = (bf16[1,256,2304]{2,1,0:T(8,128)(2,1)S(1)}, bf16[1,256,2304]{2,1,0:T(8,128)(2,1)}, u32[]{:S(2)}) copy-start(bf16[1,256,2304]{2,1,0:T(8,128)(2,1)} %param.15) | copy-start | bytes 3538948
  140.0 15.3 %copy-start.32 = (bf16[256,2304]{1,0:T(8,128)(2,1)}, bf16[256,2304]{1,0:T(8,128)(2,1)S(1)}, u32[]{:S(2)}) copy-start(bf16[256,2304]{1,0:T(8,128)(2,1)S(1)} %collective-permute-done.10.ro) | copy-start | bytes 3538948
  140.0 43.0 %collective-permute-start.25 = (bf16[256,2304]{1,0:T(8,128)(2,1)}, bf16[256,2304]{1,0:T(8,128)(2,1)}, u32[]{:S(2)}, u32[]{:S(2)}) collective-permute-start(bf16[256,2304]{1,0:T(8,128)(2,1)} %collective-permute-done.21.refs_2_), channel_id=1, source_target_pairs={{0,4},{1,3},{2,6},{3,1},{4,0},{5,7},{6,2},{7,5},{8,12},{9,11},{10,... | collective-permute-start | bytes 3538952 | tf_op jit(solution)/shard_map/ppermute | solution.py:131
  161.6 32.6 %collective-permute-start.17 = (bf16[256,2304]{1,0:T(8,128)(2,1)}, bf16[256,2304]{1,0:T(8,128)(2,1)}, u32[]{:S(2)}, u32[]{:S(2)}) collective-permute-start(bf16[256,2304]{1,0:T(8,128)(2,1)} %get-tuple-element.84.refs_0_.skip), channel_id=1, source_target_pairs={{0,4},{1,3},{2,6},{3,1},{4,0},{5,7},{6,2},{7,5},{8,12},{9,11},{10,... | collective-permute-start | bytes 3538952 | tf_op jit(solution)/shard_map/ppermute | solution.py:131
  162.5 29.2 %collective-permute-start.14 = (bf16[256,2304]{1,0:T(8,128)(2,1)}, bf16[256,2304]{1,0:T(8,128)(2,1)}, u32[]{:S(2)}, u32[]{:S(2)}) collective-permute-start(bf16[256,2304]{1,0:T(8,128)(2,1)} %get-tuple-element.84.refs_0_.skip), channel_id=1, source_target_pairs={{0,2},{1,5},{2,0},{3,7},{4,6},{5,1},{6,4},{7,3},{8,10},{9,13},{10,... | collective-permute-start | bytes 3538952 | tf_op jit(solution)/shard_map/ppermute | solution.py:131
  182.9 9.2 %copy-start.38 = (f32[2304]{0:T(1024)S(1)}, f32[2304]{0:T(1024)}, u32[]{:S(2)}) copy-start(f32[2304]{0:T(1024)} %param.22) | copy-start | bytes 27652
  182.9 9.2 %copy-start.41 = (f32[2304]{0:T(1024)S(1)}, f32[2304]{0:T(1024)}, u32[]{:S(2)}) copy-start(f32[2304]{0:T(1024)} %param.23) | copy-start | bytes 27652
  183.0 11.8 %collective-permute-start.24 = (bf16[256,2304]{1,0:T(8,128)(2,1)}, bf16[256,2304]{1,0:T(8,128)(2,1)}, u32[]{:S(2)}, u32[]{:S(2)}) collective-permute-start(bf16[256,2304]{1,0:T(8,128)(2,1)} %collective-permute-done.21.refs_2_), channel_id=1, source_target_pairs={{0,1},{1,0},{2,3},{3,2},{4,5},{5,4},{6,7},{7,6},{8,9},{9,8},{10,11... | collective-permute-start | bytes 3538952 | tf_op jit(solution)/shard_map/ppermute | solution.py:131
  191.7 4.2 %collective-permute-start.26 = (bf16[256,2304]{1,0:T(8,128)(2,1)}, bf16[256,2304]{1,0:T(8,128)(2,1)}, u32[]{:S(2)}, u32[]{:S(2)}) collective-permute-start(bf16[256,2304]{1,0:T(8,128)(2,1)} %collective-permute-done.25.refs_6_), channel_id=1, source_target_pairs={{0,1},{1,0},{2,3},{3,2},{4,5},{5,4},{6,7},{7,6},{8,9},{9,8},{10,11... | collective-permute-start | bytes 3538952 | tf_op jit(solution)/shard_map/ppermute | solution.py:131
  193.7 21.3 %collective-permute-start.16 = (bf16[256,2304]{1,0:T(8,128)(2,1)S(1)}, bf16[256,2304]{1,0:T(8,128)(2,1)}, u32[]{:S(2)}, u32[]{:S(2)}) collective-permute-start(bf16[256,2304]{1,0:T(8,128)(2,1)S(1)} %copy-done), channel_id=1, source_target_pairs={{0,1},{1,0},{2,3},{3,2},{4,5},{5,4},{6,7},{7,6},{8,9},{9,8},{10,11... | collective-permute-start | bytes 3538952 | tf_op jit(solution)/shard_map/ppermute | solution.py:131
  194.2 20.8 %collective-permute-start.18 = (bf16[256,2304]{1,0:T(8,128)(2,1)}, bf16[256,2304]{1,0:T(8,128)(2,1)}, u32[]{:S(2)}, u32[]{:S(2)}) collective-permute-start(bf16[256,2304]{1,0:T(8,128)(2,1)} %collective-permute-done.17.refs_4_), channel_id=1, source_target_pairs={{0,1},{1,0},{2,3},{3,2},{4,5},{5,4},{6,7},{7,6},{8,9},{9,8},{10,11... | collective-permute-start | bytes 3538952 | tf_op jit(solution)/shard_map/ppermute | solution.py:131
  194.3 20.7 %collective-permute-start.19 = (bf16[256,2304]{1,0:T(8,128)(2,1)}, bf16[256,2304]{1,0:T(8,128)(2,1)}, u32[]{:S(2)}, u32[]{:S(2)}) collective-permute-start(bf16[256,2304]{1,0:T(8,128)(2,1)} %collective-permute-done.14.refs_2_), channel_id=1, source_target_pairs={{0,1},{1,0},{2,3},{3,2},{4,5},{5,4},{6,7},{7,6},{8,9},{9,8},{10,11... | collective-permute-start | bytes 3538952 | tf_op jit(solution)/shard_map/ppermute | solution.py:131
  194.8 20.3 %copy-start.1 = (bf16[3,96,2304]{2,1,0:T(8,128)(2,1)S(1)}, bf16[3,96,2304]{2,1,0:T(8,128)(2,1)}, u32[]{:S(2)}) copy-start(bf16[3,96,2304]{2,1,0:T(8,128)(2,1)} %param.27) | copy-start | bytes 3981316
  194.8 24.7 %collective-permute-start.15 = (bf16[256,2304]{1,0:T(8,128)(2,1)}, bf16[256,2304]{1,0:T(8,128)(2,1)}, u32[]{:S(2)}, u32[]{:S(2)}) collective-permute-start(bf16[256,2304]{1,0:T(8,128)(2,1)} %collective-permute-done.14.refs_2_), channel_id=1, source_target_pairs={{0,4},{1,3},{2,6},{3,1},{4,0},{5,7},{6,2},{7,5},{8,12},{9,11},{10,... | collective-permute-start | bytes 3538952 | tf_op jit(solution)/shard_map/ppermute | solution.py:131
  219.4 3.1 collective-permute-start.27
  219.5 28.3 %collective-permute-start.30 = (bf16[256,2304]{1,0:T(8,128)(2,1)S(1)}, bf16[256,2304]{1,0:T(8,128)(2,1)}, u32[]{:S(2)}, u32[]{:S(2)}) collective-permute-start(bf16[256,2304]{1,0:T(8,128)(2,1)S(1)} %copy-done.30), channel_id=1, source_target_pairs={{0,2},{1,5},{2,0},{3,7},{4,6},{5,1},{6,4},{7,3},{8,10},{9,13},{10,... | collective-permute-start | bytes 3538952 | tf_op jit(solution)/shard_map/ppermute | solution.py:131
  247.8 11.3 %copy-start.18 = (bf16[3,2304,3,96]{1,3,2,0:T(8,128)(2,1)S(1)}, bf16[3,2304,3,96]{1,3,2,0:T(8,128)(2,1)}, u32[]{:S(2)}) copy-start(bf16[3,2304,3,96]{1,3,2,0:T(8,128)(2,1)} %param.26) | copy-start | bytes 11943940
  259.1 12.3 %copy-start.4 = (bf16[3,3,96,2048]{3,2,1,0:T(8,128)(2,1)}, bf16[3,3,96,2048]{3,2,1,0:T(8,128)(2,1)S(1)}, u32[]{:S(2)}) copy-start(bf16[3,3,96,2048]{3,2,1,0:T(8,128)(2,1)S(1)} %shard_map.217) | copy-start | bytes 10616836
  268.3 2.9 collective-permute-start.28
  268.4 41.6 %collective-permute-start.31 = (bf16[256,2304]{1,0:T(8,128)(2,1)S(1)}, bf16[256,2304]{1,0:T(8,128)(2,1)S(1)}, u32[]{:S(2)}, u32[]{:S(2)}) collective-permute-start(bf16[256,2304]{1,0:T(8,128)(2,1)S(1)} %copy-done.30), channel_id=1, source_target_pairs={{0,4},{1,3},{2,6},{3,1},{4,0},{5,7},{6,2},{7,5},{8,12},{9,11},{10,... | collective-permute-start | bytes 3538952 | tf_op jit(solution)/shard_map/ppermute | solution.py:131
  269.3 40.7 %collective-permute-start.34 = (bf16[256,2304]{1,0:T(8,128)(2,1)}, bf16[256,2304]{1,0:T(8,128)(2,1)}, u32[]{:S(2)}, u32[]{:S(2)}) collective-permute-start(bf16[256,2304]{1,0:T(8,128)(2,1)} %collective-permute-done.30.refs_2_), channel_id=1, source_target_pairs={{0,4},{1,3},{2,6},{3,1},{4,0},{5,7},{6,2},{7,5},{8,12},{9,11},{10,... | collective-permute-start | bytes 3538952 | tf_op jit(solution)/shard_map/ppermute | solution.py:131
  281.1 29.7 %copy-start.11 = (bf16[256,2304]{1,0:T(8,128)(2,1)}, bf16[256,2304]{1,0:T(8,128)(2,1)S(1)}, u32[]{:S(2)}) copy-start(bf16[256,2304]{1,0:T(8,128)(2,1)S(1)} %get-tuple-element.109.own) | copy-start | bytes 3538948
  281.1 29.4 %collective-permute-start.37 = (bf16[256,2304]{1,0:T(8,128)(2,1)S(1)}, bf16[256,2304]{1,0:T(8,128)(2,1)S(1)}, u32[]{:S(2)}, u32[]{:S(2)}) collective-permute-start(bf16[256,2304]{1,0:T(8,128)(2,1)S(1)} %get-tuple-element.106), channel_id=1, source_target_pairs={{0,1},{1,0},{2,3},{3,2},{4,5},{5,4},{6,7},{7,6},{8,9},{9,8},{10,11... | collective-permute-start | bytes 3538952 | tf_op jit(solution)/shard_map/ppermute | solution.py:131
  281.3 29.8 %collective-permute-start.36 = (bf16[256,2304]{1,0:T(8,128)(2,1)S(1)}, bf16[256,2304]{1,0:T(8,128)(2,1)S(1)}, u32[]{:S(2)}, u32[]{:S(2)}) collective-permute-start(bf16[256,2304]{1,0:T(8,128)(2,1)S(1)} %get-tuple-element.104), channel_id=1, source_target_pairs={{0,1},{1,0},{2,3},{3,2},{4,5},{5,4},{6,7},{7,6},{8,9},{9,8},{10,11... | collective-permute-start | bytes 3538952 | tf_op jit(solution)/shard_map/ppermute | solution.py:131
  281.7 29.9 %collective-permute-start.38 = (bf16[256,2304]{1,0:T(8,128)(2,1)S(1)}, bf16[256,2304]{1,0:T(8,128)(2,1)S(1)}, u32[]{:S(2)}, u32[]{:S(2)}) collective-permute-start(bf16[256,2304]{1,0:T(8,128)(2,1)S(1)} %add_convert_fusion.2), channel_id=1, source_target_pairs={{0,2},{1,5},{2,0},{3,7},{4,6},{5,1},{6,4},{7,3},{8,10},{9,13},{10,... | collective-permute-start | bytes 3538952 | tf_op jit(solution)/shard_map/ppermute | solution.py:131
  310.0 3.1 collective-permute-start.29
  310.0 9.4 %collective-permute-start.33 = (bf16[256,2304]{1,0:T(8,128)(2,1)}, bf16[256,2304]{1,0:T(8,128)(2,1)}, u32[]{:S(2)}, u32[]{:S(2)}) collective-permute-start(bf16[256,2304]{1,0:T(8,128)(2,1)} %collective-permute-done.30.refs_2_), channel_id=1, source_target_pairs={{0,1},{1,0},{2,3},{3,2},{4,5},{5,4},{6,7},{7,6},{8,9},{9,8},{10,11... | collective-permute-start | bytes 3538952 | tf_op jit(solution)/shard_map/ppermute | solution.py:131
  310.5 5.7 %collective-permute-start.32 = (bf16[256,2304]{1,0:T(8,128)(2,1)S(1)}, bf16[256,2304]{1,0:T(8,128)(2,1)S(1)}, u32[]{:S(2)}, u32[]{:S(2)}) collective-permute-start(bf16[256,2304]{1,0:T(8,128)(2,1)S(1)} %collective-permute-done.31.refs_4_), channel_id=1, source_target_pairs={{0,1},{1,0},{2,3},{3,2},{4,5},{5,4},{6,7},{7,6},{8,9},{9,8},{10,11... | collective-permute-start | bytes 3538952 | tf_op jit(solution)/shard_map/ppermute | solution.py:131
  311.0 8.4 %collective-permute-start.35 = (bf16[256,2304]{1,0:T(8,128)(2,1)}, bf16[256,2304]{1,0:T(8,128)(2,1)}, u32[]{:S(2)}, u32[]{:S(2)}) collective-permute-start(bf16[256,2304]{1,0:T(8,128)(2,1)} %collective-permute-done.34.refs_6_), channel_id=1, source_target_pairs={{0,1},{1,0},{2,3},{3,2},{4,5},{5,4},{6,7},{7,6},{8,9},{9,8},{10,11... | collective-permute-start | bytes 3538952 | tf_op jit(solution)/shard_map/ppermute | solution.py:131
  311.6 22.3 %collective-permute-start.39 = (bf16[256,2304]{1,0:T(8,128)(2,1)}, bf16[256,2304]{1,0:T(8,128)(2,1)S(1)}, u32[]{:S(2)}, u32[]{:S(2)}) collective-permute-start(bf16[256,2304]{1,0:T(8,128)(2,1)} %get-tuple-element.110), channel_id=1, source_target_pairs={{0,1},{1,0},{2,3},{3,2},{4,5},{5,4},{6,7},{7,6},{8,9},{9,8},{10,11... | collective-permute-start | bytes 3538952 | tf_op jit(solution)/shard_map/ppermute | solution.py:131
  313.1 26.9 %collective-permute-start.41 = (bf16[256,2304]{1,0:T(8,128)(2,1)}, bf16[256,2304]{1,0:T(8,128)(2,1)S(1)}, u32[]{:S(2)}, u32[]{:S(2)}) collective-permute-start(bf16[256,2304]{1,0:T(8,128)(2,1)} %add_convert_fusion), channel_id=1, source_target_pairs={{0,4},{1,3},{2,6},{3,1},{4,0},{5,7},{6,2},{7,5},{8,12},{9,11},{10,... | collective-permute-start | bytes 3538952 | tf_op jit(solution)/shard_map/ppermute | solution.py:131
  316.2 25.5 %collective-permute-start.40 = (bf16[256,2304]{1,0:T(8,128)(2,1)S(1)}, bf16[256,2304]{1,0:T(8,128)(2,1)}, u32[]{:S(2)}, u32[]{:S(2)}) collective-permute-start(bf16[256,2304]{1,0:T(8,128)(2,1)S(1)} %add_convert_fusion.1), channel_id=1, source_target_pairs={{0,2},{1,5},{2,0},{3,7},{4,6},{5,1},{6,4},{7,3},{8,10},{9,13},{10,... | collective-permute-start | bytes 3538952 | tf_op jit(solution)/shard_map/ppermute | solution.py:131
  349.6 8.2 %collective-permute-start.42 = (f32[6,2304]{1,0:T(8,128)S(1)}, f32[6,2304]{1,0:T(8,128)S(1)}, u32[]{:S(2)}, u32[]{:S(2)}) collective-permute-start(f32[6,2304]{1,0:T(8,128)S(1)} %pad_maximum_fusion), channel_id=1, source_target_pairs={{0,1},{1,0},{2,3},{3,2},{4,5},{5,4},{6,7},{7,6},{8,9},{9,8},{10,11... | collective-permute-start | bytes 165896 | tf_op jit(solution)/shard_map/ppermute | solution.py:131
  350.0 8.9 %copy-start.17 = (f32[8,1152]{1,0:T(8,128)S(1)}, f32[8,1152]{1,0:T(8,128)}, u32[]{:S(2)}) copy-start(f32[8,1152]{1,0:T(8,128)} %copy-done.16) | copy-start | bytes 110596
  350.0 13.2 %copy-start.5 = (bf16[3,3,96,2048]{3,2,1,0:T(8,128)(2,1)S(1)}, bf16[3,3,96,2048]{3,2,1,0:T(8,128)(2,1)}, u32[]{:S(2)}) copy-start(bf16[3,3,96,2048]{3,2,1,0:T(8,128)(2,1)} %copy-done.4) | copy-start | bytes 10616836
  357.9 4.4 %collective-permute-start.43 = (f32[6,2304]{1,0:T(8,128)S(1)}, f32[6,2304]{1,0:T(8,128)S(1)}, u32[]{:S(2)}, u32[]{:S(2)}) collective-permute-start(f32[6,2304]{1,0:T(8,128)S(1)} %fusion.17), channel_id=1, source_target_pairs={{0,2},{1,3},{2,0},{3,1},{4,6},{5,7},{6,4},{7,5},{8,10},{9,11},{10,... | collective-permute-start | bytes 165896 | tf_op jit(solution)/shard_map/ppermute | solution.py:131
  362.3 4.4 %collective-permute-start.44 = (f32[6,2304]{1,0:T(8,128)S(1)}, f32[6,2304]{1,0:T(8,128)S(1)}, u32[]{:S(2)}, u32[]{:S(2)}) collective-permute-start(f32[6,2304]{1,0:T(8,128)S(1)} %add.115), channel_id=1, source_target_pairs={{0,4},{1,5},{2,6},{3,7},{4,0},{5,1},{6,2},{7,3},{8,12},{9,13},{10,... | collective-permute-start | bytes 165896 | tf_op jit(solution)/shard_map/ppermute | solution.py:131
  (28 other events, 94.5 us)
where the time goes:
time: 368 us; the launch traced here: 367 us
  Pallas kernels  216 us (59%)
  waiting for transfers between devices  102 us (28%)
  starting transfers between devices  27.6 us (8%)
  other arithmetic  12.3 us (3%)
  local copies, waits for them, and re-layouts  8.73 us (2%)
    ppermute x45, waiting for transfers between devices, send(): return lax.ppermute(a, 'tp', pairs)  102 us
    pallas_call x4, Pallas kernels, gathered_mm(): pl.pallas_call(kernel, grid=(n,), in_specs=[any_] * 8 + [pl.BlockSpec(oth...  60.3 us
    pallas_call x4, Pallas kernels, attn_call(): pl.pallas_call(kernel, grid_spec=pltpu.PrefetchScalarGridSpec(num_scalar_...  55.3 us
    pallas_call x3, Pallas kernels, mlp(): pl.pallas_call(kernel, grid=(2 * n,), in_specs=[any_] * (2 * n) + [step]...  50 us
    ppermute x45, starting transfers between devices, send(): return lax.ppermute(a, 'tp', pairs)  27.6 us
    pallas_call x2, Pallas kernels, call(): pl.pallas_call(kernel, grid=grid, in_specs=in_specs, out_specs=out_specs,...  18.8 us
    pallas_call x2, Pallas kernels, ln_bwd(): pl.pallas_call(ln_bwd_kernel, grid=(256 // R,), in_specs=[blk] * 6 + [pl....  12.3 us
    pallas_call x1, Pallas kernels, gelu(): pl.pallas_call(gelu_kernel, name='gelu', grid_spec=pltpu.PrefetchScalarGr...  11.9 us
  transfers between devices with their start and end apart: 45, of which 14 were waited for; matrix products, arithmetic and copies ran while one was open for 3% of the time, Pallas kernels for 48%

commit v1 on v0

--- a/solution.py
+++ b/solution.py
@@ -23,25 +23,33 @@
     r=lax.broadcasted_iota(jnp.int32,s.shape,0); c=lax.broadcasted_iota(jnp.int32,s.shape,1)
     return jnp.where(r<=c,s,fill)
 
-def fwd_kernel(me_ref,q_ref,k_ref,v_ref,_,ctx_ref,lse_ref,kt,sc,acc):
+def fwd_kernel(me_ref,q_ref,k_ref,v_ref,_,ctx_ref,lse_ref,kt,sc,acc,m8):
     i=pl.program_id(1)
     @pl.when(i==0)
     def _(): kt[...]=k_ref[0].T
     q=q_ref[0]
     def rows(j): return pl.ds(pl.multiple_of(j*BQ,BQ),BQ)
+    halves=[(pl.ds(pl.multiple_of(i*BQ+c,BLK),BLK),c) for c in (0,BLK)]
     def p1(j,m):
         s=jnp.dot(kt[rows(j),:],q,preferred_element_type=f32)
         sc[rows(j),:]=s
         return jnp.maximum(m,foldmax8(s))
-    m=lax.fori_loop(0,i,p1,jnp.full((8,BQ),-1e30,f32))
-    s=causal(jnp.dot(kt[rows(i),:],q,preferred_element_type=f32),-1e30)
-    sc[rows(i),:]=s
-    m=jnp.max(jnp.maximum(m,foldmax8(s)),axis=0,keepdims=True)*C2
+    m8[...]=lax.fori_loop(0,i,p1,jnp.full((8,BQ),-1e30,f32))
+    for r,c in halves:
+        s=causal(jnp.dot(kt[r,:],q[:,c:],preferred_element_type=f32),-1e30)
+        sc[r,c:]=s
+        m8[:,c:]=jnp.maximum(m8[:,c:],foldmax8(s))
+    m=jnp.max(m8[...],axis=0,keepdims=True)*C2
     def p2(j,l):
         e=jnp.exp2(sc[rows(j),:]*C2-m)
         sc[rows(j),:]=e
         return l+fold8(e)
-    l=jnp.sum(lax.fori_loop(0,i+1,p2,jnp.zeros((8,BQ),f32)),axis=0,keepdims=True)
+    m8[...]=lax.fori_loop(0,i,p2,jnp.zeros((8,BQ),f32))
+    for r,c in halves:
+        e=jnp.exp2(sc[r,c:]*C2-m[:,c:])
+        sc[r,c:]=e
+        m8[:,c:]+=fold8(e)
+    l=jnp.sum(m8[...],axis=0,keepdims=True)
     inv=1.0/l
     lse_ref[0]=m+jnp.log2(l)
     acc[...]=jnp.zeros_like(acc)
@@ -49,12 +57,14 @@
         p=(sc[rows(j),:]*inv).astype(bf16)
         acc[...]+=jnp.dot(v_ref[0,:,rows(j)],p,preferred_element_type=f32)
         return 0
-    lax.fori_loop(0,i+1,p3,0)
+    lax.fori_loop(0,i,p3,0)
+    for r,c in halves:
+        acc[:,c:]+=jnp.dot(v_ref[0,:,r],(sc[r,c:]*inv[:,c:]).astype(bf16),preferred_element_type=f32)
     for a in range(BQ//BLK):
         pos=rel_pos(i*(BQ//BLK)+a,me_ref[0])
         ctx_ref[0,:,pl.ds(pl.multiple_of(pos*BLK,BLK),BLK)]=acc[:,a*BLK:(a+1)*BLK].astype(bf16)
 
-def bwd_kernel(me_ref,q_ref,k_ref,v_ref,g_ref,lse_ref,_,out_ref,kt,vt,psc,dsc,g_sc,dq,dk,dv):
+def bwd_kernel(me_ref,q_ref,k_ref,v_ref,g_ref,lse_ref,_,out_ref,kt,vt,psc,dsc,g_sc,dq,dk,dv,d8):
     i=pl.program_id(1)
     @pl.when(i==0)
     def _():
@@ -66,24 +76,29 @@
         pos=rel_pos(i*(BQ//BLK)+a,me_ref[0])
         g_sc[:,a*BLK:(a+1)*BLK]=g_ref[0,:,pl.ds(pl.multiple_of(pos*BLK,BLK),BLK)]
     q=q_ref[0]; g=g_sc[...]; lse=lse_ref[0]
-    def tile(j,d,diag):
-        s=jnp.dot(kt[rows(j),:],q,preferred_element_type=f32)
-        p=jnp.exp2(s*C2-lse)
+    halves=[(pl.ds(pl.multiple_of(i*BQ+c,BLK),BLK),c) for c in (0,BLK)]
+    def tile(r,c,diag):
+        s=jnp.dot(kt[r,:],q[:,c:],preferred_element_type=f32)
+        p=jnp.exp2(s*C2-lse[:,c:])
         if diag: p=causal(p,0.0)
-        dp=jnp.dot(vt[rows(j),:],g,preferred_element_type=f32)
-        psc[rows(j),:]=p; dsc[rows(j),:]=dp
-        return d+fold8(p*dp)
-    d=lax.fori_loop(0,i,lambda j,d: tile(j,d,False),jnp.zeros((8,BQ),f32))
-    delta=jnp.sum(tile(i,d,True),axis=0,keepdims=True)
+        dp=jnp.dot(vt[r,:],g[:,c:],preferred_element_type=f32)
+        psc[r,c:]=p; dsc[r,c:]=dp
+        return fold8(p*dp)
+    d8[...]=lax.fori_loop(0,i,lambda j,d: d+tile(rows(j),0,False),jnp.zeros((8,BQ),f32))
+    for r,c in halves: d8[:,c:]+=tile(r,c,True)
+    delta=jnp.sum(d8[...],axis=0,keepdims=True)
     dq[...]=jnp.zeros_like(dq)
+    def grads(r,c):
+        p=psc[r,c:]
+        ds=(p*(dsc[r,c:]-delta[:,c:])*C).astype(bf16)
+        dq[:,c:]+=jnp.dot(k_ref[0,:,r],ds,preferred_element_type=f32)
+        dk[:,r]+=tn(q[:,c:],ds,1,1)
+        dv[:,r]+=tn(g[:,c:],p.astype(bf16),1,1)
     def p2(j,_):
-        p=psc[rows(j),:]
-        ds=(p*(dsc[rows(j),:]-delta)*C).astype(bf16)
-        dq[...]+=jnp.dot(k_ref[0,:,rows(j)],ds,preferred_element_type=f32)
-        dk[:,rows(j)]+=tn(q,ds,1,1)
-        dv[:,rows(j)]+=tn(g,p.astype(bf16),1,1)
+        grads(rows(j),0)
         return 0
-    lax.fori_loop(0,i+1,p2,0)
+    lax.fori_loop(0,i,p2,0)
+    for r,c in halves: grads(r,c)
     for a in range(BQ//BLK):
         pos=rel_pos(i*(BQ//BLK)+a,me_ref[0])
         out_ref[0,0,:,pl.ds(pl.multiple_of(pos*BLK,BLK),BLK)]=dq[:,a*BLK:(a+1)*BLK].astype(bf16)
@@ -112,13 +127,13 @@
     full,qblk,lblk=head_specs(h0)
     return attn_call(fwd_kernel,n,(me,q,k,v),[qblk,full,full],[full,lblk],
         [jax.ShapeDtypeStruct((NH,E,T),bf16),jax.ShapeDtypeStruct((n,1,T),f32)],
-        [pltpu.VMEM((T,E),bf16),pltpu.VMEM((T,BQ),f32),pltpu.VMEM((E,BQ),f32)],NEL*1024,prev)
+        [pltpu.VMEM((T,E),bf16),pltpu.VMEM((T,BQ),f32),pltpu.VMEM((E,BQ),f32),pltpu.VMEM((8,BQ),f32)],NEL*1024,prev)
 def attn_bwd(h0,n,me,q,k,v,g,lse,prev):
     full,qblk,lblk=head_specs(h0)
     return attn_call(bwd_kernel,n,(me,q,k,v,g,lse),[qblk,full,full,full,lblk],
         pl.BlockSpec((3,1,E,T),lambda h,i,me:(0,h+h0,0,0)),jax.ShapeDtypeStruct((3,NH,E,T),bf16),
         [pltpu.VMEM((T,E),bf16),pltpu.VMEM((T,E),bf16),pltpu.VMEM((T,BQ),f32),pltpu.VMEM((T,BQ),f32),
-         pltpu.VMEM((E,BQ),bf16),pltpu.VMEM((E,BQ),f32),pltpu.VMEM((E,T),f32),pltpu.VMEM((E,T),f32)],NEL*2048,prev)
+         pltpu.VMEM((E,BQ),bf16),pltpu.VMEM((E,BQ),f32),pltpu.VMEM((E,T),f32),pltpu.VMEM((E,T),f32),pltpu.VMEM((8,BQ),f32)],NEL*2048,prev)
 
 LN_EPS=1e-5
 GELU_COEF=0.044715
@@ -137,15 +152,24 @@
 
 def add2(a, b): return (a.astype(f32)+b.astype(f32)).astype(bf16)
 
-def layer_norm_fwd(token_rows, norm_gain, norm_bias):
-    rows_f32 = token_rows.astype(f32)
-    centered = rows_f32 - jnp.mean(rows_f32, axis=-1, keepdims=True)
-    inv_std = lax.rsqrt(jnp.mean(centered * centered, axis=-1, keepdims=True) + LN_EPS)
-    return (centered * inv_std * norm_gain + norm_bias).astype(bf16)
-
-def ln_bwd_kernel(own, ro, a_in, b_in, rows, skip, gain, out, vec):
+def ln_fwd_kernel(rows, gain, bias, out):
+    r=rows[...].astype(f32)
+    cen=r-jnp.mean(r,axis=-1,keepdims=True)
+    rstd=lax.rsqrt(jnp.mean(cen*cen,axis=-1,keepdims=True)+LN_EPS)
+    out[...]=(cen*rstd*gain[...]+bias[...]).astype(bf16)
+
+def layer_norm_fwd(rows, gain, bias):
+    R=64
+    blk=pl.BlockSpec((R,D),lambda i:(i,0)); vec=pl.BlockSpec((1,D),lambda i:(0,0))
+    return pl.pallas_call(ln_fwd_kernel,grid=(256//R,),in_specs=[blk,vec,vec],out_specs=blk,out_shape=jax.ShapeDtypeStruct((256,D),bf16),
+        compiler_params=pltpu.CompilerParams(dimension_semantics=("arbitrary",),vmem_limit_bytes=16<<20),
+        cost_estimate=pl.CostEstimate(flops=256*D*1000,bytes_accessed=3<<20,transcendentals=0))(rows,gain.reshape(1,D),bias.reshape(1,D))
+
+def ln_bwd_kernel(own, ro, a_in, *refs):
+    rows, skip, gain, more, out, total, vec=refs[-7:]
     i=pl.program_id(0)
-    dh=(own[...].astype(f32)+ro[...].astype(f32))+(a_in[...].astype(f32)+b_in[...].astype(f32))
+    b_in=refs[0][...].astype(f32) if len(refs)==8 else jnp.where(i<2,refs[0][...].astype(f32),refs[1][...].astype(f32))
+    dh=(own[...].astype(f32)+ro[...].astype(f32))+(a_in[...].astype(f32)+b_in)
     r=rows[...].astype(f32)
     cen=r-jnp.mean(r,axis=-1,keepdims=True)
     rstd=lax.rsqrt(jnp.mean(cen*cen,axis=-1,keepdims=True)+LN_EPS)
@@ -157,46 +181,45 @@
     out[...]=o
     @pl.when(i==0)
     def _(): vec[...]=jnp.zeros_like(vec)
-    vec[0]+=fold8(dh*hat); vec[1]+=fold8(dh); vec[2]+=fold8(o.astype(f32)); vec[3]+=fold8(sk)
-
-def ln_bwd(parts, rows, skip, gain):
+    vec[0]+=fold8(dh*hat); vec[1]+=fold8(dh)
+    if total.shape[0]==4: vec[2]+=fold8(o.astype(f32)); vec[3]+=fold8(sk)
+    @pl.when(i==3)
+    def _():
+        for k in range(2 if total.shape[0]==6 else 4): total[k:k+1,:]=jnp.sum(vec[k],axis=0,keepdims=True)
+        if total.shape[0]==6: total[2:6,:]=more[...]
+
+def ln_bwd(parts, rows, skip, gain, more):
     R=64
     blk=pl.BlockSpec((R,D),lambda i:(i,0))
+    n=6 if more.shape[0]==4 else 4
+    b_specs=[blk] if len(parts)==4 else [pl.BlockSpec((R,D),lambda i:(jnp.minimum(i,1),0)),pl.BlockSpec((R,D),lambda i:(jnp.maximum(i-2,0),0))]
     out,vec=pl.pallas_call(ln_bwd_kernel,grid=(256//R,),
-        in_specs=[blk]*6+[pl.BlockSpec((1,D),lambda i:(0,0))],
-        out_specs=[blk,pl.BlockSpec((4,8,D),lambda i:(0,0,0))],
-        out_shape=[jax.ShapeDtypeStruct((256,D),bf16),jax.ShapeDtypeStruct((4,8,D),f32)],
-        compiler_params=pltpu.CompilerParams(dimension_semantics=("arbitrary",)),
-        cost_estimate=pl.CostEstimate(flops=256*D*1000,bytes_accessed=6<<20,transcendentals=0))(*parts,rows,skip,gain.reshape(1,D))
-    return out,jnp.sum(vec,axis=1)
+        in_specs=[blk]*3+b_specs+[blk]*2+[pl.BlockSpec((1,D),lambda i:(0,0)),pl.BlockSpec(more.shape,lambda i:(0,0))],
+        out_specs=[blk,pl.BlockSpec((n,D),lambda i:(0,0))],scratch_shapes=[pltpu.VMEM((4,8,D),f32)],
+        out_shape=[jax.ShapeDtypeStruct((256,D),bf16),jax.ShapeDtypeStruct((n,D),f32)],
+        compiler_params=pltpu.CompilerParams(dimension_semantics=("arbitrary",),vmem_limit_bytes=16<<20),
+        cost_estimate=pl.CostEstimate(flops=256*D*1000,bytes_accessed=6<<20,transcendentals=0))(*parts,rows,skip,gain.reshape(1,D),more)
+    return out,vec
+
+def join(a, b):
+    def kernel(a, b, out):
+        out[0]=a[0]; out[1]=b[0]
+    return pl.pallas_call(kernel,name="lse_join",out_shape=jax.ShapeDtypeStruct((2,1,T),f32),compiler_params=pltpu.CompilerParams(vmem_limit_bytes=4<<20),
+        cost_estimate=pl.CostEstimate(flops=T*100,bytes_accessed=8*T,transcendentals=0))(a,b)
 
 def call(kernel, grid, in_specs, out_specs, out_shape, scratch, flops, args):
     return pl.pallas_call(kernel,grid=grid,in_specs=in_specs,out_specs=out_specs,out_shape=out_shape,
         scratch_shapes=scratch,compiler_params=pltpu.CompilerParams(dimension_semantics=("arbitrary",)*len(grid),vmem_limit_bytes=40<<20),
         cost_estimate=pl.CostEstimate(flops=flops,bytes_accessed=30<<20,transcendentals=0))(*args)
 
-def gelu_kernel(blk_ref, z, u, slope):
-    zf=z[...].astype(f32)
-    th=jnp.tanh(GELU_SCALE*(zf+GELU_COEF*zf*zf*zf))
-    u[...]=(0.5*zf*(1.0+th)).astype(bf16)
-    slope[...]=0.5*(1.0+th)+0.5*zf*(1.0-th*th)*GELU_SCALE*(1.0+3.0*GELU_COEF*zf*zf)
-
-def gelu(blk, z):
-    out=pl.BlockSpec((BLK,F),lambda p,blk:(p,0))
-    return pl.pallas_call(gelu_kernel,name="gelu",
-        grid_spec=pltpu.PrefetchScalarGridSpec(num_scalar_prefetch=1,grid=(8,),
-            in_specs=[pl.BlockSpec((BLK,F),lambda p,blk:(blk[p],0))],out_specs=[out,out]),
-        out_shape=[jax.ShapeDtypeStruct((T,F),bf16),jax.ShapeDtypeStruct((T,F),f32)],
-        compiler_params=pltpu.CompilerParams(dimension_semantics=("arbitrary",)),
-        cost_estimate=pl.CostEstimate(flops=T*F*1000,bytes_accessed=20<<20,transcendentals=T*F))(blk,z)
-
-def mlp(first, pieces, slope, w2, w1, prev):
+RB=256; SUB=BLK//RB
+def mlp(first, blk, pieces, z, w2, w1, prev):
     n=len(pieces)//2
     def kernel(*refs):
-        dy=refs[:2*n]; sl,w2h,w1h=refs[2*n:2*n+3]
-        refs=refs[2*n+(3 if prev is None else 4):]
-        dz_ref,db_ref=refs[:2]; dh=refs[2:2+2*n]
-        x,w2s,w1s,st,xsem,wsem,osem=refs[2+2*n:]
+        dy=refs[1:1+2*n]; z_ref,w2h,w1h=refs[1+2*n:4+2*n]
+        refs=refs[2*n+(4 if prev is None else 6):]
+        dz_ref,u_ref,db_ref=refs[:3]; dh=refs[3:3+2*n]
+        x,w2s,w1s,st,xsem,wsem,osem=refs[3+2*n:]
         s=pl.program_id(0)
         class wcopy:
             def __init__(self, k):
@@ -218,37 +241,47 @@
             db_ref[...]=jnp.zeros_like(db_ref)
             wcopy(0).wait()
         for k in range(2*n):
-            @pl.when(s==k)
+            @pl.when(s==k*SUB)
             def _(): xcopy(k).wait()
-        rows=pl.ds(pl.multiple_of(s*BLK,BLK),BLK)
-        dz=(tn(x[rows,:],w2s[...],1,1)*sl[...]).astype(bf16)
+        rows=pl.ds(pl.multiple_of(s*RB,RB),RB)
+        zf=z_ref[...].astype(f32)
+        t=zf*zf
+        th=jnp.tanh(zf*(GELU_SCALE*GELU_COEF*t+GELU_SCALE))
+        hz=0.5*zf
+        u_ref[...]=(hz*th+hz).astype(bf16)
+        slope=(0.5*th+0.5)+hz*(1.0-th*th)*(3.0*GELU_SCALE*GELU_COEF*t+GELU_SCALE)
+        dz=(tn(x[rows,:],w2s[...],1,1)*slope).astype(bf16)
         dz_ref[...]=dz
         db_ref[...]+=fold8(dz.astype(f32))
         @pl.when(s==0)
         def _(): wcopy(1).wait()
-        def part(c,_):
-            at=pl.ds(pl.multiple_of(c*768,768),768)
-            st[rows,at]=tn(dz_ref[...],w1s[at,:],1,1).astype(bf16)
-            return 0
-        lax.fori_loop(0,3,part,0)
+        if first>0: st[rows,:]=tn(dz_ref[...],w1s[...],1,1).astype(bf16)
+        else:
+            def part(c,_):
+                at=pl.ds(pl.multiple_of(c*768,768),768)
+                st[rows,at]=tn(dz_ref[...],w1s[at,:],1,1).astype(bf16)
+                return 0
+            lax.fori_loop(0,3,part,0)
         for k in range(2*n):
-            @pl.when(s==k)
+            @pl.when(s==k*SUB+SUB-1)
             def _(): ocopy(k).start()
-        @pl.when(s==2*n-1)
+        @pl.when(s==2*n*SUB-1)
         def _():
             for p in range(2*n): ocopy(p).wait()
     any_=pl.BlockSpec(memory_space=ANY)
-    step=pl.BlockSpec((BLK,F),lambda s:(s+2*first,0))
-    outs=pl.pallas_call(kernel,grid=(2*n,),
-        in_specs=[any_]*(2*n)+[step]+[any_]*(2 if prev is None else 3),
-        out_specs=[step,pl.BlockSpec((8,F),lambda s:(0,0))]+[any_]*(2*n),
-        out_shape=[jax.ShapeDtypeStruct((T,F),bf16),jax.ShapeDtypeStruct((8,F),f32)]+[jax.ShapeDtypeStruct((BLK,D),bf16)]*(2*n),
-        scratch_shapes=[pltpu.VMEM((2*n*BLK,D),bf16),pltpu.VMEM((F,D),bf16),pltpu.VMEM((D,F),bf16),pltpu.VMEM((2*n*BLK,D),bf16),
-         pltpu.SemaphoreType.DMA((2*n,)),pltpu.SemaphoreType.DMA((2,4)),pltpu.SemaphoreType.DMA((2*n,))],
-        input_output_aliases={} if prev is None else {2*n+3:0},
+    step=pl.BlockSpec((RB,F),lambda s,blk:(s+2*first*SUB,0))
+    extra=() if prev is None else prev
+    outs=pl.pallas_call(kernel,
+        grid_spec=pltpu.PrefetchScalarGridSpec(num_scalar_prefetch=1,grid=(2*n*SUB,),
+            in_specs=[any_]*(2*n)+[pl.BlockSpec((RB,F),lambda s,blk:(blk[s//SUB+2*first]*SUB+s%SUB,0))]+[any_]*(2+len(extra)),
+            out_specs=[step,step,pl.BlockSpec((8,F),lambda s,blk:(0,0))]+[any_]*(2*n),
+            scratch_shapes=[pltpu.VMEM((2*n*BLK,D),bf16),pltpu.VMEM((F,D),bf16),pltpu.VMEM((D,F),bf16),pltpu.VMEM((2*n*BLK,D),bf16),
+             pltpu.SemaphoreType.DMA((2*n,)),pltpu.SemaphoreType.DMA((2,4)),pltpu.SemaphoreType.DMA((2*n,))]),
+        out_shape=[jax.ShapeDtypeStruct((T,F),bf16)]*2+[jax.ShapeDtypeStruct((8,F),f32)]+[jax.ShapeDtypeStruct((BLK,D),bf16)]*(2*n),
+        input_output_aliases={2*n+4+k:k for k in range(len(extra))},
         compiler_params=pltpu.CompilerParams(dimension_semantics=("arbitrary",),vmem_limit_bytes=48<<20),
-        cost_estimate=pl.CostEstimate(flops=n*T*D*F,bytes_accessed=20<<20,transcendentals=0))(*pieces,slope,w2,w1,*(() if prev is None else (prev,)))
-    return outs[0],outs[1],list(outs[2:])
+        cost_estimate=pl.CostEstimate(flops=n*T*D*F,bytes_accessed=20<<20,transcendentals=0))(blk,*pieces,z,w2,w1,*extra)
+    return (outs[0],outs[1]),outs[2],list(outs[3:])
 
 def attn_in_grad(chips, dqkv, wqkv):
     c0,c1=chips
@@ -257,11 +290,7 @@
         s=pl.program_id(0)
         def ocopy(p): return pltpu.make_async_copy(st.at[p*BLK:(p+1)*BLK],dh[p],sem.at[p])
         rows=pl.ds(pl.multiple_of(s*BLK,BLK),BLK)
-        def part(c,_):
-            at=pl.ds(pl.multiple_of(c*768,768),768)
-            st[rows,at]=tn(g[...],w[:,at],0,0).astype(bf16)
-            return 0
-        lax.fori_loop(0,3,part,0)
+        st[rows,:]=tn(g[...],w[...],0,0).astype(bf16)
         for k in range(4):
             @pl.when(s==k)
             def _(): ocopy(k).start()
@@ -329,40 +358,49 @@
         wqkv=w_qkv.transpose(0,2,3,1).reshape(3*NH*E,D)
         wo=w_proj.reshape(NH*E,D)
         dya,dyb,dyp=hop_a(d_out),hop_b(d_out),partner(d_out)
-        u,slope=gelu(blk,z)
-        dz,db_0,(o0,o1)=mlp(0,[d_out,dyp],slope,w_fc2,w_fc1,None)
-        dya=after(dya,db_0)
+        dzu,db_0,(o0,o1)=mlp(0,blk,[d_out,dyp],z,w_fc2,w_fc1,None)
+        h2_local=layer_norm_fwd(after(x_mid,db_0),g2,b2)
+        ctx,lse0=attn_fwd(0,1,me1,after(q,db_0),k,v,None)
+        dya=after(dya,lse0,h2_local)
         dyd=hop_b(dya)
-        h2_local=layer_norm_fwd(after(x_mid,dya),g2,b2)
+        h2_local=after(h2_local,dya)
         h2a,h2b,h2p=hop_a(h2_local),hop_b(h2_local),partner(h2_local)
         dypa,dypb=partner(dya),partner(dyb)
-        dz,db_1,(pa0,pa1,pb0,pb1)=mlp(1,[dya,dypb,dyb,dypa],slope,w_fc2,w_fc1,dz)
+        dzu,db_1,(pa0,pa1,pb0,pb1)=mlp(1,blk,[dya,dypb,dyb,dypa],z,w_fc2,w_fc1,dzu)
         ra,rb,ro=partner(pb1),partner(pa1),partner(o1)
         a_in=hop_a(add2(pa0,ra))
         dypd=partner(dyd)
-        dz,db_2,(pd0,pd1)=mlp(3,[dyd,dypd],slope,w_fc2,w_fc1,dz)
-        d_sum=add2(pd0,partner(pd1))
-        d_in=hop_a(d_sum)
-        ctx,lse01=attn_fwd(0,2,me1,after(q,d_sum),k,v,None)
-        b_sum=(pb0.astype(f32)+after(rb,lse01).astype(f32)+d_in.astype(f32)).astype(bf16)
-        b_in=hop_b(b_sum)
+        (dz,u),db_2,(pd0,pd1)=mlp(3,blk,[dyd,dypd],z,w_fc2,w_fc1,dzu)
+        rd=partner(pd1)
+        d_sum=[add2(pd0[:128],rd[:128]),add2(pd0[128:],rd[128:])]
+        d_in=[hop_a(d_sum[0]),hop_a(d_sum[1])]
+        def b_half(k,lse): return (pb0[128*k:128*k+128].astype(f32)+after(rb,lse)[128*k:128*k+128].astype(f32)+d_in[k].astype(f32)).astype(bf16)
+        ctx,lse1=attn_fwd(1,1,me1,after(q,*d_sum),k,v,ctx)
+        b_sum=b_half(0,lse1)
+        b_in0=hop_b(b_sum)
+        b_sum=b_half(1,b_sum)
+        b_in1=hop_b(b_sum)
+        ctx,lse2=attn_fwd(2,1,me1,after(q,b_sum),k,v,ctx)
+        lse01=join(lse0,lse1)
         h2a=after(h2a,b_sum)
         h2d=hop_b(h2a); h2pa,h2pb=partner(h2a),partner(h2b)
-        ctx,lse2=attn_fwd(2,1,me1,after(q,b_sum),k,v,ctx)
-        mid,vec2=ln_bwd((after(o0,lse2),ro,a_in,b_in),x_mid,d_out,g2)
+        mid,vec2=ln_bwd((after(o0,lse2),ro,a_in,b_in0,b_in1),x_mid,d_out,g2,g2.reshape(1,D))
         grad_bfc1=jnp.sum(db_0+db_1+db_2,axis=0)
         dxa,dxb,dxp=hop_a(mid),hop_b(mid),partner(mid)
         dys=[d_out,dyp,dya,dypb,dyb,dypa,dyd,dypd]
         grad_wfc2=gathered_mm(lambda x,o: tn(o[...],x,0,0),dys,after(u,mid),9,
             pl.BlockSpec((F,256),lambda s:(0,s)),jax.ShapeDtypeStruct((F,D),f32),2*T*D*F)
-        h1_local=layer_norm_fwd(after(x_in,mid),g1,b1)
-        dxa=after(dxa,grad_wfc2,h1_local)
+        h2pd=partner(after(h2d,grad_wfc2))
+        h2=[h2_local,h2p,h2a,h2pb,h2b,h2pa,h2d,h2pd]
+        h1_local=layer_norm_fwd(after(x_in,grad_wfc2),g1,b1)
+        def w1_part(c0,n,left,into):
+            return gathered_mm(lambda x,o: tn(x,o[...],0,0),h2,left,n,
+                pl.BlockSpec((256,F),lambda s:(s+c0,0)),jax.ShapeDtypeStruct((D,F),f32),2*T*256*n*F,cols=(256*c0,256*(c0+n)),into=into)
+        grad_wfc1=w1_part(0,3,after(dz,h1_local),None)
+        dxa=after(dxa,grad_wfc1)
         dxd=hop_b(dxa)
         dxpa,dxpb=partner(dxa),partner(dxb)
-        h2pd=partner(after(h2d,grad_wfc2))
-        h2=[h2_local,h2p,h2a,h2pb,h2b,h2pa,h2d,h2pd]
-        grad_wfc1=gathered_mm(lambda x,o: tn(x,o[...],0,0),h2,after(dz,dxa),3,
-            pl.BlockSpec((768,F),lambda s:(s,0)),jax.ShapeDtypeStruct((D,F),f32),2*T*D*F)
+        grad_wfc1=w1_part(3,6,after(dz,dxa),grad_wfc1)
         dctx=ctx_grad(0,[mid,dxp,dxa,dxpb,dxb,dxpa],after(wo,grad_wfc1),None)
         dxd=after(dxd,dctx)
         dxpd=partner(dxd)
@@ -389,15 +427,18 @@
         h1=[h1_local,h1p,h1a,h1pb,h1b,h1pa,h1d,h1pd]
         grad_wqkv=gathered_mm(lambda x,o: jnp.dot(o[...],x,preferred_element_type=f32),h1,after(dqkv,b_sum),3,
             pl.BlockSpec((3*NH*E,768),lambda s:(0,s)),jax.ShapeDtypeStruct((3*NH*E,D),f32),6*T*D*NH*E)
-        dx,vec1=ln_bwd((after(o0,grad_wqkv),ro,a_in,b_in),x_in,mid,g1)
-        grad_vecs=jnp.concatenate([vec1[:2],vec2],axis=0)
-        def all_sum(vecs,k): return vecs+send(vecs,[(i,i^k) for i in range(8)])
-        vecs=all_sum(grad_vecs,1)
-        grad_wproj=gathered_mm(lambda x,o: jnp.dot(o[...],x,preferred_element_type=f32),dx1,after(ctx,dx).reshape(NH*E,T),3,
-            pl.BlockSpec((NH*E,768),lambda s:(0,s)),jax.ShapeDtypeStruct((NH*E,D),f32),2*T*D*NH*E)
-        vecs=all_sum(after(vecs,grad_wproj),2)
-        grad_bqkv=jnp.sum(after(dqkv,grad_wproj),axis=1,dtype=f32).reshape(3,NH,E)
-        grad_vecs=all_sum(vecs,4)
+        def wo_part(c0,n,left,into):
+            return gathered_mm(lambda x,o: jnp.dot(o[...],x,preferred_element_type=f32),dx1,left,n,
+                pl.BlockSpec((NH*E,256),lambda s:(0,s+c0)),jax.ShapeDtypeStruct((NH*E,D),f32),n*T*256*NH*E*2,cols=(256*c0,256*(c0+n)),into=into)
+        ctx=ctx.reshape(NH*E,T)
+        grad_wproj=wo_part(0,3,after(ctx,grad_wqkv),None)
+        dx,grad_vecs=ln_bwd((after(o0,grad_wproj),ro,a_in,b_in),x_in,mid,g1,vec2)
+        v2,v4,v6=(send(grad_vecs,[(i,i^k) for i in range(8)]) for k in (2,4,6))
+        grad_wproj=wo_part(3,6,after(ctx,dx),grad_wproj)
+        vecs=(grad_vecs+after(v2,grad_wproj))+(v4+v6)
+        v1=send(vecs,[(i,i^1) for i in range(8)])
+        grad_bqkv=jnp.sum(after(dqkv,vecs),axis=1,dtype=f32).reshape(3,NH,E)
+        grad_vecs=vecs+v1
         grad_wproj=grad_wproj.reshape(NH,E,D)
         grad_wqkv=grad_wqkv.reshape(3,NH,E,D).transpose(0,3,1,2)
         return dx[None], grad_wqkv, grad_bqkv, grad_wproj, grad_wfc1, grad_bfc1, grad_wfc2, grad_vecs

time: 368 us -> 360 us (0.978)
  Pallas kernels: 216 us -> 209 us
  other arithmetic: 12.3 us -> 5.87 us
  local copies, waits for them, and re-layouts: 8.73 us -> 14.2 us
    pallas_call x6 -> x8, Pallas kernels: 74.2 us -> 63.3 us  [the longest x3 51.8 us: mlp(): pl.pallas_call(kernel, grid_spec=pltpu.PrefetchScalarGridSpec(num_scalar_...]
    pallas_call x4 -> x6, Pallas kernels: 60.3 us -> 70.7 us  [gathered_mm(): pl.pallas_call(kernel, grid=(n,), in_specs=[any_] * 8 + [pl.BlockSpec(oth...]
    unnamed x94 -> x92, local copies, waits for them, and re-layouts: 6.86 us -> 12.1 us
    reduce_sum x7 -> x1, other arithmetic: 4.62 us -> 0.54 us  [layer(): grad_bqkv = jnp.sum(after(dqkv, vecs), axis=1, dtype=f32).reshape(3, NH, E)]
    pallas_call x4 -> x5, Pallas kernels: 55.3 us -> 52.5 us  [attn_call(): pl.pallas_call(kernel, grid_spec=pltpu.PrefetchScalarGridSpec(num_scalar_...]
    ppermute x45 -> x48, waiting for transfers between devices: 102 us -> 101 us  [send(): return lax.ppermute(a, 'tp', pairs)]
    ppermute x45 -> x48, starting transfers between devices: 27.6 us -> 27.8 us  [send(): return lax.ppermute(a, 'tp', pairs)]
  transfers between devices with their start and end apart: 45 -> 48, of which waited for: 14 -> 14; matrix products, arithmetic and copies ran while one was open for 3% -> 2% of each run, Pallas kernels for 48% -> 48%
where the time goes in v1:
time: 360 us; the launch traced here: 359 us
  Pallas kernels  209 us (58%)
  waiting for transfers between devices  101 us (28%)
  starting transfers between devices  27.8 us (8%)
  local copies, waits for them, and re-layouts  14.2 us (4%)
  other arithmetic  5.87 us (2%)
    ppermute x48, waiting for transfers between devices, send(): return lax.ppermute(a, 'tp', pairs)  101 us
    pallas_call x6, Pallas kernels, gathered_mm(): pl.pallas_call(kernel, grid=(n,), in_specs=[any_] * 8 + [pl.BlockSpec(oth...  70.7 us
    pallas_call x5, Pallas kernels, attn_call(): pl.pallas_call(kernel, grid_spec=pltpu.PrefetchScalarGridSpec(num_scalar_...  52.5 us
    pallas_call x3, Pallas kernels, mlp(): pl.pallas_call(kernel, grid_spec=pltpu.PrefetchScalarGridSpec(num_scalar_...  51.8 us
    ppermute x48, starting transfers between devices, send(): return lax.ppermute(a, 'tp', pairs)  27.8 us
    pallas_call x2, Pallas kernels, call(): pl.pallas_call(kernel, grid=grid, in_specs=in_specs, out_specs=out_specs,...  15.1 us
    unnamed x92, local copies, waits for them, and re-layouts  12.1 us
    pallas_call x2, Pallas kernels, ln_bwd(): pl.pallas_call(ln_bwd_kernel, grid=(256 // R,), in_specs=[blk] * 3 + b_sp...  8.99 us
  transfers between devices with their start and end apart: 48, of which 14 were waited for; matrix products, arithmetic and copies ran while one was open for 2% of the time, Pallas kernels for 48%

profile of v1, /device:TPU:0, one launch (start us, length us, event | category | flops | bytes accessed | tf_op | source)
XLA Modules:
  0.0 358.9 jit_solution(15241353535872885843)
XLA Ops:
  0.6 0.8 collective-permute-start
  1.4 2.5 collective-permute-start.1
  3.9 1.5 collective-permute-start.2
  5.4 0.7 reshape.59.gain.refs_4_.refs_5_
  6.1 0.7 reshape.60.bias
  6.9 1.7 copy-done.17
  8.6 14.5 %shard_map.206 = (bf16[2048,1152]{1,0:T(8,128)(2,1)}, bf16[2048,1152]{1,0:T(8,128)(2,1)}, f32[8,1152]{1,0:T(8,128)S(1)}, bf16[256,2304]{1,0:T(8,128)(2,1)S(1)}, bf16[256,2304]{1,0:T(8,128)(2,1)S(1)}) custom-call(s32[8]{0:T(128)S(1)} %fusion.1.refs_0_, bf16[256,2304]{1,0:T(8,128)(2,1)S(1)} %bitcast.44, ...), custom_call_target="tpu_custom_call" | custom-call | flops 5435817984 | bytes 20971520 | tf_op jit(solution)/shard_map/pallas_call | solution.py:274
  23.1 1.0 copy-done.31
  24.1 1.3 shard_map.208.refs_0_
  25.8 6.9 %shard_map.207 = (bf16[3,96,2048]{2,1,0:T(8,128)(2,1)S(1)}, f32[1,1,2048]{2,1,0:T(1,128)S(1)}) custom-call(s32[1]{0:T(128)} %bitcast.me_ref._, bf16[3,96,2048]{2,1,0:T(8,128)(2,1)S(1)} %bitcast.48, bf16[3,96,2048]{2,1,0:T(8,128)(2,1)S(1)} %bitcast.53, bf16[3,96,2048]{2,1,0:T(8,128)(2,1)S(1)} %bitcast.58, s32[1]{0:T(128)} %bitcast.me_ref._), custom_call_target="tpu_custom_call" | custom-call | flops 2684354560 | bytes 3145728 | tf_op jit(solution)/shard_map/pallas_call | solution.py:117
  33.8 15.4 %collective-permute-done.6.refs_1_.refs_6_ = bf16[256,2304]{1,0:T(8,128)(2,1)S(1)} collective-permute-done((bf16[256,2304]{1,0:T(8,128)(2,1)}, bf16[256,2304]{1,0:T(8,128)(2,1)S(1)}, u32[]{:S(2)}, u32[]{:S(2)}) %collective-permute-start.6) | collective-permute-done | bytes 1179680 | tf_op jit(solution)/shard_map/ppermute | solution.py:146
  49.2 1.4 copy-done.39
  50.6 22.7 %shard_map.209 = (bf16[2048,1152]{1,0:T(8,128)(2,1)}, bf16[2048,1152]{1,0:T(8,128)(2,1)}, f32[8,1152]{1,0:T(8,128)S(1)}, bf16[256,2304]{1,0:T(8,128)(2,1)S(1)}, ...) custom-call(s32[8]{0:T(128)S(1)} %fusion.1.refs_0_, ...), custom_call_target="tpu_custom_call", output_to_operand_aliasing={{0}: (8, {}), {1}: (9, {})} | custom-call | flops 10871635968 | bytes 20971520 | tf_op jit(solution)/shard_map/pallas_call | solution.py:274
  73.3 1.0 copy-done.33
  74.3 1.0 copy-done.35
  75.3 14.6 %shard_map.210 = (bf16[2048,1152]{1,0:T(8,128)(2,1)}, bf16[2048,1152]{1,0:T(8,128)(2,1)}, f32[8,1152]{1,0:T(8,128)S(1)}, bf16[256,2304]{1,0:T(8,128)(2,1)S(1)}, bf16[256,2304]{1,0:T(8,128)(2,1)}) custom-call(s32[8]{0:T(128)S(1)} %fusion.1.refs_0_, ...), custom_call_target="tpu_custom_call", output_to_operand_aliasing={{0}: (6, {}), {1}: (7, {})} | custom-call | flops 5435817984 | bytes 20971520 | tf_op jit(solution)/shard_map/pallas_call | solution.py:274
  91.0 1.1 collective-permute-start.18
  92.1 1.0 collective-permute-done.8
  93.8 1.0 collective-permute-done.12
  95.6 1.0 copy-done.25
  97.0 6.9 %shard_map.211 = (bf16[3,96,2048]{2,1,0:T(8,128)(2,1)S(1)}, f32[1,1,2048]{2,1,0:T(1,128)S(1)}) custom-call(s32[1]{0:T(128)} %bitcast.me_ref._, bf16[3,96,2048]{2,1,0:T(8,128)(2,1)S(1)} %bitcast.49, bf16[3,96,2048]{2,1,0:T(8,128)(2,1)S(1)} %bitcast.54, bf16[3,96,2048]{2,1,0:T(8,128)(2,1)S(1)} %bitcast.59, ...), custom_call_target="tpu_custom_call", output_to_operand_aliasing={{0}: (4, {})} | custom-call | flops 2684354560 | bytes 3145728 | tf_op jit(solution)/shard_map/pallas_call | solution.py:117
  103.9 1.5 collective-permute-start.13
  105.5 19.7 %collective-permute-done.9 = bf16[128,2304]{1,0:T(8,128)(2,1)S(1)} collective-permute-done((bf16[128,2304]{1,0:T(8,128)(2,1)S(1)}, bf16[128,2304]{1,0:T(8,128)(2,1)S(1)}, u32[]{:S(2)}, u32[]{:S(2)}) %collective-permute-start.9) | collective-permute-done | bytes 589856 | tf_op jit(solution)/shard_map/ppermute | solution.py:146
  125.9 18.2 %collective-permute-done.10 = bf16[128,2304]{1,0:T(8,128)(2,1)S(1)} collective-permute-done((bf16[128,2304]{1,0:T(8,128)(2,1)S(1)}, bf16[128,2304]{1,0:T(8,128)(2,1)S(1)}, u32[]{:S(2)}, u32[]{:S(2)}) %collective-permute-start.10) | collective-permute-done | bytes 589856 | tf_op jit(solution)/shard_map/ppermute | solution.py:146
  144.9 1.6 collective-permute-start.15
  146.9 7.0 %shard_map.212 = (bf16[3,96,2048]{2,1,0:T(8,128)(2,1)S(1)}, f32[1,1,2048]{2,1,0:T(1,128)S(1)}) custom-call(s32[1]{0:T(128)} %bitcast.me_ref._, bf16[3,96,2048]{2,1,0:T(8,128)(2,1)S(1)} %bitcast.50, bf16[3,96,2048]{2,1,0:T(8,128)(2,1)S(1)} %bitcast.55, bf16[3,96,2048]{2,1,0:T(8,128)(2,1)S(1)} %bitcast.60, ...), custom_call_target="tpu_custom_call", output_to_operand_aliasing={{0}: (4, {})} | custom-call | flops 2684354560 | bytes 3145728 | tf_op jit(solution)/shard_map/pallas_call | solution.py:117
  154.6 5.8 %collective-permute-done.15.refs_1_ = bf16[128,2304]{1,0:T(8,128)(2,1)S(1)} collective-permute-done((bf16[128,2304]{1,0:T(8,128)(2,1)S(1)}, bf16[128,2304]{1,0:T(8,128)(2,1)S(1)}, u32[]{:S(2)}, u32[]{:S(2)}) %collective-permute-start.15) | collective-permute-done | bytes 589856 | tf_op jit(solution)/shard_map/ppermute | solution.py:146
  160.3 3.7 %shard_map.213 = (bf16[256,2304]{1,0:T(8,128)(2,1)S(1)}, f32[4,2304]{1,0:T(4,128)S(1)}) custom-call(bf16[256,2304]{1,0:T(8,128)(2,1)S(1)} %get-tuple-element.94.own, bf16[256,2304]{1,0:T(8,128)(2,1)S(1)} %collective-permute-done.11.ro, bf16[256,2304]{1,0:T(8,128)(2,1)S(1)} %collective-permute-done.13.a_in, ...), custom_call_target="tpu_custom_call" | custom-call | flops 589824000 | bytes 6291456 | tf_op jit(solution)/shard_map/pallas_call | solution.py:196
  164.6 19.0 %shard_map.214 = f32[1152,2304]{1,0:T(8,128)} custom-call(bf16[256,2304]{1,0:T(8,128)(2,1)} %bitcast.43, bf16[256,2304]{1,0:T(8,128)(2,1)} %copy-done.30, bf16[256,2304]{1,0:T(8,128)(2,1)} %collective-permute-done.1.refs_1_.refs_2_, bf16[256,2304]{1,0:T(8,128)(2,1)} %copy-done.38, bf16[256,2304]{1,0:T(8,128)(2,1)} %collective-permute-done.2.refs_3_.refs_4_, ...), custom_call_target="tpu_custom_call" | custom-call | flops 10871635968 | bytes 31457280 | tf_op jit(solution)/shard_map/pallas_call | solution.py:322
  183.7 1.1 collective-permute-start.16
  184.9 1.3 copy-done.8
  186.2 1.3 shard_map.215.refs_0_
  187.4 1.0 copy-done.15
  189.1 10.0 %shard_map.216.refs_9_ = f32[2304,1152]{1,0:T(8,128)} custom-call(bf16[256,2304]{1,0:T(8,128)(2,1)} %copy-done.2, bf16[256,2304]{1,0:T(8,128)(2,1)} %collective-permute-done.17.refs_1_, bf16[256,2304]{1,0:T(8,128)(2,1)} %collective-permute-done.18.refs_2_, bf16[256,2304]{1,0:T(8,128)(2,1)} %collective-permute-done.20.refs_3_, ...), custom_call_target="tpu_custom_call" | custom-call | flops 3623878656 | bytes 31457280 | tf_op jit(solution)/shard_map/pallas_call | solution.py:322
  199.1 0.8 collective-permute-done.16.refs_2_
  199.9 1.5 collective-permute-start.24
  201.5 14.7 %shard_map.217 = f32[2304,1152]{1,0:T(8,128)} custom-call(bf16[256,2304]{1,0:T(8,128)(2,1)} %copy-done.2, bf16[256,2304]{1,0:T(8,128)(2,1)} %collective-permute-done.17.refs_1_, bf16[256,2304]{1,0:T(8,128)(2,1)} %collective-permute-done.18.refs_2_, bf16[256,2304]{1,0:T(8,128)(2,1)} %collective-permute-done.20.refs_3_, ...), custom_call_target="tpu_custom_call", output_to_operand_aliasing={{}: (9, {})} | custom-call | flops 7247757312 | bytes 31457280 | tf_op jit(solution)/shard_map/pallas_call | solution.py:322
  216.2 1.3 copy-done.6
  217.5 4.4 %shard_map.218.refs_3_ = bf16[288,2048]{1,0:T(8,128)(2,1)S(1)} custom-call(bf16[256,2304]{1,0:T(8,128)(2,1)S(1)} %get-tuple-element.98.refs_0_.refs_2_, bf16[256,2304]{1,0:T(8,128)(2,1)} %collective-permute-done.25.refs_1_, bf16[256,2304]{1,0:T(8,128)(2,1)S(1)} %collective-permute-done.16.refs_2_, bf16[256,2304]{1,0:T(8,128)(2,1)} %collective-permute-done.27.refs_3_, ...), custom_call_target="tpu_custom_call" | custom-call | flops 2038431744 | bytes 10485760 | tf_op jit(solution)/shard_map/pallas_call | solution.py:343
  222.0 0.7 collective-permute-start.32
  222.7 2.3 collective-permute-done.29.refs_1_.refs_7_
  225.0 2.6 shard_map.219
  227.7 21.2 %shard_map.220._ = bf16[3,3,96,2048]{3,2,1,0:T(8,128)(2,1)S(1)} custom-call(s32[1]{0:T(128)} %bitcast.me_ref._, bf16[3,96,2048]{2,1,0:T(8,128)(2,1)S(1)} %bitcast.51, bf16[3,96,2048]{2,1,0:T(8,128)(2,1)S(1)} %bitcast.56, bf16[3,96,2048]{2,1,0:T(8,128)(2,1)S(1)} %bitcast.61, bf16[3,96,2048]{2,1,0:T(8,128)(2,1)S(1)} %bitcast.28, ...), custom_call_target="tpu_custom_call" | custom-call | flops 10737418240 | bytes 6291456 | tf_op jit(solution)/shard_map/pallas_call | solution.py:117
  248.9 10.5 %shard_map.221 = bf16[3,3,96,2048]{3,2,1,0:T(8,128)(2,1)S(1)} custom-call(s32[1]{0:T(128)} %bitcast.me_ref._, bf16[3,96,2048]{2,1,0:T(8,128)(2,1)S(1)} %bitcast.52, bf16[3,96,2048]{2,1,0:T(8,128)(2,1)S(1)} %bitcast.57, bf16[3,96,2048]{2,1,0:T(8,128)(2,1)S(1)} %bitcast.62, bf16[3,96,2048]{2,1,0:T(8,128)(2,1)S(1)} %bitcast.29, ...), custom_call_target="tpu_custom_call", output_to_operand_aliasing={{}: (6, {})} | custom-call | flops 5368709120 | bytes 3145728 | tf_op jit(solution)/shard_map/pallas_call | solution.py:117
  259.4 7.2 %shard_map.222 = (bf16[256,2304]{1,0:T(8,128)(2,1)S(1)}, bf16[256,2304]{1,0:T(8,128)(2,1)S(1)}, bf16[256,2304]{1,0:T(8,128)(2,1)S(1)}, bf16[256,2304]{1,0:T(8,128)(2,1)S(1)}) custom-call(bf16[864,2048]{1,0:T(8,128)(2,1)S(1)} %bitcast.36, bf16[864,2304]{1,0:T(8,128)(2,1)S(1)} %bitcast.46), custom_call_target="tpu_custom_call" | custom-call | flops 4076863488 | bytes 31457280 | tf_op jit(solution)/shard_map/pallas_call | solution.py:211
  267.4 1.4 collective-permute-start.36
  268.8 0.7 collective-permute-done.30
  269.8 7.9 %shard_map.223 = (bf16[256,2304]{1,0:T(8,128)(2,1)S(1)}, bf16[256,2304]{1,0:T(8,128)(2,1)S(1)}, bf16[256,2304]{1,0:T(8,128)(2,1)S(1)}, bf16[256,2304]{1,0:T(8,128)(2,1)}) custom-call(bf16[864,2048]{1,0:T(8,128)(2,1)S(1)} %bitcast.37, bf16[864,2304]{1,0:T(8,128)(2,1)S(1)} %bitcast.47), custom_call_target="tpu_custom_call" | custom-call | flops 4076863488 | bytes 31457280 | tf_op jit(solution)/shard_map/pallas_call | solution.py:211
  277.9 0.7 collective-permute-start.40
  278.6 29.7 %collective-permute-done.36.refs_6_ = bf16[256,2304]{1,0:T(8,128)(2,1)S(1)} collective-permute-done((bf16[256,2304]{1,0:T(8,128)(2,1)S(1)}, bf16[256,2304]{1,0:T(8,128)(2,1)S(1)}, u32[]{:S(2)}, u32[]{:S(2)}) %collective-permute-start.36) | collective-permute-done | bytes 1179680 | tf_op jit(solution)/shard_map/ppermute | solution.py:146
  309.3 1.3 add_convert_fusion.1
  310.7 1.5 add_convert_fusion
  312.8 1.7 collective-permute-done.34.refs_3_
  314.5 0.7 collective-permute-start.42
  316.8 14.4 %shard_map.224 = f32[864,2304]{1,0:T(8,128)} custom-call(bf16[256,2304]{1,0:T(8,128)(2,1)} %copy-done.15, bf16[256,2304]{1,0:T(8,128)(2,1)} %copy-done.43, bf16[256,2304]{1,0:T(8,128)(2,1)} %copy-done.40, bf16[256,2304]{1,0:T(8,128)(2,1)} %copy-done.45, bf16[256,2304]{1,0:T(8,128)(2,1)} %copy-done.41, bf16[256,2304]{1,0:T(8,128)(2,1)} %copy-done.44, ...), custom_call_target="tpu_custom_call" | custom-call | flops 8153726976 | bytes 31457280 | tf_op jit(solution)/shard_map/pallas_call | solution.py:322
  331.2 5.3 %shard_map.225.refs_9_ = f32[288,2304]{1,0:T(8,128)} custom-call(bf16[256,2304]{1,0:T(8,128)(2,1)} %copy-done, bf16[256,2304]{1,0:T(8,128)(2,1)} %collective-permute-done.25.refs_1_, bf16[256,2304]{1,0:T(8,128)(2,1)} %copy-done.4, bf16[256,2304]{1,0:T(8,128)(2,1)} %collective-permute-done.27.refs_3_, bf16[256,2304]{1,0:T(8,128)(2,1)} %copy-done.3, ...), custom_call_target="tpu_custom_call" | custom-call | flops 905969664 | bytes 31457280 | tf_op jit(solution)/shard_map/pallas_call | solution.py:322
  336.6 3.3 collective-permute-done.43.refs_0_
  339.9 0.9 collective-permute-done.42.a_in
  340.8 5.3 %shard_map.226 = (bf16[256,2304]{1,0:T(8,128)(2,1)}, f32[6,2304]{1,0:T(8,128)S(1)}) custom-call(bf16[256,2304]{1,0:T(8,128)(2,1)S(1)} %copy-done.20, bf16[256,2304]{1,0:T(8,128)(2,1)} %collective-permute-done.41.ro, bf16[256,2304]{1,0:T(8,128)(2,1)} %collective-permute-done.42.a_in, bf16[256,2304]{1,0:T(8,128)(2,1)} %collective-permute-done.43.refs_0_, ...), custom_call_target="tpu_custom_call" | custom-call | flops 589824000 | bytes 6291456 | tf_op jit(solution)/shard_map/pallas_call | solution.py:196
  346.1 1.6 collective-permute-start.46
  348.3 1.3 collective-permute-start.44
  349.6 7.3 %shard_map.227 = f32[288,2304]{1,0:T(8,128)} custom-call(bf16[256,2304]{1,0:T(8,128)(2,1)} %copy-done, bf16[256,2304]{1,0:T(8,128)(2,1)} %collective-permute-done.25.refs_1_, bf16[256,2304]{1,0:T(8,128)(2,1)} %copy-done.4, bf16[256,2304]{1,0:T(8,128)(2,1)} %collective-permute-done.27.refs_3_, ...), custom_call_target="tpu_custom_call", output_to_operand_aliasing={{}: (9, {})} | custom-call | flops 1811939328 | bytes 31457280 | tf_op jit(solution)/shard_map/pallas_call | solution.py:322
  357.6 0.7 reshape.69
  358.3 0.6 add.94
  (164 shorter events, 14.1 us)
Async XLA Ops:
  0.6 6.2 %collective-permute-start = (bf16[256,2304]{1,0:T(8,128)(2,1)}, bf16[256,2304]{1,0:T(8,128)(2,1)S(1)}, u32[]{:S(2)}, u32[]{:S(2)}) collective-permute-start(bf16[256,2304]{1,0:T(8,128)(2,1)} %bitcast.40), channel_id=1, source_target_pairs={{0,1},{1,0},{2,3},{3,2},{4,5},{5,4},{6,7},{7,6},{8,9},{9,8},{10,11... | collective-permute-start | bytes 3538952 | tf_op jit(solution)/shard_map/ppermute | solution.py:146
  1.4 31.3 %collective-permute-start.1 = (bf16[256,2304]{1,0:T(8,128)(2,1)}, bf16[256,2304]{1,0:T(8,128)(2,1)}, u32[]{:S(2)}, u32[]{:S(2)}) collective-permute-start(bf16[256,2304]{1,0:T(8,128)(2,1)} %bitcast.41), channel_id=1, source_target_pairs={{0,2},{1,5},{2,0},{3,7},{4,6},{5,1},{6,4},{7,3},{8,10},{9,13},{10,... | collective-permute-start | bytes 3538952 | tf_op jit(solution)/shard_map/ppermute | solution.py:146
  3.9 29.3 %collective-permute-start.2 = (bf16[256,2304]{1,0:T(8,128)(2,1)}, bf16[256,2304]{1,0:T(8,128)(2,1)}, u32[]{:S(2)}, u32[]{:S(2)}) collective-permute-start(bf16[256,2304]{1,0:T(8,128)(2,1)} %bitcast.42), channel_id=1, source_target_pairs={{0,4},{1,3},{2,6},{3,1},{4,0},{5,7},{6,2},{7,5},{8,12},{9,11},{10,... | collective-permute-start | bytes 3538952 | tf_op jit(solution)/shard_map/ppermute | solution.py:146
  6.9 16.2 %copy-start.30 = (bf16[256,2304]{1,0:T(8,128)(2,1)}, bf16[256,2304]{1,0:T(8,128)(2,1)S(1)}, u32[]{:S(2)}) copy-start(bf16[256,2304]{1,0:T(8,128)(2,1)S(1)} %collective-permute-done.refs_2_.refs_1_) | copy-start | bytes 3538948
  8.6 15.5 %copy-start.7 = (bf16[1,256,2304]{2,1,0:T(8,128)(2,1)S(1)}, bf16[1,256,2304]{2,1,0:T(8,128)(2,1)}, u32[]{:S(2)}) copy-start(bf16[1,256,2304]{2,1,0:T(8,128)(2,1)} %param.16) | copy-start | bytes 3538948
  8.6 16.8 %copy-start.27 = (bf16[1,2048,3,96]{1,3,2,0:T(8,128)(2,1)S(1)}, bf16[1,2048,3,96]{1,3,2,0:T(8,128)(2,1)}, u32[]{:S(2)}) copy-start(bf16[1,2048,3,96]{1,3,2,0:T(8,128)(2,1)} %param.20) | copy-start | bytes 3538948
  25.4 128.5 %copy-start.2 = (bf16[256,2304]{1,0:T(8,128)(2,1)}, bf16[256,2304]{1,0:T(8,128)(2,1)S(1)}, u32[]{:S(2)}) copy-start(bf16[256,2304]{1,0:T(8,128)(2,1)S(1)} %shard_map.208.refs_0_) | copy-start | bytes 3538948
  32.7 16.4 %collective-permute-start.6 = (bf16[256,2304]{1,0:T(8,128)(2,1)}, bf16[256,2304]{1,0:T(8,128)(2,1)S(1)}, u32[]{:S(2)}, u32[]{:S(2)}) collective-permute-start(bf16[256,2304]{1,0:T(8,128)(2,1)} %collective-permute-done.1.refs_1_.refs_2_), channel_id=1, source_target_pairs={{0,4},{1,3},{2,6},{3,1},{4,0},{5,7},{6,2},{7,5},{8,12},{9,11},{10,... | collective-permute-start | bytes 3538952 | tf_op jit(solution)/shard_map/ppermute | solution.py:146
  33.3 15.9 %collective-permute-start.3 = (bf16[256,2304]{1,0:T(8,128)(2,1)}, bf16[256,2304]{1,0:T(8,128)(2,1)S(1)}, u32[]{:S(2)}, u32[]{:S(2)}) collective-permute-start(bf16[256,2304]{1,0:T(8,128)(2,1)} %collective-permute-done.2.refs_3_.refs_4_), channel_id=1, source_target_pairs={{0,1},{1,0},{2,3},{3,2},{4,5},{5,4},{6,7},{7,6},{8,9},{9,8},{10,11... | collective-permute-start | bytes 3538952 | tf_op jit(solution)/shard_map/ppermute | solution.py:146
  33.3 15.9 %collective-permute-start.4 = (bf16[256,2304]{1,0:T(8,128)(2,1)}, bf16[256,2304]{1,0:T(8,128)(2,1)S(1)}, u32[]{:S(2)}, u32[]{:S(2)}) collective-permute-start(bf16[256,2304]{1,0:T(8,128)(2,1)} %collective-permute-done.1.refs_1_.refs_2_), channel_id=1, source_target_pairs={{0,1},{1,0},{2,3},{3,2},{4,5},{5,4},{6,7},{7,6},{8,9},{9,8},{10,11... | collective-permute-start | bytes 3538952 | tf_op jit(solution)/shard_map/ppermute | solution.py:146
  49.2 26.2 %copy-start.13 = (bf16[256,2304]{1,0:T(8,128)(2,1)}, bf16[256,2304]{1,0:T(8,128)(2,1)S(1)}, u32[]{:S(2)}) copy-start(bf16[256,2304]{1,0:T(8,128)(2,1)S(1)} %collective-permute-done.6.refs_1_.refs_6_) | copy-start | bytes 3538948
  49.2 25.2 %collective-permute-start.7 = (bf16[256,2304]{1,0:T(8,128)(2,1)S(1)}, bf16[256,2304]{1,0:T(8,128)(2,1)S(1)}, u32[]{:S(2)}, u32[]{:S(2)}) collective-permute-start(bf16[256,2304]{1,0:T(8,128)(2,1)S(1)} %collective-permute-done.6.refs_1_.refs_6_), channel_id=1, source_target_pairs={{0,1},{1,0},{2,3},{3,2},{4,5},{5,4},{6,7},{7,6},{8,9},{9,8},{10,11... | collective-permute-start | bytes 3538952 | tf_op jit(solution)/shard_map/ppermute | solution.py:146
  74.3 15.6 %copy-start.14 = (bf16[256,2304]{1,0:T(8,128)(2,1)}, bf16[256,2304]{1,0:T(8,128)(2,1)S(1)}, u32[]{:S(2)}) copy-start(bf16[256,2304]{1,0:T(8,128)(2,1)S(1)} %collective-permute-done.7.refs_2_.refs_7_) | copy-start | bytes 3538948
  75.3 16.8 %copy-start.32 = (bf16[256,2304]{1,0:T(8,128)(2,1)S(1)}, bf16[256,2304]{1,0:T(8,128)(2,1)}, u32[]{:S(2)}) copy-start(bf16[256,2304]{1,0:T(8,128)(2,1)} %copy-done.31) | copy-start | bytes 3538948
  75.3 17.8 %copy-start.34 = (bf16[256,2304]{1,0:T(8,128)(2,1)S(1)}, bf16[256,2304]{1,0:T(8,128)(2,1)}, u32[]{:S(2)}) copy-start(bf16[256,2304]{1,0:T(8,128)(2,1)} %copy-done.33) | copy-start | bytes 3538948
  90.0 3.2 collective-permute-start.8
  90.5 4.4 %collective-permute-start.12 = (bf16[256,2304]{1,0:T(8,128)(2,1)}, bf16[256,2304]{1,0:T(8,128)(2,1)S(1)}, u32[]{:S(2)}, u32[]{:S(2)}) collective-permute-start(bf16[256,2304]{1,0:T(8,128)(2,1)} %copy-done.35), channel_id=1, source_target_pairs={{0,1},{1,0},{2,3},{3,2},{4,5},{5,4},{6,7},{7,6},{8,9},{9,8},{10,11... | collective-permute-start | bytes 3538952 | tf_op jit(solution)/shard_map/ppermute | solution.py:146
  90.5 55.9 %collective-permute-start.19 = (bf16[256,2304]{1,0:T(8,128)(2,1)S(1)}, bf16[256,2304]{1,0:T(8,128)(2,1)}, u32[]{:S(2)}, u32[]{:S(2)}) collective-permute-start(bf16[256,2304]{1,0:T(8,128)(2,1)S(1)} %shard_map.208.refs_0_), channel_id=1, source_target_pairs={{0,4},{1,3},{2,6},{3,1},{4,0},{5,7},{6,2},{7,5},{8,12},{9,11},{10,... | collective-permute-start | bytes 3538952 | tf_op jit(solution)/shard_map/ppermute | solution.py:146
  91.0 53.9 %collective-permute-start.18 = (bf16[256,2304]{1,0:T(8,128)(2,1)S(1)}, bf16[256,2304]{1,0:T(8,128)(2,1)}, u32[]{:S(2)}, u32[]{:S(2)}) collective-permute-start(bf16[256,2304]{1,0:T(8,128)(2,1)S(1)} %shard_map.208.refs_0_), channel_id=1, source_target_pairs={{0,2},{1,5},{2,0},{3,7},{4,6},{5,1},{6,4},{7,3},{8,10},{9,13},{10,... | collective-permute-start | bytes 3538952 | tf_op jit(solution)/shard_map/ppermute | solution.py:146
  92.1 61.8 %collective-permute-start.11 = (bf16[256,2304]{1,0:T(8,128)(2,1)S(1)}, bf16[256,2304]{1,0:T(8,128)(2,1)S(1)}, u32[]{:S(2)}, u32[]{:S(2)}) collective-permute-start(bf16[256,2304]{1,0:T(8,128)(2,1)S(1)} %copy-done.32), channel_id=1, source_target_pairs={{0,1},{1,0},{2,3},{3,2},{4,5},{5,4},{6,7},{7,6},{8,9},{9,8},{10,11... | collective-permute-start | bytes 3538952 | tf_op jit(solution)/shard_map/ppermute | solution.py:146
  93.2 10.8 %collective-permute-start.5 = (bf16[256,2304]{1,0:T(8,128)(2,1)S(1)}, bf16[256,2304]{1,0:T(8,128)(2,1)S(1)}, u32[]{:S(2)}, u32[]{:S(2)}) collective-permute-start(bf16[256,2304]{1,0:T(8,128)(2,1)S(1)} %copy-done.34), channel_id=1, source_target_pairs={{0,1},{1,0},{2,3},{3,2},{4,5},{5,4},{6,7},{7,6},{8,9},{9,8},{10,11... | collective-permute-start | bytes 3538952 | tf_op jit(solution)/shard_map/ppermute | solution.py:146
  94.8 30.3 %collective-permute-start.9 = (bf16[128,2304]{1,0:T(8,128)(2,1)S(1)}, bf16[128,2304]{1,0:T(8,128)(2,1)S(1)}, u32[]{:S(2)}, u32[]{:S(2)}) collective-permute-start(bf16[128,2304]{1,0:T(8,128)(2,1)S(1)} %get-tuple-element.136), channel_id=1, source_target_pairs={{0,2},{1,5},{2,0},{3,7},{4,6},{5,1},{6,4},{7,3},{8,10},{9,13},{10,... | collective-permute-start | bytes 1769480 | tf_op jit(solution)/shard_map/ppermute | solution.py:146
  103.9 50.0 %collective-permute-start.13 = (bf16[256,2304]{1,0:T(8,128)(2,1)S(1)}, bf16[256,2304]{1,0:T(8,128)(2,1)S(1)}, u32[]{:S(2)}, u32[]{:S(2)}) collective-permute-start(bf16[256,2304]{1,0:T(8,128)(2,1)S(1)} %add_convert_fusion.3), channel_id=1, source_target_pairs={{0,2},{1,5},{2,0},{3,7},{4,6},{5,1},{6,4},{7,3},{8,10},{9,13},{10,... | collective-permute-start | bytes 3538952 | tf_op jit(solution)/shard_map/ppermute | solution.py:146
  125.2 19.0 %collective-permute-start.10 = (bf16[128,2304]{1,0:T(8,128)(2,1)S(1)}, bf16[128,2304]{1,0:T(8,128)(2,1)S(1)}, u32[]{:S(2)}, u32[]{:S(2)}) collective-permute-start(bf16[128,2304]{1,0:T(8,128)(2,1)S(1)} %get-tuple-element.137), channel_id=1, source_target_pairs={{0,2},{1,5},{2,0},{3,7},{4,6},{5,1},{6,4},{7,3},{8,10},{9,13},{10,... | collective-permute-start | bytes 1769480 | tf_op jit(solution)/shard_map/ppermute | solution.py:146
  144.1 10.4 %collective-permute-start.14 = (bf16[128,2304]{1,0:T(8,128)(2,1)S(1)}, bf16[128,2304]{1,0:T(8,128)(2,1)S(1)}, u32[]{:S(2)}, u32[]{:S(2)}) collective-permute-start(bf16[128,2304]{1,0:T(8,128)(2,1)S(1)} %add_convert_fusion.5), channel_id=1, source_target_pairs={{0,4},{1,3},{2,6},{3,1},{4,0},{5,7},{6,2},{7,5},{8,12},{9,11},{10,... | collective-permute-start | bytes 1769480 | tf_op jit(solution)/shard_map/ppermute | solution.py:146
  144.9 15.4 %collective-permute-start.15 = (bf16[128,2304]{1,0:T(8,128)(2,1)S(1)}, bf16[128,2304]{1,0:T(8,128)(2,1)S(1)}, u32[]{:S(2)}, u32[]{:S(2)}) collective-permute-start(bf16[128,2304]{1,0:T(8,128)(2,1)S(1)} %add_convert_fusion.4), channel_id=1, source_target_pairs={{0,4},{1,3},{2,6},{3,1},{4,0},{5,7},{6,2},{7,5},{8,12},{9,11},{10,... | collective-permute-start | bytes 1769480 | tf_op jit(solution)/shard_map/ppermute | solution.py:146
  146.4 37.2 %collective-permute-start.22 = (bf16[256,2304]{1,0:T(8,128)(2,1)}, bf16[256,2304]{1,0:T(8,128)(2,1)}, u32[]{:S(2)}, u32[]{:S(2)}) collective-permute-start(bf16[256,2304]{1,0:T(8,128)(2,1)} %collective-permute-done.18.refs_2_), channel_id=1, source_target_pairs={{0,4},{1,3},{2,6},{3,1},{4,0},{5,7},{6,2},{7,5},{8,12},{9,11},{10,... | collective-permute-start | bytes 3538952 | tf_op jit(solution)/shard_map/ppermute | solution.py:146
  146.9 13.4 %copy-start.18 = (bf16[1,256,2304]{2,1,0:T(8,128)(2,1)S(1)}, bf16[1,256,2304]{2,1,0:T(8,128)(2,1)}, u32[]{:S(2)}) copy-start(bf16[1,256,2304]{2,1,0:T(8,128)(2,1)} %param.17) | copy-start | bytes 3538948
  153.9 29.8 %collective-permute-start.17 = (bf16[256,2304]{1,0:T(8,128)(2,1)S(1)}, bf16[256,2304]{1,0:T(8,128)(2,1)}, u32[]{:S(2)}, u32[]{:S(2)}) collective-permute-start(bf16[256,2304]{1,0:T(8,128)(2,1)S(1)} %shard_map.208.refs_0_), channel_id=1, source_target_pairs={{0,1},{1,0},{2,3},{3,2},{4,5},{5,4},{6,7},{7,6},{8,9},{9,8},{10,11... | collective-permute-start | bytes 3538952 | tf_op jit(solution)/shard_map/ppermute | solution.py:146
  154.0 34.5 %collective-permute-start.20 = (bf16[256,2304]{1,0:T(8,128)(2,1)}, bf16[256,2304]{1,0:T(8,128)(2,1)}, u32[]{:S(2)}, u32[]{:S(2)}) collective-permute-start(bf16[256,2304]{1,0:T(8,128)(2,1)} %collective-permute-done.19.refs_4_), channel_id=1, source_target_pairs={{0,1},{1,0},{2,3},{3,2},{4,5},{5,4},{6,7},{7,6},{8,9},{9,8},{10,11... | collective-permute-start | bytes 3538952 | tf_op jit(solution)/shard_map/ppermute | solution.py:146
  154.5 34.6 %collective-permute-start.21 = (bf16[256,2304]{1,0:T(8,128)(2,1)}, bf16[256,2304]{1,0:T(8,128)(2,1)}, u32[]{:S(2)}, u32[]{:S(2)}) collective-permute-start(bf16[256,2304]{1,0:T(8,128)(2,1)} %collective-permute-done.18.refs_2_), channel_id=1, source_target_pairs={{0,1},{1,0},{2,3},{3,2},{4,5},{5,4},{6,7},{7,6},{8,9},{9,8},{10,11... | collective-permute-start | bytes 3538952 | tf_op jit(solution)/shard_map/ppermute | solution.py:146
  164.0 52.1 %copy-start = (bf16[256,2304]{1,0:T(8,128)(2,1)}, bf16[256,2304]{1,0:T(8,128)(2,1)S(1)}, u32[]{:S(2)}) copy-start(bf16[256,2304]{1,0:T(8,128)(2,1)S(1)} %get-tuple-element.98.refs_0_.refs_2_) | copy-start | bytes 3538948
  164.1 25.0 %collective-permute-start.26 = (bf16[256,2304]{1,0:T(8,128)(2,1)S(1)}, bf16[256,2304]{1,0:T(8,128)(2,1)S(1)}, u32[]{:S(2)}, u32[]{:S(2)}) collective-permute-start(bf16[256,2304]{1,0:T(8,128)(2,1)S(1)} %get-tuple-element.98.refs_0_.refs_2_), channel_id=1, source_target_pairs={{0,4},{1,3},{2,6},{3,1},{4,0},{5,7},{6,2},{7,5},{8,12},{9,11},{10,... | collective-permute-start | bytes 3538952 | tf_op jit(solution)/shard_map/ppermute | solution.py:146
  164.6 20.2 %copy-start.36 = (f32[2304]{0:T(1024)S(1)}, f32[2304]{0:T(1024)}, u32[]{:S(2)}) copy-start(f32[2304]{0:T(1024)} %param.22) | copy-start | bytes 27652
  164.6 20.3 %copy-start.37 = (f32[2304]{0:T(1024)S(1)}, f32[2304]{0:T(1024)}, u32[]{:S(2)}) copy-start(f32[2304]{0:T(1024)} %param.23) | copy-start | bytes 27652
  183.6 5.5 %collective-permute-start.23 = (bf16[256,2304]{1,0:T(8,128)(2,1)}, bf16[256,2304]{1,0:T(8,128)(2,1)}, u32[]{:S(2)}, u32[]{:S(2)}) collective-permute-start(bf16[256,2304]{1,0:T(8,128)(2,1)} %collective-permute-done.22.refs_6_), channel_id=1, source_target_pairs={{0,1},{1,0},{2,3},{3,2},{4,5},{5,4},{6,7},{7,6},{8,9},{9,8},{10,11... | collective-permute-start | bytes 3538952 | tf_op jit(solution)/shard_map/ppermute | solution.py:146
  183.7 16.2 %collective-permute-start.16 = (bf16[256,2304]{1,0:T(8,128)(2,1)S(1)}, bf16[256,2304]{1,0:T(8,128)(2,1)S(1)}, u32[]{:S(2)}, u32[]{:S(2)}) collective-permute-start(bf16[256,2304]{1,0:T(8,128)(2,1)S(1)} %get-tuple-element.98.refs_0_.refs_2_), channel_id=1, source_target_pairs={{0,2},{1,5},{2,0},{3,7},{4,6},{5,1},{6,4},{7,3},{8,10},{9,13},{10,... | collective-permute-start | bytes 3538952 | tf_op jit(solution)/shard_map/ppermute | solution.py:146
  188.5 27.7 %collective-permute-start.25 = (bf16[256,2304]{1,0:T(8,128)(2,1)S(1)}, bf16[256,2304]{1,0:T(8,128)(2,1)}, u32[]{:S(2)}, u32[]{:S(2)}) collective-permute-start(bf16[256,2304]{1,0:T(8,128)(2,1)S(1)} %get-tuple-element.98.refs_0_.refs_2_), channel_id=1, source_target_pairs={{0,1},{1,0},{2,3},{3,2},{4,5},{5,4},{6,7},{7,6},{8,9},{9,8},{10,11... | collective-permute-start | bytes 3538952 | tf_op jit(solution)/shard_map/ppermute | solution.py:146
  189.0 27.1 %copy-start.3 = (bf16[256,2304]{1,0:T(8,128)(2,1)}, bf16[256,2304]{1,0:T(8,128)(2,1)S(1)}, u32[]{:S(2)}) copy-start(bf16[256,2304]{1,0:T(8,128)(2,1)S(1)} %collective-permute-done.26.refs_4_) | copy-start | bytes 3538948
  189.0 27.1 %collective-permute-start.27 = (bf16[256,2304]{1,0:T(8,128)(2,1)S(1)}, bf16[256,2304]{1,0:T(8,128)(2,1)}, u32[]{:S(2)}, u32[]{:S(2)}) collective-permute-start(bf16[256,2304]{1,0:T(8,128)(2,1)S(1)} %collective-permute-done.26.refs_4_), channel_id=1, source_target_pairs={{0,1},{1,0},{2,3},{3,2},{4,5},{5,4},{6,7},{7,6},{8,9},{9,8},{10,11... | collective-permute-start | bytes 3538952 | tf_op jit(solution)/shard_map/ppermute | solution.py:146
  199.9 16.3 %copy-start.4 = (bf16[256,2304]{1,0:T(8,128)(2,1)}, bf16[256,2304]{1,0:T(8,128)(2,1)S(1)}, u32[]{:S(2)}) copy-start(bf16[256,2304]{1,0:T(8,128)(2,1)S(1)} %collective-permute-done.16.refs_2_) | copy-start | bytes 3538948
  199.9 16.2 %collective-permute-start.28 = (bf16[256,2304]{1,0:T(8,128)(2,1)S(1)}, bf16[256,2304]{1,0:T(8,128)(2,1)}, u32[]{:S(2)}, u32[]{:S(2)}) collective-permute-start(bf16[256,2304]{1,0:T(8,128)(2,1)S(1)} %collective-permute-done.16.refs_2_), channel_id=1, source_target_pairs={{0,1},{1,0},{2,3},{3,2},{4,5},{5,4},{6,7},{7,6},{8,9},{9,8},{10,11... | collective-permute-start | bytes 3538952 | tf_op jit(solution)/shard_map/ppermute | solution.py:146
  199.9 22.0 %collective-permute-start.24 = (bf16[256,2304]{1,0:T(8,128)(2,1)S(1)}, bf16[256,2304]{1,0:T(8,128)(2,1)}, u32[]{:S(2)}, u32[]{:S(2)}) collective-permute-start(bf16[256,2304]{1,0:T(8,128)(2,1)S(1)} %collective-permute-done.16.refs_2_), channel_id=1, source_target_pairs={{0,4},{1,3},{2,6},{3,1},{4,0},{5,7},{6,2},{7,5},{8,12},{9,11},{10,... | collective-permute-start | bytes 3538952 | tf_op jit(solution)/shard_map/ppermute | solution.py:146
  221.9 3.1 collective-permute-start.29
  222.0 26.9 %collective-permute-start.32 = (bf16[256,2304]{1,0:T(8,128)(2,1)S(1)}, bf16[256,2304]{1,0:T(8,128)(2,1)S(1)}, u32[]{:S(2)}, u32[]{:S(2)}) collective-permute-start(bf16[256,2304]{1,0:T(8,128)(2,1)S(1)} %copy-done.16), channel_id=1, source_target_pairs={{0,2},{1,5},{2,0},{3,7},{4,6},{5,1},{6,4},{7,3},{8,10},{9,13},{10,... | collective-permute-start | bytes 3538952 | tf_op jit(solution)/shard_map/ppermute | solution.py:146
  248.9 59.3 %copy-start.40 = (bf16[256,2304]{1,0:T(8,128)(2,1)}, bf16[256,2304]{1,0:T(8,128)(2,1)S(1)}, u32[]{:S(2)}) copy-start(bf16[256,2304]{1,0:T(8,128)(2,1)S(1)} %collective-permute-done.32.refs_2_) | copy-start | bytes 3538948
  266.6 2.9 collective-permute-start.30
  266.8 41.5 %collective-permute-start.33 = (bf16[256,2304]{1,0:T(8,128)(2,1)S(1)}, bf16[256,2304]{1,0:T(8,128)(2,1)S(1)}, u32[]{:S(2)}, u32[]{:S(2)}) collective-permute-start(bf16[256,2304]{1,0:T(8,128)(2,1)S(1)} %copy-done.16), channel_id=1, source_target_pairs={{0,4},{1,3},{2,6},{3,1},{4,0},{5,7},{6,2},{7,5},{8,12},{9,11},{10,... | collective-permute-start | bytes 3538952 | tf_op jit(solution)/shard_map/ppermute | solution.py:146
  267.4 40.9 %collective-permute-start.36 = (bf16[256,2304]{1,0:T(8,128)(2,1)S(1)}, bf16[256,2304]{1,0:T(8,128)(2,1)S(1)}, u32[]{:S(2)}, u32[]{:S(2)}) collective-permute-start(bf16[256,2304]{1,0:T(8,128)(2,1)S(1)} %collective-permute-done.32.refs_2_), channel_id=1, source_target_pairs={{0,4},{1,3},{2,6},{3,1},{4,0},{5,7},{6,2},{7,5},{8,12},{9,11},{10,... | collective-permute-start | bytes 3538952 | tf_op jit(solution)/shard_map/ppermute | solution.py:146
  268.8 40.0 %collective-permute-start.38 = (bf16[256,2304]{1,0:T(8,128)(2,1)S(1)}, bf16[256,2304]{1,0:T(8,128)(2,1)S(1)}, u32[]{:S(2)}, u32[]{:S(2)}) collective-permute-start(bf16[256,2304]{1,0:T(8,128)(2,1)S(1)} %get-tuple-element.120), channel_id=1, source_target_pairs={{0,1},{1,0},{2,3},{3,2},{4,5},{5,4},{6,7},{7,6},{8,9},{9,8},{10,11... | collective-permute-start | bytes 3538952 | tf_op jit(solution)/shard_map/ppermute | solution.py:146
  277.7 32.9 %copy-start.19 = (bf16[256,2304]{1,0:T(8,128)(2,1)}, bf16[256,2304]{1,0:T(8,128)(2,1)S(1)}, u32[]{:S(2)}) copy-start(bf16[256,2304]{1,0:T(8,128)(2,1)S(1)} %get-tuple-element.126.own) | copy-start | bytes 3538948
  277.7 31.1 %collective-permute-start.39 = (bf16[256,2304]{1,0:T(8,128)(2,1)S(1)}, bf16[256,2304]{1,0:T(8,128)(2,1)S(1)}, u32[]{:S(2)}, u32[]{:S(2)}) collective-permute-start(bf16[256,2304]{1,0:T(8,128)(2,1)S(1)} %get-tuple-element.122), channel_id=1, source_target_pairs={{0,1},{1,0},{2,3},{3,2},{4,5},{5,4},{6,7},{7,6},{8,9},{9,8},{10,11... | collective-permute-start | bytes 3538952 | tf_op jit(solution)/shard_map/ppermute | solution.py:146
  277.9 32.7 %collective-permute-start.40 = (bf16[256,2304]{1,0:T(8,128)(2,1)S(1)}, bf16[256,2304]{1,0:T(8,128)(2,1)S(1)}, u32[]{:S(2)}, u32[]{:S(2)}) collective-permute-start(bf16[256,2304]{1,0:T(8,128)(2,1)S(1)} %add_convert_fusion.2), channel_id=1, source_target_pairs={{0,2},{1,5},{2,0},{3,7},{4,6},{5,1},{6,4},{7,3},{8,10},{9,13},{10,... | collective-permute-start | bytes 3538952 | tf_op jit(solution)/shard_map/ppermute | solution.py:146
  308.2 3.9 %collective-permute-start.31 = (bf16[256,2304]{1,0:T(8,128)(2,1)S(1)}, bf16[256,2304]{1,0:T(8,128)(2,1)S(1)}, u32[]{:S(2)}, u32[]{:S(2)}) collective-permute-start(bf16[256,2304]{1,0:T(8,128)(2,1)S(1)} %copy-done.16), channel_id=1, source_target_pairs={{0,1},{1,0},{2,3},{3,2},{4,5},{5,4},{6,7},{7,6},{8,9},{9,8},{10,11... | collective-permute-start | bytes 3538952 | tf_op jit(solution)/shard_map/ppermute | solution.py:146
  308.3 7.5 %collective-permute-start.35 = (bf16[256,2304]{1,0:T(8,128)(2,1)S(1)}, bf16[256,2304]{1,0:T(8,128)(2,1)S(1)}, u32[]{:S(2)}, u32[]{:S(2)}) collective-permute-start(bf16[256,2304]{1,0:T(8,128)(2,1)S(1)} %collective-permute-done.32.refs_2_), channel_id=1, source_target_pairs={{0,1},{1,0},{2,3},{3,2},{4,5},{5,4},{6,7},{7,6},{8,9},{9,8},{10,11... | collective-permute-start | bytes 3538952 | tf_op jit(solution)/shard_map/ppermute | solution.py:146
  308.8 5.7 %collective-permute-start.34 = (bf16[256,2304]{1,0:T(8,128)(2,1)S(1)}, bf16[256,2304]{1,0:T(8,128)(2,1)S(1)}, u32[]{:S(2)}, u32[]{:S(2)}) collective-permute-start(bf16[256,2304]{1,0:T(8,128)(2,1)S(1)} %collective-permute-done.33.refs_4_), channel_id=1, source_target_pairs={{0,1},{1,0},{2,3},{3,2},{4,5},{5,4},{6,7},{7,6},{8,9},{9,8},{10,11... | collective-permute-start | bytes 3538952 | tf_op jit(solution)/shard_map/ppermute | solution.py:146
  308.8 7.4 %collective-permute-start.37 = (bf16[256,2304]{1,0:T(8,128)(2,1)S(1)}, bf16[256,2304]{1,0:T(8,128)(2,1)}, u32[]{:S(2)}, u32[]{:S(2)}) collective-permute-start(bf16[256,2304]{1,0:T(8,128)(2,1)S(1)} %collective-permute-done.36.refs_6_), channel_id=1, source_target_pairs={{0,1},{1,0},{2,3},{3,2},{4,5},{5,4},{6,7},{7,6},{8,9},{9,8},{10,11... | collective-permute-start | bytes 3538952 | tf_op jit(solution)/shard_map/ppermute | solution.py:146
  310.6 26.0 %collective-permute-start.41 = (bf16[256,2304]{1,0:T(8,128)(2,1)}, bf16[256,2304]{1,0:T(8,128)(2,1)}, u32[]{:S(2)}, u32[]{:S(2)}) collective-permute-start(bf16[256,2304]{1,0:T(8,128)(2,1)} %get-tuple-element.127), channel_id=1, source_target_pairs={{0,1},{1,0},{2,3},{3,2},{4,5},{5,4},{6,7},{7,6},{8,9},{9,8},{10,11... | collective-permute-start | bytes 3538952 | tf_op jit(solution)/shard_map/ppermute | solution.py:146
  312.2 27.7 %collective-permute-start.43 = (bf16[256,2304]{1,0:T(8,128)(2,1)}, bf16[256,2304]{1,0:T(8,128)(2,1)}, u32[]{:S(2)}, u32[]{:S(2)}) collective-permute-start(bf16[256,2304]{1,0:T(8,128)(2,1)} %add_convert_fusion), channel_id=1, source_target_pairs={{0,4},{1,3},{2,6},{3,1},{4,0},{5,7},{6,2},{7,5},{8,12},{9,11},{10,... | collective-permute-start | bytes 3538952 | tf_op jit(solution)/shard_map/ppermute | solution.py:146
  314.5 26.4 %collective-permute-start.42 = (bf16[256,2304]{1,0:T(8,128)(2,1)}, bf16[256,2304]{1,0:T(8,128)(2,1)}, u32[]{:S(2)}, u32[]{:S(2)}) collective-permute-start(bf16[256,2304]{1,0:T(8,128)(2,1)} %add_convert_fusion.1), channel_id=1, source_target_pairs={{0,2},{1,5},{2,0},{3,7},{4,6},{5,1},{6,4},{7,3},{8,10},{9,13},{10,... | collective-permute-start | bytes 3538952 | tf_op jit(solution)/shard_map/ppermute | solution.py:146
  346.1 10.8 %collective-permute-start.46 = (f32[6,2304]{1,0:T(8,128)S(1)}, f32[6,2304]{1,0:T(8,128)S(1)}, u32[]{:S(2)}, u32[]{:S(2)}) collective-permute-start(f32[6,2304]{1,0:T(8,128)S(1)} %get-tuple-element.130), channel_id=1, source_target_pairs={{0,6},{1,7},{2,4},{3,5},{4,2},{5,3},{6,0},{7,1},{8,14},{9,15},{10,... | collective-permute-start | bytes 165896 | tf_op jit(solution)/shard_map/ppermute | solution.py:146
  347.8 9.2 %collective-permute-start.45 = (f32[6,2304]{1,0:T(8,128)S(1)}, f32[6,2304]{1,0:T(8,128)S(1)}, u32[]{:S(2)}, u32[]{:S(2)}) collective-permute-start(f32[6,2304]{1,0:T(8,128)S(1)} %get-tuple-element.130), channel_id=1, source_target_pairs={{0,4},{1,5},{2,6},{3,7},{4,0},{5,1},{6,2},{7,3},{8,12},{9,13},{10,... | collective-permute-start | bytes 165896 | tf_op jit(solution)/shard_map/ppermute | solution.py:146
  348.3 8.6 %collective-permute-start.44 = (f32[6,2304]{1,0:T(8,128)S(1)}, f32[6,2304]{1,0:T(8,128)S(1)}, u32[]{:S(2)}, u32[]{:S(2)}) collective-permute-start(f32[6,2304]{1,0:T(8,128)S(1)} %get-tuple-element.130), channel_id=1, source_target_pairs={{0,2},{1,3},{2,0},{3,1},{4,6},{5,7},{6,4},{7,5},{8,10},{9,11},{10,... | collective-permute-start | bytes 165896 | tf_op jit(solution)/shard_map/ppermute | solution.py:146
  357.0 1.3 collective-permute-start.47
  (30 other events, 117.9 us)

commit v2 on v1

--- a/solution.py
+++ b/solution.py
@@ -209,7 +209,7 @@
 
 def call(kernel, grid, in_specs, out_specs, out_shape, scratch, flops, args):
     return pl.pallas_call(kernel,grid=grid,in_specs=in_specs,out_specs=out_specs,out_shape=out_shape,
-        scratch_shapes=scratch,compiler_params=pltpu.CompilerParams(dimension_semantics=("arbitrary",)*len(grid),vmem_limit_bytes=40<<20),
+        scratch_shapes=scratch,compiler_params=pltpu.CompilerParams(dimension_semantics=("arbitrary",)*len(grid),vmem_limit_bytes=24<<20),
         cost_estimate=pl.CostEstimate(flops=flops,bytes_accessed=30<<20,transcendentals=0))(*args)
 
 RB=256; SUB=BLK//RB
@@ -255,7 +255,7 @@
         db_ref[...]+=fold8(dz.astype(f32))
         @pl.when(s==0)
         def _(): wcopy(1).wait()
-        if first>0: st[rows,:]=tn(dz_ref[...],w1s[...],1,1).astype(bf16)
+        if first==1: st[rows,:]=tn(dz_ref[...],w1s[...],1,1).astype(bf16)
         else:
             def part(c,_):
                 at=pl.ds(pl.multiple_of(c*768,768),768)
@@ -302,7 +302,7 @@
         [pl.BlockSpec(memory_space=ANY)]*4,[jax.ShapeDtypeStruct((BLK,D),bf16)]*4,
         [pltpu.VMEM((4*BLK,D),bf16),pltpu.SemaphoreType.DMA((4,))],T*D*K,(dqkv,wqkv))
 
-def gathered_mm(body, pieces, other, n, out_spec, out_shape, flops, cols=(0,D), into=None):
+def gathered_mm(body, pieces, other, n, out_spec, out_shape, flops, cols=(0,D), into=None, vmem=60):
     W=(cols[1]-cols[0])//n
     def kernel(*refs):
         ps=refs[:8]; o_ref=refs[8]; out,full,sem=refs[-3:]
@@ -321,7 +321,7 @@
     extra=() if into is None else (into,)
     return pl.pallas_call(kernel,grid=(n,),in_specs=[any_]*8+[pl.BlockSpec(other.shape,lambda s:(0,0))]+[any_]*len(extra),out_specs=out_spec,out_shape=out_shape,
         scratch_shapes=[pltpu.VMEM((n,T,W),bf16),pltpu.SemaphoreType.DMA((n,8))],input_output_aliases={9:0} if extra else {},
-        compiler_params=pltpu.CompilerParams(dimension_semantics=("arbitrary",),vmem_limit_bytes=60<<20),
+        compiler_params=pltpu.CompilerParams(dimension_semantics=("arbitrary",),vmem_limit_bytes=vmem<<20),
         cost_estimate=pl.CostEstimate(flops=flops,bytes_accessed=30<<20,transcendentals=0))(*pieces,other,*extra)
 
 def ctx_grad(first, pieces, wo, into):
@@ -360,14 +360,14 @@
         dya,dyb,dyp=hop_a(d_out),hop_b(d_out),partner(d_out)
         dzu,db_0,(o0,o1)=mlp(0,blk,[d_out,dyp],z,w_fc2,w_fc1,None)
         h2_local=layer_norm_fwd(after(x_mid,db_0),g2,b2)
-        ctx,lse0=attn_fwd(0,1,me1,after(q,db_0),k,v,None)
-        dya=after(dya,lse0,h2_local)
+        dya=after(dya,db_0,h2_local)
         dyd=hop_b(dya)
         h2_local=after(h2_local,dya)
         h2a,h2b,h2p=hop_a(h2_local),hop_b(h2_local),partner(h2_local)
         dypa,dypb=partner(dya),partner(dyb)
         dzu,db_1,(pa0,pa1,pb0,pb1)=mlp(1,blk,[dya,dypb,dyb,dypa],z,w_fc2,w_fc1,dzu)
         ra,rb,ro=partner(pb1),partner(pa1),partner(o1)
+        h1_local=layer_norm_fwd(after(x_in,db_1),g1,b1)
         a_in=hop_a(add2(pa0,ra))
         dypd=partner(dyd)
         (dz,u),db_2,(pd0,pd1)=mlp(3,blk,[dyd,dypd],z,w_fc2,w_fc1,dzu)
@@ -375,13 +375,13 @@
         d_sum=[add2(pd0[:128],rd[:128]),add2(pd0[128:],rd[128:])]
         d_in=[hop_a(d_sum[0]),hop_a(d_sum[1])]
         def b_half(k,lse): return (pb0[128*k:128*k+128].astype(f32)+after(rb,lse)[128*k:128*k+128].astype(f32)+d_in[k].astype(f32)).astype(bf16)
-        ctx,lse1=attn_fwd(1,1,me1,after(q,*d_sum),k,v,ctx)
-        b_sum=b_half(0,lse1)
+        ctx,lse0=attn_fwd(0,1,me1,after(q,*d_sum),k,v,None)
+        b_sum=b_half(0,lse0)
         b_in0=hop_b(b_sum)
-        b_sum=b_half(1,b_sum)
+        ctx,lse1=attn_fwd(1,1,me1,after(q,b_sum),k,v,ctx)
+        b_sum=b_half(1,lse1)
         b_in1=hop_b(b_sum)
         ctx,lse2=attn_fwd(2,1,me1,after(q,b_sum),k,v,ctx)
-        lse01=join(lse0,lse1)
         h2a=after(h2a,b_sum)
         h2d=hop_b(h2a); h2pa,h2pb=partner(h2a),partner(h2b)
         mid,vec2=ln_bwd((after(o0,lse2),ro,a_in,b_in0,b_in1),x_mid,d_out,g2,g2.reshape(1,D))
@@ -389,14 +389,14 @@
         dxa,dxb,dxp=hop_a(mid),hop_b(mid),partner(mid)
         dys=[d_out,dyp,dya,dypb,dyb,dypa,dyd,dypd]
         grad_wfc2=gathered_mm(lambda x,o: tn(o[...],x,0,0),dys,after(u,mid),9,
-            pl.BlockSpec((F,256),lambda s:(0,s)),jax.ShapeDtypeStruct((F,D),f32),2*T*D*F)
+            pl.BlockSpec((F,256),lambda s:(0,s)),jax.ShapeDtypeStruct((F,D),f32),2*T*D*F,vmem=60)
         h2pd=partner(after(h2d,grad_wfc2))
         h2=[h2_local,h2p,h2a,h2pb,h2b,h2pa,h2d,h2pd]
-        h1_local=layer_norm_fwd(after(x_in,grad_wfc2),g1,b1)
+        lse01=join(after(lse0,grad_wfc2),lse1)
         def w1_part(c0,n,left,into):
             return gathered_mm(lambda x,o: tn(x,o[...],0,0),h2,left,n,
-                pl.BlockSpec((256,F),lambda s:(s+c0,0)),jax.ShapeDtypeStruct((D,F),f32),2*T*256*n*F,cols=(256*c0,256*(c0+n)),into=into)
-        grad_wfc1=w1_part(0,3,after(dz,h1_local),None)
+                pl.BlockSpec((256,F),lambda s:(s+c0,0)),jax.ShapeDtypeStruct((D,F),f32),2*T*256*n*F,cols=(256*c0,256*(c0+n)),into=into,vmem=26)
+        grad_wfc1=w1_part(0,3,after(dz,grad_wfc2),None)
         dxa=after(dxa,grad_wfc1)
         dxd=hop_b(dxa)
         dxpa,dxpb=partner(dxa),partner(dxb)
@@ -413,6 +413,7 @@
         h1d=hop_b(h1a); h1pa,h1pb=partner(h1a),partner(h1b)
         dqkv=attn_bwd(2,1,me1,q,k,v,dctx,lse2,dqkv)
         dqkv=dqkv.reshape(3*NH*E,T)
+        grad_bqkv=jnp.sum(dqkv,axis=1,dtype=f32).reshape(3,NH,E)
         pd0,pd1,pa0,pa1=attn_in_grad((3,1),dqkv,wqkv)
         d_sum=add2(pd0,partner(pd1))
         d_in=hop_a(d_sum)
@@ -426,18 +427,17 @@
         h1pd=partner(after(h1d,dqkv))
         h1=[h1_local,h1p,h1a,h1pb,h1b,h1pa,h1d,h1pd]
         grad_wqkv=gathered_mm(lambda x,o: jnp.dot(o[...],x,preferred_element_type=f32),h1,after(dqkv,b_sum),3,
-            pl.BlockSpec((3*NH*E,768),lambda s:(0,s)),jax.ShapeDtypeStruct((3*NH*E,D),f32),6*T*D*NH*E)
+            pl.BlockSpec((3*NH*E,768),lambda s:(0,s)),jax.ShapeDtypeStruct((3*NH*E,D),f32),6*T*D*NH*E,vmem=30)
         def wo_part(c0,n,left,into):
             return gathered_mm(lambda x,o: jnp.dot(o[...],x,preferred_element_type=f32),dx1,left,n,
-                pl.BlockSpec((NH*E,256),lambda s:(0,s+c0)),jax.ShapeDtypeStruct((NH*E,D),f32),n*T*256*NH*E*2,cols=(256*c0,256*(c0+n)),into=into)
+                pl.BlockSpec((NH*E,256),lambda s:(0,s+c0)),jax.ShapeDtypeStruct((NH*E,D),f32),n*T*256*NH*E*2,cols=(256*c0,256*(c0+n)),into=into,vmem=14)
         ctx=ctx.reshape(NH*E,T)
-        grad_wproj=wo_part(0,3,after(ctx,grad_wqkv),None)
+        grad_wproj=wo_part(0,6,after(ctx,grad_wqkv),None)
         dx,grad_vecs=ln_bwd((after(o0,grad_wproj),ro,a_in,b_in),x_in,mid,g1,vec2)
         v2,v4,v6=(send(grad_vecs,[(i,i^k) for i in range(8)]) for k in (2,4,6))
-        grad_wproj=wo_part(3,6,after(ctx,dx),grad_wproj)
+        grad_wproj=wo_part(6,3,after(ctx,dx),grad_wproj)
         vecs=(grad_vecs+after(v2,grad_wproj))+(v4+v6)
         v1=send(vecs,[(i,i^1) for i in range(8)])
-        grad_bqkv=jnp.sum(after(dqkv,vecs),axis=1,dtype=f32).reshape(3,NH,E)
         grad_vecs=vecs+v1
         grad_wproj=grad_wproj.reshape(NH,E,D)
         grad_wqkv=grad_wqkv.reshape(3,NH,E,D).transpose(0,3,1,2)

time: 360 us -> 349 us (0.969)
  Pallas kernels: 209 us -> 192 us
  starting transfers between devices: 27.8 us -> 38.9 us
  waiting for transfers between devices: 101 us -> 90 us
  local copies, waits for them, and re-layouts: 14.2 us -> 20 us
    pallas_call x6, Pallas kernels: 70.7 us -> 58 us  [gathered_mm(): pl.pallas_call(kernel, grid=(n,), in_specs=[any_] * 8 + [pl.BlockSpec(oth...]
    ppermute x48, waiting for transfers between devices: 101 us -> 90 us  [send(): return lax.ppermute(a, 'tp', pairs)]
    ppermute x48, starting transfers between devices: 27.8 us -> 38.9 us  [send(): return lax.ppermute(a, 'tp', pairs)]
    unnamed x92 -> x68, local copies, waits for them, and re-layouts: 12.1 us -> 18.6 us
  transfers between devices with their start and end apart: 48 -> 48, of which waited for: 14 -> 14; matrix products, arithmetic and copies ran while one was open for 2% -> 2% of each run, Pallas kernels for 48% -> 45%
where the time goes in v2:
time: 349 us; the launch traced here: 348 us
  Pallas kernels  192 us (55%)
  waiting for transfers between devices  90 us (26%)
  starting transfers between devices  38.9 us (11%)
  local copies, waits for them, and re-layouts  20 us (6%)
  other arithmetic  6.62 us (2%)
    ppermute x48, waiting for transfers between devices, send(): return lax.ppermute(a, 'tp', pairs)  90 us
    pallas_call x6, Pallas kernels, gathered_mm(): pl.pallas_call(kernel, grid=(n,), in_specs=[any_] * 8 + [pl.BlockSpec(oth...  58 us
    pallas_call x5, Pallas kernels, attn_call(): pl.pallas_call(kernel, grid_spec=pltpu.PrefetchScalarGridSpec(num_scalar_...  52.7 us
    pallas_call x3, Pallas kernels, mlp(): pl.pallas_call(kernel, grid_spec=pltpu.PrefetchScalarGridSpec(num_scalar_...  51.1 us
    ppermute x48, starting transfers between devices, send(): return lax.ppermute(a, 'tp', pairs)  38.9 us
    unnamed x68, local copies, waits for them, and re-layouts  18.6 us
    pallas_call x2, Pallas kernels, call(): pl.pallas_call(kernel, grid=grid, in_specs=in_specs, out_specs=out_specs,...  14.3 us
    pallas_call x2, Pallas kernels, ln_bwd(): pl.pallas_call(ln_bwd_kernel, grid=(256 // R,), in_specs=[blk] * 3 + b_sp...  7.22 us
  transfers between devices with their start and end apart: 48, of which 14 were waited for; matrix products, arithmetic and copies ran while one was open for 2% of the time, Pallas kernels for 45%

profile of v2, /device:TPU:0, one launch (start us, length us, event | category | flops | bytes accessed | tf_op | source)
XLA Modules:
  0.0 348.3 jit_solution(4758198815292062560)
XLA Ops:
  1.4 2.5 collective-permute-start.1
  3.9 1.5 collective-permute-start.2
  6.9 1.7 copy-done.8
  8.6 14.4 %shard_map.206 = (bf16[2048,1152]{1,0:T(8,128)(2,1)}, bf16[2048,1152]{1,0:T(8,128)(2,1)}, f32[8,1152]{1,0:T(8,128)S(1)}, bf16[256,2304]{1,0:T(8,128)(2,1)S(1)}, bf16[256,2304]{1,0:T(8,128)(2,1)S(1)}) custom-call(s32[8]{0:T(128)S(1)} %fusion.1.refs_0_, bf16[256,2304]{1,0:T(8,128)(2,1)S(1)} %bitcast.43, ...), custom_call_target="tpu_custom_call" | custom-call | flops 5435817984 | bytes 20971520 | tf_op jit(solution)/shard_map/pallas_call | solution.py:274
  23.0 1.3 shard_map.207.refs_0_
  24.3 5.6 %collective-permute-done.1.refs_1_.refs_2_ = bf16[256,2304]{1,0:T(8,128)(2,1)} collective-permute-done((bf16[256,2304]{1,0:T(8,128)(2,1)}, bf16[256,2304]{1,0:T(8,128)(2,1)}, u32[]{:S(2)}, u32[]{:S(2)}) %collective-permute-start.1) | collective-permute-done | bytes 1179680 | tf_op jit(solution)/shard_map/ppermute | solution.py:146
  29.9 2.7 collective-permute-start.6
  33.1 13.9 %collective-permute-done.6.refs_1_.refs_6_ = bf16[256,2304]{1,0:T(8,128)(2,1)S(1)} collective-permute-done((bf16[256,2304]{1,0:T(8,128)(2,1)}, bf16[256,2304]{1,0:T(8,128)(2,1)S(1)}, u32[]{:S(2)}, u32[]{:S(2)}) %collective-permute-start.6) | collective-permute-done | bytes 1179680 | tf_op jit(solution)/shard_map/ppermute | solution.py:146
  47.0 1.0 copy-done.32
  48.4 22.4 %shard_map.208 = (bf16[2048,1152]{1,0:T(8,128)(2,1)}, bf16[2048,1152]{1,0:T(8,128)(2,1)}, f32[8,1152]{1,0:T(8,128)S(1)}, bf16[256,2304]{1,0:T(8,128)(2,1)S(1)}, ...) custom-call(s32[8]{0:T(128)S(1)} %fusion.1.refs_0_, ...), custom_call_target="tpu_custom_call", output_to_operand_aliasing={{0}: (8, {}), {1}: (9, {})} | custom-call | flops 10871635968 | bytes 20971520 | tf_op jit(solution)/shard_map/pallas_call | solution.py:274
  70.9 14.4 %shard_map.209 = (bf16[2048,1152]{1,0:T(8,128)(2,1)}, bf16[2048,1152]{1,0:T(8,128)(2,1)}, f32[8,1152]{1,0:T(8,128)S(1)}, bf16[256,2304]{1,0:T(8,128)(2,1)S(1)}, bf16[256,2304]{1,0:T(8,128)(2,1)S(1)}) custom-call(s32[8]{0:T(128)S(1)} %fusion.1.refs_0_, ...), custom_call_target="tpu_custom_call", output_to_operand_aliasing={{0}: (6, {}), {1}: (7, {})} | custom-call | flops 5435817984 | bytes 20971520 | tf_op jit(solution)/shard_map/pallas_call | solution.py:274
  85.8 2.0 collective-permute-start.19
  87.8 1.7 collective-permute-start.18
  90.4 1.3 collective-permute-start.9
  92.0 1.0 copy-done.11
  93.7 6.9 %shard_map.210 = (bf16[3,96,2048]{2,1,0:T(8,128)(2,1)S(1)}, f32[1,1,2048]{2,1,0:T(1,128)S(1)}) custom-call(s32[1]{0:T(128)} %bitcast.me_ref._, bf16[3,96,2048]{2,1,0:T(8,128)(2,1)S(1)} %bitcast.47, bf16[3,96,2048]{2,1,0:T(8,128)(2,1)S(1)} %bitcast.52, bf16[3,96,2048]{2,1,0:T(8,128)(2,1)S(1)} %bitcast.57, s32[1]{0:T(128)} %bitcast.me_ref._), custom_call_target="tpu_custom_call" | custom-call | flops 2684354560 | bytes 3145728 | tf_op jit(solution)/shard_map/pallas_call | solution.py:117
  101.4 19.0 %collective-permute-done.9 = bf16[128,2304]{1,0:T(8,128)(2,1)S(1)} collective-permute-done((bf16[128,2304]{1,0:T(8,128)(2,1)S(1)}, bf16[128,2304]{1,0:T(8,128)(2,1)S(1)}, u32[]{:S(2)}, u32[]{:S(2)}) %collective-permute-start.9) | collective-permute-done | bytes 589856 | tf_op jit(solution)/shard_map/ppermute | solution.py:146
  120.5 1.7 collective-permute-start.10
  122.5 7.2 %shard_map.211 = (bf16[3,96,2048]{2,1,0:T(8,128)(2,1)S(1)}, f32[1,1,2048]{2,1,0:T(1,128)S(1)}) custom-call(s32[1]{0:T(128)} %bitcast.me_ref._, bf16[3,96,2048]{2,1,0:T(8,128)(2,1)S(1)} %bitcast.48, bf16[3,96,2048]{2,1,0:T(8,128)(2,1)S(1)} %bitcast.53, bf16[3,96,2048]{2,1,0:T(8,128)(2,1)S(1)} %bitcast.58, ...), custom_call_target="tpu_custom_call", output_to_operand_aliasing={{0}: (4, {})} | custom-call | flops 2684354560 | bytes 3145728 | tf_op jit(solution)/shard_map/pallas_call | solution.py:117
  129.6 9.8 %collective-permute-done.10 = bf16[128,2304]{1,0:T(8,128)(2,1)S(1)} collective-permute-done((bf16[128,2304]{1,0:T(8,128)(2,1)S(1)}, bf16[128,2304]{1,0:T(8,128)(2,1)S(1)}, u32[]{:S(2)}, u32[]{:S(2)}) %collective-permute-start.10) | collective-permute-done | bytes 589856 | tf_op jit(solution)/shard_map/ppermute | solution.py:146
  139.7 2.0 collective-permute-start.15
  141.8 2.0 collective-permute-start.22
  143.8 7.0 %shard_map.212 = (bf16[3,96,2048]{2,1,0:T(8,128)(2,1)S(1)}, f32[1,1,2048]{2,1,0:T(1,128)S(1)}) custom-call(s32[1]{0:T(128)} %bitcast.me_ref._, bf16[3,96,2048]{2,1,0:T(8,128)(2,1)S(1)} %bitcast.49, bf16[3,96,2048]{2,1,0:T(8,128)(2,1)S(1)} %bitcast.54, bf16[3,96,2048]{2,1,0:T(8,128)(2,1)S(1)} %bitcast.59, ...), custom_call_target="tpu_custom_call", output_to_operand_aliasing={{0}: (4, {})} | custom-call | flops 2684354560 | bytes 3145728 | tf_op jit(solution)/shard_map/pallas_call | solution.py:117
  151.3 4.6 %collective-permute-done.14.refs_0_ = bf16[128,2304]{1,0:T(8,128)(2,1)S(1)} collective-permute-done((bf16[128,2304]{1,0:T(8,128)(2,1)S(1)}, bf16[128,2304]{1,0:T(8,128)(2,1)S(1)}, u32[]{:S(2)}, u32[]{:S(2)}) %collective-permute-start.14) | collective-permute-done | bytes 589856 | tf_op jit(solution)/shard_map/ppermute | solution.py:146
  155.9 3.7 %shard_map.213 = (bf16[256,2304]{1,0:T(8,128)(2,1)S(1)}, f32[4,2304]{1,0:T(4,128)S(1)}) custom-call(bf16[256,2304]{1,0:T(8,128)(2,1)S(1)} %get-tuple-element.94.own, bf16[256,2304]{1,0:T(8,128)(2,1)S(1)} %collective-permute-done.11.ro, bf16[256,2304]{1,0:T(8,128)(2,1)S(1)} %collective-permute-done.13.a_in, ...), custom_call_target="tpu_custom_call" | custom-call | flops 589824000 | bytes 6291456 | tf_op jit(solution)/shard_map/pallas_call | solution.py:196
  159.6 2.0 collective-permute-start.26
  161.7 19.0 %shard_map.214 = f32[1152,2304]{1,0:T(8,128)} custom-call(bf16[256,2304]{1,0:T(8,128)(2,1)} %bitcast.42, bf16[256,2304]{1,0:T(8,128)(2,1)} %copy-done.17, bf16[256,2304]{1,0:T(8,128)(2,1)} %collective-permute-done.1.refs_1_.refs_2_, bf16[256,2304]{1,0:T(8,128)(2,1)} %copy-done.32, bf16[256,2304]{1,0:T(8,128)(2,1)} %collective-permute-done.2.refs_3_.refs_4_, ...), custom_call_target="tpu_custom_call" | custom-call | flops 10871635968 | bytes 31457280 | tf_op jit(solution)/shard_map/pallas_call | solution.py:322
  180.7 1.7 collective-permute-start.16
  183.8 2.3 copy-done
  186.1 7.2 %shard_map.215.refs_9_ = f32[2304,1152]{1,0:T(8,128)} custom-call(bf16[256,2304]{1,0:T(8,128)(2,1)S(1)} %shard_map.207.refs_0_, bf16[256,2304]{1,0:T(8,128)(2,1)} %collective-permute-done.17.refs_1_, bf16[256,2304]{1,0:T(8,128)(2,1)} %collective-permute-done.18.refs_2_, bf16[256,2304]{1,0:T(8,128)(2,1)} %collective-permute-done.20.refs_3_, ...), custom_call_target="tpu_custom_call" | custom-call | flops 3623878656 | bytes 31457280 | tf_op jit(solution)/shard_map/pallas_call | solution.py:322
  193.3 3.7 %collective-permute-done.16.refs_2_ = bf16[256,2304]{1,0:T(8,128)(2,1)S(1)} collective-permute-done((bf16[256,2304]{1,0:T(8,128)(2,1)S(1)}, bf16[256,2304]{1,0:T(8,128)(2,1)S(1)}, u32[]{:S(2)}, u32[]{:S(2)}) %collective-permute-start.16) | collective-permute-done | bytes 1179680 | tf_op jit(solution)/shard_map/ppermute | solution.py:146
  197.6 12.3 %shard_map.216 = f32[2304,1152]{1,0:T(8,128)} custom-call(bf16[256,2304]{1,0:T(8,128)(2,1)S(1)} %shard_map.207.refs_0_, bf16[256,2304]{1,0:T(8,128)(2,1)} %collective-permute-done.17.refs_1_, bf16[256,2304]{1,0:T(8,128)(2,1)} %collective-permute-done.18.refs_2_, bf16[256,2304]{1,0:T(8,128)(2,1)} %collective-permute-done.20.refs_3_, ...), custom_call_target="tpu_custom_call", output_to_operand_aliasing={{}: (9, {})} | custom-call | flops 7247757312 | bytes 31457280 | tf_op jit(solution)/shard_map/pallas_call | solution.py:322
  210.0 4.2 %shard_map.217.refs_3_ = bf16[288,2048]{1,0:T(8,128)(2,1)S(1)} custom-call(bf16[256,2304]{1,0:T(8,128)(2,1)S(1)} %get-tuple-element.98.refs_0_.refs_2_, bf16[256,2304]{1,0:T(8,128)(2,1)S(1)} %collective-permute-done.25.refs_1_, bf16[256,2304]{1,0:T(8,128)(2,1)S(1)} %collective-permute-done.16.refs_2_, bf16[256,2304]{1,0:T(8,128)(2,1)S(1)} %collective-permute-done.27.refs_3_, ...), custom_call_target="tpu_custom_call" | custom-call | flops 2038431744 | bytes 10485760 | tf_op jit(solution)/shard_map/pallas_call | solution.py:343
  214.2 1.3 collective-permute-start.29
  215.6 1.3 shard_map.223.refs_0_
  218.0 1.4 shard_map.218
  219.4 21.0 %shard_map.219._ = bf16[3,3,96,2048]{3,2,1,0:T(8,128)(2,1)S(1)} custom-call(s32[1]{0:T(128)} %bitcast.me_ref._, bf16[3,96,2048]{2,1,0:T(8,128)(2,1)S(1)} %bitcast.50, bf16[3,96,2048]{2,1,0:T(8,128)(2,1)S(1)} %bitcast.55, bf16[3,96,2048]{2,1,0:T(8,128)(2,1)S(1)} %bitcast.60, bf16[3,96,2048]{2,1,0:T(8,128)(2,1)S(1)} %bitcast.28, ...), custom_call_target="tpu_custom_call" | custom-call | flops 10737418240 | bytes 6291456 | tf_op jit(solution)/shard_map/pallas_call | solution.py:117
  240.4 10.7 %shard_map.220 = bf16[3,3,96,2048]{3,2,1,0:T(8,128)(2,1)S(1)} custom-call(s32[1]{0:T(128)} %bitcast.me_ref._, bf16[3,96,2048]{2,1,0:T(8,128)(2,1)S(1)} %bitcast.51, bf16[3,96,2048]{2,1,0:T(8,128)(2,1)S(1)} %bitcast.56, bf16[3,96,2048]{2,1,0:T(8,128)(2,1)S(1)} %bitcast.61, bf16[3,96,2048]{2,1,0:T(8,128)(2,1)S(1)} %bitcast.29, ...), custom_call_target="tpu_custom_call", output_to_operand_aliasing={{}: (6, {})} | custom-call | flops 5368709120 | bytes 3145728 | tf_op jit(solution)/shard_map/pallas_call | solution.py:117
  251.2 2.1 copy-done.10
  253.3 7.2 %shard_map.221 = (bf16[256,2304]{1,0:T(8,128)(2,1)S(1)}, bf16[256,2304]{1,0:T(8,128)(2,1)S(1)}, bf16[256,2304]{1,0:T(8,128)(2,1)S(1)}, bf16[256,2304]{1,0:T(8,128)(2,1)S(1)}) custom-call(bf16[864,2048]{1,0:T(8,128)(2,1)S(1)} %bitcast.36, bf16[864,2304]{1,0:T(8,128)(2,1)S(1)} %bitcast.45), custom_call_target="tpu_custom_call" | custom-call | flops 4076863488 | bytes 31457280 | tf_op jit(solution)/shard_map/pallas_call | solution.py:211
  260.8 0.9 collective-permute-start.33
  261.8 1.1 collective-permute-start.36
  263.6 7.2 %shard_map.222 = (bf16[256,2304]{1,0:T(8,128)(2,1)S(1)}, bf16[256,2304]{1,0:T(8,128)(2,1)S(1)}, bf16[256,2304]{1,0:T(8,128)(2,1)S(1)}, bf16[256,2304]{1,0:T(8,128)(2,1)S(1)}) custom-call(bf16[864,2048]{1,0:T(8,128)(2,1)S(1)} %bitcast.37, bf16[864,2304]{1,0:T(8,128)(2,1)S(1)} %bitcast.46), custom_call_target="tpu_custom_call" | custom-call | flops 4076863488 | bytes 31457280 | tf_op jit(solution)/shard_map/pallas_call | solution.py:211
  271.2 1.3 collective-permute-start.40
  272.5 29.8 %collective-permute-done.36.refs_6_ = bf16[256,2304]{1,0:T(8,128)(2,1)S(1)} collective-permute-done((bf16[256,2304]{1,0:T(8,128)(2,1)}, bf16[256,2304]{1,0:T(8,128)(2,1)S(1)}, u32[]{:S(2)}, u32[]{:S(2)}) %collective-permute-start.36) | collective-permute-done | bytes 1179680 | tf_op jit(solution)/shard_map/ppermute | solution.py:146
  303.3 1.3 add_convert_fusion.1
  304.7 1.5 add_convert_fusion
  306.3 1.0 copy-done.22
  307.3 0.9 collective-permute-start.43
  308.5 1.0 copy-done.26
  309.5 1.2 collective-permute-start.42
  311.4 1.0 copy-done.24
  312.4 1.1 copy-done.28
  313.5 1.3 copy-done.23
  314.8 1.3 copy-done.25
  316.1 1.3 copy-done.27
  317.3 1.3 copy-done.29
  318.6 11.6 %shard_map.224 = f32[864,2304]{1,0:T(8,128)} custom-call(bf16[256,2304]{1,0:T(8,128)(2,1)S(1)} %shard_map.223.refs_0_, bf16[256,2304]{1,0:T(8,128)(2,1)S(1)} %copy-done.23, bf16[256,2304]{1,0:T(8,128)(2,1)} %collective-permute-done.32.refs_2_, bf16[256,2304]{1,0:T(8,128)(2,1)S(1)} %copy-done.27, bf16[256,2304]{1,0:T(8,128)(2,1)S(1)} %copy-done.19, ...), custom_call_target="tpu_custom_call" | custom-call | flops 8153726976 | bytes 31457280 | tf_op jit(solution)/shard_map/pallas_call | solution.py:322
  330.2 5.1 %shard_map.225.refs_9_ = f32[288,2304]{1,0:T(8,128)} custom-call(bf16[256,2304]{1,0:T(8,128)(2,1)S(1)} %get-tuple-element.98.refs_0_.refs_2_, bf16[256,2304]{1,0:T(8,128)(2,1)S(1)} %collective-permute-done.25.refs_1_, bf16[256,2304]{1,0:T(8,128)(2,1)S(1)} %collective-permute-done.16.refs_2_, bf16[256,2304]{1,0:T(8,128)(2,1)S(1)} %collective-permute-done.27.refs_3_, ...), custom_call_target="tpu_custom_call" | custom-call | flops 1811939328 | bytes 31457280 | tf_op jit(solution)/shard_map/pallas_call | solution.py:322
  335.8 3.5 %shard_map.226 = (bf16[256,2304]{1,0:T(8,128)(2,1)}, f32[6,2304]{1,0:T(8,128)S(1)}) custom-call(bf16[256,2304]{1,0:T(8,128)(2,1)S(1)} %get-tuple-element.128.own, bf16[256,2304]{1,0:T(8,128)(2,1)S(1)} %collective-permute-done.41.ro, bf16[256,2304]{1,0:T(8,128)(2,1)S(1)} %collective-permute-done.42.a_in, ...), custom_call_target="tpu_custom_call" | custom-call | flops 589824000 | bytes 6291456 | tf_op jit(solution)/shard_map/pallas_call | solution.py:196
  339.4 1.4 collective-permute-start.46
  340.8 1.2 collective-permute-start.45
  342.8 2.9 shard_map.227
  346.4 1.2 convert_reduce_fusion
  (139 shorter events, 17.0 us)
Async XLA Ops:
  0.6 6.2 %collective-permute-start = (bf16[256,2304]{1,0:T(8,128)(2,1)}, bf16[256,2304]{1,0:T(8,128)(2,1)S(1)}, u32[]{:S(2)}, u32[]{:S(2)}) collective-permute-start(bf16[256,2304]{1,0:T(8,128)(2,1)} %bitcast.39), channel_id=1, source_target_pairs={{0,1},{1,0},{2,3},{3,2},{4,5},{5,4},{6,7},{7,6},{8,9},{9,8},{10,11... | collective-permute-start | bytes 3538952 | tf_op jit(solution)/shard_map/ppermute | solution.py:146
  1.4 28.5 %collective-permute-start.1 = (bf16[256,2304]{1,0:T(8,128)(2,1)}, bf16[256,2304]{1,0:T(8,128)(2,1)}, u32[]{:S(2)}, u32[]{:S(2)}) collective-permute-start(bf16[256,2304]{1,0:T(8,128)(2,1)} %bitcast.40), channel_id=1, source_target_pairs={{0,2},{1,5},{2,0},{3,7},{4,6},{5,1},{6,4},{7,3},{8,10},{9,13},{10,... | collective-permute-start | bytes 3538952 | tf_op jit(solution)/shard_map/ppermute | solution.py:146
  3.9 28.7 %collective-permute-start.2 = (bf16[256,2304]{1,0:T(8,128)(2,1)}, bf16[256,2304]{1,0:T(8,128)(2,1)}, u32[]{:S(2)}, u32[]{:S(2)}) collective-permute-start(bf16[256,2304]{1,0:T(8,128)(2,1)} %bitcast.41), channel_id=1, source_target_pairs={{0,4},{1,3},{2,6},{3,1},{4,0},{5,7},{6,2},{7,5},{8,12},{9,11},{10,... | collective-permute-start | bytes 3538952 | tf_op jit(solution)/shard_map/ppermute | solution.py:146
  6.9 16.1 %copy-start.17 = (bf16[256,2304]{1,0:T(8,128)(2,1)}, bf16[256,2304]{1,0:T(8,128)(2,1)S(1)}, u32[]{:S(2)}) copy-start(bf16[256,2304]{1,0:T(8,128)(2,1)S(1)} %collective-permute-done.refs_2_.refs_1_) | copy-start | bytes 3538948
  8.6 14.4 %copy-start.2 = (bf16[1,256,2304]{2,1,0:T(8,128)(2,1)S(1)}, bf16[1,256,2304]{2,1,0:T(8,128)(2,1)}, u32[]{:S(2)}) copy-start(bf16[1,256,2304]{2,1,0:T(8,128)(2,1)} %param.16) | copy-start | bytes 3538948
  29.9 17.1 %collective-permute-start.6 = (bf16[256,2304]{1,0:T(8,128)(2,1)}, bf16[256,2304]{1,0:T(8,128)(2,1)S(1)}, u32[]{:S(2)}, u32[]{:S(2)}) collective-permute-start(bf16[256,2304]{1,0:T(8,128)(2,1)} %collective-permute-done.1.refs_1_.refs_2_), channel_id=1, source_target_pairs={{0,4},{1,3},{2,6},{3,1},{4,0},{5,7},{6,2},{7,5},{8,12},{9,11},{10,... | collective-permute-start | bytes 3538952 | tf_op jit(solution)/shard_map/ppermute | solution.py:146
  32.6 14.4 %collective-permute-start.3 = (bf16[256,2304]{1,0:T(8,128)(2,1)}, bf16[256,2304]{1,0:T(8,128)(2,1)S(1)}, u32[]{:S(2)}, u32[]{:S(2)}) collective-permute-start(bf16[256,2304]{1,0:T(8,128)(2,1)} %collective-permute-done.2.refs_3_.refs_4_), channel_id=1, source_target_pairs={{0,1},{1,0},{2,3},{3,2},{4,5},{5,4},{6,7},{7,6},{8,9},{9,8},{10,11... | collective-permute-start | bytes 3538952 | tf_op jit(solution)/shard_map/ppermute | solution.py:146
  32.6 14.4 %collective-permute-start.4 = (bf16[256,2304]{1,0:T(8,128)(2,1)}, bf16[256,2304]{1,0:T(8,128)(2,1)S(1)}, u32[]{:S(2)}, u32[]{:S(2)}) collective-permute-start(bf16[256,2304]{1,0:T(8,128)(2,1)} %collective-permute-done.1.refs_1_.refs_2_), channel_id=1, source_target_pairs={{0,1},{1,0},{2,3},{3,2},{4,5},{5,4},{6,7},{7,6},{8,9},{9,8},{10,11... | collective-permute-start | bytes 3538952 | tf_op jit(solution)/shard_map/ppermute | solution.py:146
  47.0 23.9 %copy-start.6 = (bf16[256,2304]{1,0:T(8,128)(2,1)}, bf16[256,2304]{1,0:T(8,128)(2,1)S(1)}, u32[]{:S(2)}) copy-start(bf16[256,2304]{1,0:T(8,128)(2,1)S(1)} %collective-permute-done.6.refs_1_.refs_6_) | copy-start | bytes 3538948
  47.0 23.9 %collective-permute-start.7 = (bf16[256,2304]{1,0:T(8,128)(2,1)S(1)}, bf16[256,2304]{1,0:T(8,128)(2,1)S(1)}, u32[]{:S(2)}, u32[]{:S(2)}) collective-permute-start(bf16[256,2304]{1,0:T(8,128)(2,1)S(1)} %collective-permute-done.6.refs_1_.refs_6_), channel_id=1, source_target_pairs={{0,1},{1,0},{2,3},{3,2},{4,5},{5,4},{6,7},{7,6},{8,9},{9,8},{10,11... | collective-permute-start | bytes 3538952 | tf_op jit(solution)/shard_map/ppermute | solution.py:146
  70.9 14.4 %copy-start.7 = (bf16[256,2304]{1,0:T(8,128)(2,1)}, bf16[256,2304]{1,0:T(8,128)(2,1)S(1)}, u32[]{:S(2)}) copy-start(bf16[256,2304]{1,0:T(8,128)(2,1)S(1)} %collective-permute-done.7.refs_2_.refs_7_) | copy-start | bytes 3538948
  85.2 4.3 %collective-permute-start.8 = (bf16[256,2304]{1,0:T(8,128)(2,1)S(1)}, bf16[256,2304]{1,0:T(8,128)(2,1)S(1)}, u32[]{:S(2)}, u32[]{:S(2)}) collective-permute-start(bf16[256,2304]{1,0:T(8,128)(2,1)S(1)} %get-tuple-element.83), channel_id=1, source_target_pairs={{0,1},{1,0},{2,3},{3,2},{4,5},{5,4},{6,7},{7,6},{8,9},{9,8},{10,11... | collective-permute-start | bytes 3538952 | tf_op jit(solution)/shard_map/ppermute | solution.py:146
  85.8 4.6 %collective-permute-start.12 = (bf16[256,2304]{1,0:T(8,128)(2,1)S(1)}, bf16[256,2304]{1,0:T(8,128)(2,1)S(1)}, u32[]{:S(2)}, u32[]{:S(2)}) collective-permute-start(bf16[256,2304]{1,0:T(8,128)(2,1)S(1)} %get-tuple-element.97), channel_id=1, source_target_pairs={{0,1},{1,0},{2,3},{3,2},{4,5},{5,4},{6,7},{7,6},{8,9},{9,8},{10,11... | collective-permute-start | bytes 3538952 | tf_op jit(solution)/shard_map/ppermute | solution.py:146
  85.8 56.0 %collective-permute-start.19 = (bf16[256,2304]{1,0:T(8,128)(2,1)S(1)}, bf16[256,2304]{1,0:T(8,128)(2,1)}, u32[]{:S(2)}, u32[]{:S(2)}) collective-permute-start(bf16[256,2304]{1,0:T(8,128)(2,1)S(1)} %shard_map.207.refs_0_), channel_id=1, source_target_pairs={{0,4},{1,3},{2,6},{3,1},{4,0},{5,7},{6,2},{7,5},{8,12},{9,11},{10,... | collective-permute-start | bytes 3538952 | tf_op jit(solution)/shard_map/ppermute | solution.py:146
  87.8 53.9 %collective-permute-start.18 = (bf16[256,2304]{1,0:T(8,128)(2,1)S(1)}, bf16[256,2304]{1,0:T(8,128)(2,1)}, u32[]{:S(2)}, u32[]{:S(2)}) collective-permute-start(bf16[256,2304]{1,0:T(8,128)(2,1)S(1)} %shard_map.207.refs_0_), channel_id=1, source_target_pairs={{0,2},{1,5},{2,0},{3,7},{4,6},{5,1},{6,4},{7,3},{8,10},{9,13},{10,... | collective-permute-start | bytes 3538952 | tf_op jit(solution)/shard_map/ppermute | solution.py:146
  89.6 61.2 %collective-permute-start.11 = (bf16[256,2304]{1,0:T(8,128)(2,1)S(1)}, bf16[256,2304]{1,0:T(8,128)(2,1)S(1)}, u32[]{:S(2)}, u32[]{:S(2)}) collective-permute-start(bf16[256,2304]{1,0:T(8,128)(2,1)S(1)} %get-tuple-element.95), channel_id=1, source_target_pairs={{0,1},{1,0},{2,3},{3,2},{4,5},{5,4},{6,7},{7,6},{8,9},{9,8},{10,11... | collective-permute-start | bytes 3538952 | tf_op jit(solution)/shard_map/ppermute | solution.py:146
  89.6 11.1 %collective-permute-start.5 = (bf16[256,2304]{1,0:T(8,128)(2,1)}, bf16[256,2304]{1,0:T(8,128)(2,1)S(1)}, u32[]{:S(2)}, u32[]{:S(2)}) collective-permute-start(bf16[256,2304]{1,0:T(8,128)(2,1)} %get-tuple-element.79), channel_id=1, source_target_pairs={{0,1},{1,0},{2,3},{3,2},{4,5},{5,4},{6,7},{7,6},{8,9},{9,8},{10,11... | collective-permute-start | bytes 3538952 | tf_op jit(solution)/shard_map/ppermute | solution.py:146
  90.4 30.1 %collective-permute-start.9 = (bf16[128,2304]{1,0:T(8,128)(2,1)S(1)}, bf16[128,2304]{1,0:T(8,128)(2,1)S(1)}, u32[]{:S(2)}, u32[]{:S(2)}) collective-permute-start(bf16[128,2304]{1,0:T(8,128)(2,1)S(1)} %get-tuple-element.136), channel_id=1, source_target_pairs={{0,2},{1,5},{2,0},{3,7},{4,6},{5,1},{6,4},{7,3},{8,10},{9,13},{10,... | collective-permute-start | bytes 1769480 | tf_op jit(solution)/shard_map/ppermute | solution.py:146
  100.6 50.2 %collective-permute-start.13 = (bf16[256,2304]{1,0:T(8,128)(2,1)S(1)}, bf16[256,2304]{1,0:T(8,128)(2,1)S(1)}, u32[]{:S(2)}, u32[]{:S(2)}) collective-permute-start(bf16[256,2304]{1,0:T(8,128)(2,1)S(1)} %add_convert_fusion.3), channel_id=1, source_target_pairs={{0,2},{1,5},{2,0},{3,7},{4,6},{5,1},{6,4},{7,3},{8,10},{9,13},{10,... | collective-permute-start | bytes 3538952 | tf_op jit(solution)/shard_map/ppermute | solution.py:146
  120.5 19.0 %collective-permute-start.10 = (bf16[128,2304]{1,0:T(8,128)(2,1)S(1)}, bf16[128,2304]{1,0:T(8,128)(2,1)S(1)}, u32[]{:S(2)}, u32[]{:S(2)}) collective-permute-start(bf16[128,2304]{1,0:T(8,128)(2,1)S(1)} %get-tuple-element.137), channel_id=1, source_target_pairs={{0,2},{1,5},{2,0},{3,7},{4,6},{5,1},{6,4},{7,3},{8,10},{9,13},{10,... | collective-permute-start | bytes 1769480 | tf_op jit(solution)/shard_map/ppermute | solution.py:146
  139.7 11.6 %collective-permute-start.15 = (bf16[128,2304]{1,0:T(8,128)(2,1)S(1)}, bf16[128,2304]{1,0:T(8,128)(2,1)S(1)}, u32[]{:S(2)}, u32[]{:S(2)}) collective-permute-start(bf16[128,2304]{1,0:T(8,128)(2,1)S(1)} %add_convert_fusion.4), channel_id=1, source_target_pairs={{0,4},{1,3},{2,6},{3,1},{4,0},{5,7},{6,2},{7,5},{8,12},{9,11},{10,... | collective-permute-start | bytes 1769480 | tf_op jit(solution)/shard_map/ppermute | solution.py:146
  141.7 14.2 %collective-permute-start.14 = (bf16[128,2304]{1,0:T(8,128)(2,1)S(1)}, bf16[128,2304]{1,0:T(8,128)(2,1)S(1)}, u32[]{:S(2)}, u32[]{:S(2)}) collective-permute-start(bf16[128,2304]{1,0:T(8,128)(2,1)S(1)} %add_convert_fusion.5), channel_id=1, source_target_pairs={{0,4},{1,3},{2,6},{3,1},{4,0},{5,7},{6,2},{7,5},{8,12},{9,11},{10,... | collective-permute-start | bytes 1769480 | tf_op jit(solution)/shard_map/ppermute | solution.py:146
  141.8 38.9 %collective-permute-start.22 = (bf16[256,2304]{1,0:T(8,128)(2,1)}, bf16[256,2304]{1,0:T(8,128)(2,1)}, u32[]{:S(2)}, u32[]{:S(2)}) collective-permute-start(bf16[256,2304]{1,0:T(8,128)(2,1)} %collective-permute-done.18.refs_2_), channel_id=1, source_target_pairs={{0,4},{1,3},{2,6},{3,1},{4,0},{5,7},{6,2},{7,5},{8,12},{9,11},{10,... | collective-permute-start | bytes 3538952 | tf_op jit(solution)/shard_map/ppermute | solution.py:146
  143.7 12.2 %copy-start.9 = (bf16[1,256,2304]{2,1,0:T(8,128)(2,1)S(1)}, bf16[1,256,2304]{2,1,0:T(8,128)(2,1)}, u32[]{:S(2)}) copy-start(bf16[1,256,2304]{2,1,0:T(8,128)(2,1)} %param.17) | copy-start | bytes 3538948
  150.7 8.9 %copy-start.4 = (bf16[3,96,2048]{2,1,0:T(8,128)(2,1)}, bf16[3,96,2048]{2,1,0:T(8,128)(2,1)S(1)}, u32[]{:S(2)}) copy-start(bf16[3,96,2048]{2,1,0:T(8,128)(2,1)S(1)} %get-tuple-element.115) | copy-start | bytes 3538948
  150.7 30.0 %collective-permute-start.17 = (bf16[256,2304]{1,0:T(8,128)(2,1)S(1)}, bf16[256,2304]{1,0:T(8,128)(2,1)}, u32[]{:S(2)}, u32[]{:S(2)}) collective-permute-start(bf16[256,2304]{1,0:T(8,128)(2,1)S(1)} %shard_map.207.refs_0_), channel_id=1, source_target_pairs={{0,1},{1,0},{2,3},{3,2},{4,5},{5,4},{6,7},{7,6},{8,9},{9,8},{10,11... | collective-permute-start | bytes 3538952 | tf_op jit(solution)/shard_map/ppermute | solution.py:146
  150.8 31.7 %collective-permute-start.20 = (bf16[256,2304]{1,0:T(8,128)(2,1)}, bf16[256,2304]{1,0:T(8,128)(2,1)}, u32[]{:S(2)}, u32[]{:S(2)}) collective-permute-start(bf16[256,2304]{1,0:T(8,128)(2,1)} %collective-permute-done.19.refs_4_), channel_id=1, source_target_pairs={{0,1},{1,0},{2,3},{3,2},{4,5},{5,4},{6,7},{7,6},{8,9},{9,8},{10,11... | collective-permute-start | bytes 3538952 | tf_op jit(solution)/shard_map/ppermute | solution.py:146
  151.3 31.7 %collective-permute-start.21 = (bf16[256,2304]{1,0:T(8,128)(2,1)}, bf16[256,2304]{1,0:T(8,128)(2,1)}, u32[]{:S(2)}, u32[]{:S(2)}) collective-permute-start(bf16[256,2304]{1,0:T(8,128)(2,1)} %collective-permute-done.18.refs_2_), channel_id=1, source_target_pairs={{0,1},{1,0},{2,3},{3,2},{4,5},{5,4},{6,7},{7,6},{8,9},{9,8},{10,11... | collective-permute-start | bytes 3538952 | tf_op jit(solution)/shard_map/ppermute | solution.py:146
  159.6 22.9 %collective-permute-start.26 = (bf16[256,2304]{1,0:T(8,128)(2,1)S(1)}, bf16[256,2304]{1,0:T(8,128)(2,1)S(1)}, u32[]{:S(2)}, u32[]{:S(2)}) collective-permute-start(bf16[256,2304]{1,0:T(8,128)(2,1)S(1)} %get-tuple-element.98.refs_0_.refs_2_), channel_id=1, source_target_pairs={{0,4},{1,3},{2,6},{3,1},{4,0},{5,7},{6,2},{7,5},{8,12},{9,11},{10,... | collective-permute-start | bytes 3538952 | tf_op jit(solution)/shard_map/ppermute | solution.py:146
  180.7 3.1 collective-permute-start.23
  180.7 16.2 %collective-permute-start.16 = (bf16[256,2304]{1,0:T(8,128)(2,1)S(1)}, bf16[256,2304]{1,0:T(8,128)(2,1)S(1)}, u32[]{:S(2)}, u32[]{:S(2)}) collective-permute-start(bf16[256,2304]{1,0:T(8,128)(2,1)S(1)} %get-tuple-element.98.refs_0_.refs_2_), channel_id=1, source_target_pairs={{0,2},{1,5},{2,0},{3,7},{4,6},{5,1},{6,4},{7,3},{8,10},{9,13},{10,... | collective-permute-start | bytes 3538952 | tf_op jit(solution)/shard_map/ppermute | solution.py:146
  182.5 27.4 %collective-permute-start.25 = (bf16[256,2304]{1,0:T(8,128)(2,1)S(1)}, bf16[256,2304]{1,0:T(8,128)(2,1)S(1)}, u32[]{:S(2)}, u32[]{:S(2)}) collective-permute-start(bf16[256,2304]{1,0:T(8,128)(2,1)S(1)} %get-tuple-element.98.refs_0_.refs_2_), channel_id=1, source_target_pairs={{0,1},{1,0},{2,3},{3,2},{4,5},{5,4},{6,7},{7,6},{8,9},{9,8},{10,11... | collective-permute-start | bytes 3538952 | tf_op jit(solution)/shard_map/ppermute | solution.py:146
  182.5 27.4 %collective-permute-start.27 = (bf16[256,2304]{1,0:T(8,128)(2,1)S(1)}, bf16[256,2304]{1,0:T(8,128)(2,1)S(1)}, u32[]{:S(2)}, u32[]{:S(2)}) collective-permute-start(bf16[256,2304]{1,0:T(8,128)(2,1)S(1)} %collective-permute-done.26.refs_4_), channel_id=1, source_target_pairs={{0,1},{1,0},{2,3},{3,2},{4,5},{5,4},{6,7},{7,6},{8,9},{9,8},{10,11... | collective-permute-start | bytes 3538952 | tf_op jit(solution)/shard_map/ppermute | solution.py:146
  183.8 2.3 copy-start
  193.3 16.7 %copy-start.1 = (bf16[3,96,2304]{2,1,0:T(8,128)(2,1)S(1)}, bf16[3,96,2304]{2,1,0:T(8,128)(2,1)}, u32[]{:S(2)}) copy-start(bf16[3,96,2304]{2,1,0:T(8,128)(2,1)} %param.27) | copy-start | bytes 3981316
  197.0 13.0 %collective-permute-start.28 = (bf16[256,2304]{1,0:T(8,128)(2,1)S(1)}, bf16[256,2304]{1,0:T(8,128)(2,1)S(1)}, u32[]{:S(2)}, u32[]{:S(2)}) collective-permute-start(bf16[256,2304]{1,0:T(8,128)(2,1)S(1)} %collective-permute-done.16.refs_2_), channel_id=1, source_target_pairs={{0,1},{1,0},{2,3},{3,2},{4,5},{5,4},{6,7},{7,6},{8,9},{9,8},{10,11... | collective-permute-start | bytes 3538952 | tf_op jit(solution)/shard_map/ppermute | solution.py:146
  197.0 17.2 %collective-permute-start.24 = (bf16[256,2304]{1,0:T(8,128)(2,1)S(1)}, bf16[256,2304]{1,0:T(8,128)(2,1)S(1)}, u32[]{:S(2)}, u32[]{:S(2)}) collective-permute-start(bf16[256,2304]{1,0:T(8,128)(2,1)S(1)} %collective-permute-done.16.refs_2_), channel_id=1, source_target_pairs={{0,4},{1,3},{2,6},{3,1},{4,0},{5,7},{6,2},{7,5},{8,12},{9,11},{10,... | collective-permute-start | bytes 3538952 | tf_op jit(solution)/shard_map/ppermute | solution.py:146
  209.9 5.7 %copy-start.30 = (f32[2304]{0:T(1024)S(1)}, f32[2304]{0:T(1024)}, u32[]{:S(2)}) copy-start(f32[2304]{0:T(1024)} %param.22) | copy-start | bytes 27652
  209.9 5.7 %copy-start.31 = (f32[2304]{0:T(1024)S(1)}, f32[2304]{0:T(1024)}, u32[]{:S(2)}) copy-start(f32[2304]{0:T(1024)} %param.23) | copy-start | bytes 27652
  209.9 5.7 %copy-start.3 = (bf16[1,256,2304]{2,1,0:T(8,128)(2,1)S(1)}, bf16[1,256,2304]{2,1,0:T(8,128)(2,1)}, u32[]{:S(2)}) copy-start(bf16[1,256,2304]{2,1,0:T(8,128)(2,1)} %param.15) | copy-start | bytes 3538948
  214.2 3.8 %collective-permute-start.29 = (bf16[256,2304]{1,0:T(8,128)(2,1)S(1)}, bf16[256,2304]{1,0:T(8,128)(2,1)S(1)}, u32[]{:S(2)}, u32[]{:S(2)}) collective-permute-start(bf16[256,2304]{1,0:T(8,128)(2,1)S(1)} %collective-permute-done.24.refs_0_.refs_6_), channel_id=1, source_target_pairs={{0,1},{1,0},{2,3},{3,2},{4,5},{5,4},{6,7},{7,6},{8,9},{9,8},{10,11... | collective-permute-start | bytes 3538952 | tf_op jit(solution)/shard_map/ppermute | solution.py:146
  216.9 23.5 %collective-permute-start.32 = (bf16[256,2304]{1,0:T(8,128)(2,1)S(1)}, bf16[256,2304]{1,0:T(8,128)(2,1)}, u32[]{:S(2)}, u32[]{:S(2)}) collective-permute-start(bf16[256,2304]{1,0:T(8,128)(2,1)S(1)} %shard_map.223.refs_0_), channel_id=1, source_target_pairs={{0,2},{1,5},{2,0},{3,7},{4,6},{5,1},{6,4},{7,3},{8,10},{9,13},{10,... | collective-permute-start | bytes 3538952 | tf_op jit(solution)/shard_map/ppermute | solution.py:146
  260.4 2.9 collective-permute-start.30
  260.8 41.5 %collective-permute-start.33 = (bf16[256,2304]{1,0:T(8,128)(2,1)S(1)}, bf16[256,2304]{1,0:T(8,128)(2,1)S(1)}, u32[]{:S(2)}, u32[]{:S(2)}) collective-permute-start(bf16[256,2304]{1,0:T(8,128)(2,1)S(1)} %shard_map.223.refs_0_), channel_id=1, source_target_pairs={{0,4},{1,3},{2,6},{3,1},{4,0},{5,7},{6,2},{7,5},{8,12},{9,11},{10,... | collective-permute-start | bytes 3538952 | tf_op jit(solution)/shard_map/ppermute | solution.py:146
  261.8 40.6 %collective-permute-start.36 = (bf16[256,2304]{1,0:T(8,128)(2,1)}, bf16[256,2304]{1,0:T(8,128)(2,1)S(1)}, u32[]{:S(2)}, u32[]{:S(2)}) collective-permute-start(bf16[256,2304]{1,0:T(8,128)(2,1)} %collective-permute-done.32.refs_2_), channel_id=1, source_target_pairs={{0,4},{1,3},{2,6},{3,1},{4,0},{5,7},{6,2},{7,5},{8,12},{9,11},{10,... | collective-permute-start | bytes 3538952 | tf_op jit(solution)/shard_map/ppermute | solution.py:146
  262.8 40.0 %collective-permute-start.38 = (bf16[256,2304]{1,0:T(8,128)(2,1)S(1)}, bf16[256,2304]{1,0:T(8,128)(2,1)S(1)}, u32[]{:S(2)}, u32[]{:S(2)}) collective-permute-start(bf16[256,2304]{1,0:T(8,128)(2,1)S(1)} %get-tuple-element.122), channel_id=1, source_target_pairs={{0,1},{1,0},{2,3},{3,2},{4,5},{5,4},{6,7},{7,6},{8,9},{9,8},{10,11... | collective-permute-start | bytes 3538952 | tf_op jit(solution)/shard_map/ppermute | solution.py:146
  270.8 32.1 %collective-permute-start.39 = (bf16[256,2304]{1,0:T(8,128)(2,1)S(1)}, bf16[256,2304]{1,0:T(8,128)(2,1)S(1)}, u32[]{:S(2)}, u32[]{:S(2)}) collective-permute-start(bf16[256,2304]{1,0:T(8,128)(2,1)S(1)} %get-tuple-element.124), channel_id=1, source_target_pairs={{0,1},{1,0},{2,3},{3,2},{4,5},{5,4},{6,7},{7,6},{8,9},{9,8},{10,11... | collective-permute-start | bytes 3538952 | tf_op jit(solution)/shard_map/ppermute | solution.py:146
  271.2 33.4 %collective-permute-start.40 = (bf16[256,2304]{1,0:T(8,128)(2,1)S(1)}, bf16[256,2304]{1,0:T(8,128)(2,1)S(1)}, u32[]{:S(2)}, u32[]{:S(2)}) collective-permute-start(bf16[256,2304]{1,0:T(8,128)(2,1)S(1)} %add_convert_fusion.2), channel_id=1, source_target_pairs={{0,2},{1,5},{2,0},{3,7},{4,6},{5,1},{6,4},{7,3},{8,10},{9,13},{10,... | collective-permute-start | bytes 3538952 | tf_op jit(solution)/shard_map/ppermute | solution.py:146
  302.3 2.3 copy-start.20
  302.3 4.0 %collective-permute-start.31 = (bf16[256,2304]{1,0:T(8,128)(2,1)S(1)}, bf16[256,2304]{1,0:T(8,128)(2,1)S(1)}, u32[]{:S(2)}, u32[]{:S(2)}) collective-permute-start(bf16[256,2304]{1,0:T(8,128)(2,1)S(1)} %shard_map.223.refs_0_), channel_id=1, source_target_pairs={{0,1},{1,0},{2,3},{3,2},{4,5},{5,4},{6,7},{7,6},{8,9},{9,8},{10,11... | collective-permute-start | bytes 3538952 | tf_op jit(solution)/shard_map/ppermute | solution.py:146
  302.3 2.3 copy-start.18
  302.3 9.0 %collective-permute-start.35 = (bf16[256,2304]{1,0:T(8,128)(2,1)}, bf16[256,2304]{1,0:T(8,128)(2,1)S(1)}, u32[]{:S(2)}, u32[]{:S(2)}) collective-permute-start(bf16[256,2304]{1,0:T(8,128)(2,1)} %collective-permute-done.32.refs_2_), channel_id=1, source_target_pairs={{0,1},{1,0},{2,3},{3,2},{4,5},{5,4},{6,7},{7,6},{8,9},{9,8},{10,11... | collective-permute-start | bytes 3538952 | tf_op jit(solution)/shard_map/ppermute | solution.py:146
  302.8 5.7 %collective-permute-start.34 = (bf16[256,2304]{1,0:T(8,128)(2,1)S(1)}, bf16[256,2304]{1,0:T(8,128)(2,1)S(1)}, u32[]{:S(2)}, u32[]{:S(2)}) collective-permute-start(bf16[256,2304]{1,0:T(8,128)(2,1)S(1)} %collective-permute-done.33.refs_4_), channel_id=1, source_target_pairs={{0,1},{1,0},{2,3},{3,2},{4,5},{5,4},{6,7},{7,6},{8,9},{9,8},{10,11... | collective-permute-start | bytes 3538952 | tf_op jit(solution)/shard_map/ppermute | solution.py:146
  302.9 9.5 %collective-permute-start.37 = (bf16[256,2304]{1,0:T(8,128)(2,1)S(1)}, bf16[256,2304]{1,0:T(8,128)(2,1)S(1)}, u32[]{:S(2)}, u32[]{:S(2)}) collective-permute-start(bf16[256,2304]{1,0:T(8,128)(2,1)S(1)} %collective-permute-done.36.refs_6_), channel_id=1, source_target_pairs={{0,1},{1,0},{2,3},{3,2},{4,5},{5,4},{6,7},{7,6},{8,9},{9,8},{10,11... | collective-permute-start | bytes 3538952 | tf_op jit(solution)/shard_map/ppermute | solution.py:146
  304.6 30.7 %collective-permute-start.41 = (bf16[256,2304]{1,0:T(8,128)(2,1)S(1)}, bf16[256,2304]{1,0:T(8,128)(2,1)S(1)}, u32[]{:S(2)}, u32[]{:S(2)}) collective-permute-start(bf16[256,2304]{1,0:T(8,128)(2,1)S(1)} %get-tuple-element.129), channel_id=1, source_target_pairs={{0,1},{1,0},{2,3},{3,2},{4,5},{5,4},{6,7},{7,6},{8,9},{9,8},{10,11... | collective-permute-start | bytes 3538952 | tf_op jit(solution)/shard_map/ppermute | solution.py:146
  304.7 8.8 %copy-start.19 = (bf16[256,2304]{1,0:T(8,128)(2,1)S(1)}, bf16[256,2304]{1,0:T(8,128)(2,1)}, u32[]{:S(2)}) copy-start(bf16[256,2304]{1,0:T(8,128)(2,1)} %copy-done.18) | copy-start | bytes 3538948
  304.7 8.8 %copy-start.21 = (bf16[256,2304]{1,0:T(8,128)(2,1)S(1)}, bf16[256,2304]{1,0:T(8,128)(2,1)}, u32[]{:S(2)}) copy-start(bf16[256,2304]{1,0:T(8,128)(2,1)} %copy-done.20) | copy-start | bytes 3538948
  307.3 28.1 %collective-permute-start.43 = (bf16[256,2304]{1,0:T(8,128)(2,1)}, bf16[256,2304]{1,0:T(8,128)(2,1)S(1)}, u32[]{:S(2)}, u32[]{:S(2)}) collective-permute-start(bf16[256,2304]{1,0:T(8,128)(2,1)} %add_convert_fusion), channel_id=1, source_target_pairs={{0,4},{1,3},{2,6},{3,1},{4,0},{5,7},{6,2},{7,5},{8,12},{9,11},{10,... | collective-permute-start | bytes 3538952 | tf_op jit(solution)/shard_map/ppermute | solution.py:146
  309.5 26.3 %collective-permute-start.42 = (bf16[256,2304]{1,0:T(8,128)(2,1)}, bf16[256,2304]{1,0:T(8,128)(2,1)S(1)}, u32[]{:S(2)}, u32[]{:S(2)}) collective-permute-start(bf16[256,2304]{1,0:T(8,128)(2,1)} %add_convert_fusion.1), channel_id=1, source_target_pairs={{0,2},{1,5},{2,0},{3,7},{4,6},{5,1},{6,4},{7,3},{8,10},{9,13},{10,... | collective-permute-start | bytes 3538952 | tf_op jit(solution)/shard_map/ppermute | solution.py:146
  311.3 18.8 %copy-start.5 = (bf16[3,96,2048]{2,1,0:T(8,128)(2,1)S(1)}, bf16[3,96,2048]{2,1,0:T(8,128)(2,1)}, u32[]{:S(2)}) copy-start(bf16[3,96,2048]{2,1,0:T(8,128)(2,1)} %copy-done.4) | copy-start | bytes 3538948
  339.4 7.0 %collective-permute-start.46 = (f32[6,2304]{1,0:T(8,128)S(1)}, f32[6,2304]{1,0:T(8,128)S(1)}, u32[]{:S(2)}, u32[]{:S(2)}) collective-permute-start(f32[6,2304]{1,0:T(8,128)S(1)} %get-tuple-element.134), channel_id=1, source_target_pairs={{0,6},{1,7},{2,4},{3,5},{4,2},{5,3},{6,0},{7,1},{8,14},{9,15},{10,... | collective-permute-start | bytes 165896 | tf_op jit(solution)/shard_map/ppermute | solution.py:146
  340.8 5.6 %collective-permute-start.45 = (f32[6,2304]{1,0:T(8,128)S(1)}, f32[6,2304]{1,0:T(8,128)S(1)}, u32[]{:S(2)}, u32[]{:S(2)}) collective-permute-start(f32[6,2304]{1,0:T(8,128)S(1)} %get-tuple-element.134), channel_id=1, source_target_pairs={{0,4},{1,5},{2,6},{3,7},{4,0},{5,1},{6,2},{7,3},{8,12},{9,13},{10,... | collective-permute-start | bytes 165896 | tf_op jit(solution)/shard_map/ppermute | solution.py:146
  342.0 4.4 %collective-permute-start.44 = (f32[6,2304]{1,0:T(8,128)S(1)}, f32[6,2304]{1,0:T(8,128)S(1)}, u32[]{:S(2)}, u32[]{:S(2)}) collective-permute-start(f32[6,2304]{1,0:T(8,128)S(1)} %get-tuple-element.134), channel_id=1, source_target_pairs={{0,2},{1,3},{2,0},{3,1},{4,6},{5,7},{6,4},{7,5},{8,10},{9,11},{10,... | collective-permute-start | bytes 165896 | tf_op jit(solution)/shard_map/ppermute | solution.py:146
  346.4 1.3 collective-permute-start.47
  (18 other events, 26.9 us)
